TPU v7x, 32 devices: a whole 2x2x4 slice. The times are simulated.
32 devices in a mesh: dp: 2 (over y), tm: 16 (over z, x, core).
Axes of the slice: x: 2, y: 2, z: 4, core: 2. Of those that a mesh axis runs over, the one named last changes fastest.
Arguments:
- inputs: bfloat16 [2, 128, 14, 14, 512], P('dp', 'tm'), may hold values from -6 to 6
- clip_ids: int32 [2, 128], P('dp'), may hold values from 0 to 15, as said below
- norm1_gain: bfloat16 [2, 512], replicated, may hold values from 0.5 to 1.5
- norm1_bias: bfloat16 [2, 512], replicated, may hold values from -1.75 to 1.75
- qkv_weight: bfloat16 [2, 512, 1536], replicated, may hold values from -0.25 to 0.25
- q_bias: bfloat16 [2, 512], replicated, may hold values from -3 to 3
- v_bias: bfloat16 [2, 512], replicated, may hold values from -3 to 3
- bias_table: bfloat16 [2, 2535, 16], replicated, may hold values from -6 to 6
- proj_weight: bfloat16 [2, 512, 512], replicated, may hold values from -2 to 2
- proj_bias: bfloat16 [2, 512], replicated, may hold values from -1.75 to 1.75
- norm2_gain: bfloat16 [2, 512], replicated, may hold values from 0.5 to 1.5
- norm2_bias: bfloat16 [2, 512], replicated, may hold values from -1.75 to 1.75
- fc1_weight: bfloat16 [2, 512, 2048], replicated, may hold values from -0.25 to 0.25
- fc1_bias: bfloat16 [2, 2048], replicated, may hold values from -3 to 3
- fc2_weight: bfloat16 [2, 2048, 512], replicated, may hold values from -0.125 to 0.125
- fc2_bias: bfloat16 [2, 512], replicated, may hold values from -1.75 to 1.75
- cotangent: bfloat16 [2, 128, 14, 14, 512], P('dp', 'tm'), may hold values from -6 to 6
Outputs:
- block_output: bfloat16 [2, 128, 14, 14, 512], P('dp', 'tm')
- input_grad: bfloat16 [2, 128, 14, 14, 512], P('dp', 'tm')
- norm1_gain_grad: float32 [2, 512], replicated
- norm1_bias_grad: float32 [2, 512], replicated
- qkv_weight_grad: float32 [2, 512, 1536], P(None, 'tm')
- q_bias_grad: float32 [2, 512], replicated
- v_bias_grad: float32 [2, 512], replicated
- bias_table_grad: float32 [2, 2535, 16], replicated
- proj_weight_grad: float32 [2, 512, 512], P(None, 'tm')
- proj_bias_grad: float32 [2, 512], replicated
- norm2_gain_grad: float32 [2, 512], replicated
- norm2_bias_grad: float32 [2, 512], replicated
- fc1_weight_grad: float32 [2, 512, 2048], P(None, 'tm')
- fc1_bias_grad: float32 [2, 2048], replicated
- fc2_weight_grad: float32 [2, 2048, 512], P(None, 'tm')
- fc2_bias_grad: float32 [2, 512], replicated
Inputs may be any that keep to these rules, and one draw needn't show every extreme that they name: `clip_ids`: in each group a clip's number is the index of its first block of 8 token frames; every clip starts at a multiple of 8 token frames and has 8, 16 or 32 of them, except that the group's last 8 token frames always form a clip of their own and the clip before them may be shorter.
All inputs are finite; a program needn't handle non-finite values.
Results may differ from a plain program's by a relative error of at most 0.015.
Values may be sent and summed in bfloat16 or wider, within the bound.
A program may use at most 384 MiB of HBM per device.

v0:
```python
from functools import partial

import jax
import jax.numpy as jnp
from jax import lax
from jax.sharding import PartitionSpec as P

D = 512
HEADS = 16
HEAD_DIM = 32
SIDE = 14
WIN_T = 8
WIN_S = 7
SHIFT_T = 4
SHIFT_S = 3
LAYERS = 2
WIN_ROWS = 392
TABLE_ROWS = 2535


masked_score = -1e30


def passed_along(value, axis, steps):
    count = lax.axis_size(axis)
    pairs = [(source, (source + steps) % count) for source in range(count)]
    return lax.ppermute(value, axis, pairs)


def layer_norm(values, gain_row, shift_row):
    center = values - jnp.mean(values, axis=-1, keepdims=True)
    spread = jnp.mean(center * center, axis=-1, keepdims=True)
    return center * lax.rsqrt(spread + 1e-05) * gain_row + shift_row


def product(left_side, right_side):
    return jnp.dot(left_side, right_side, preferred_element_type=jnp.float32)


def contract_rows(left_side, right_side):
    return lax.dot_general(
        left_side, right_side, (((0,), (0,)), ((), ())), preferred_element_type=jnp.float32
    )


def times_transpose(left_side, right_side):
    return lax.dot_general(
        left_side, right_side, (((1,), (1,)), ((), ())), preferred_element_type=jnp.float32
    )


def relative_index():
    position = jnp.arange(WIN_ROWS, dtype=jnp.int32)
    time_pos = position // (WIN_S * WIN_S)
    high_pos = position // WIN_S % WIN_S
    wide_pos = position % WIN_S
    span_side = 2 * WIN_S - 1
    time_diff = time_pos[:, None] - time_pos[None, :] + (WIN_T - 1)
    high_diff = high_pos[:, None] - high_pos[None, :] + (WIN_S - 1)
    wide_diff = wide_pos[:, None] - wide_pos[None, :] + (WIN_S - 1)
    return (time_diff * span_side + high_diff) * span_side + wide_diff


def region_labels():
    places = jnp.arange(SIDE, dtype=jnp.int32)
    return (places >= SIDE - WIN_S).astype(jnp.int32) + (places >= SIDE - SHIFT_S).astype(jnp.int32)


def split_windows(grid_field):
    frames = grid_field.shape[0]
    channels = grid_field.shape[-1]
    across = SIDE // WIN_S
    shaped = grid_field.reshape(frames // WIN_T, WIN_T, across, WIN_S, across, WIN_S, channels)
    return shaped.transpose(0, 2, 4, 1, 3, 5, 6).reshape(-1, WIN_ROWS, channels)


def merge_windows(windows, frames):
    channels = windows.shape[-1]
    across = SIDE // WIN_S
    shaped = windows.reshape(frames // WIN_T, across, across, WIN_T, WIN_S, WIN_S, channels)
    return shaped.transpose(0, 3, 1, 4, 2, 5, 6).reshape(frames, SIDE, SIDE, channels)


def window_scores(qkv_block, key_block, bias_heads, masked):
    window_count = qkv_block.shape[0]
    split_parts = qkv_block.reshape(window_count, WIN_ROWS, 3, HEADS, HEAD_DIM)
    queries = split_parts[:, :, 0]
    key_part = split_parts[:, :, 1]
    valued = split_parts[:, :, 2]
    scores = (
        jnp.einsum("bihd,bjhd->bhij", queries, key_part, preferred_element_type=jnp.float32)
        * HEAD_DIM ** (-0.5)
        + bias_heads[None]
    )
    if masked:
        allowed = key_block[:, :, None] == key_block[:, None, :]
        scores = jnp.where(allowed[:, None], scores, masked_score)
    return (scores, queries, key_part, valued)


def attend_forward(block_items, bias_heads, masked):
    qkv_block, key_block = block_items
    scores, queries, key_part, valued = window_scores(qkv_block, key_block, bias_heads, masked)
    row_max = jnp.max(scores, axis=-1, keepdims=True)
    exponent = jnp.exp(scores - row_max)
    row_total = jnp.sum(exponent, axis=-1, keepdims=True)
    attn_probs = (exponent / row_total).astype(jnp.bfloat16)
    mixed_out = jnp.einsum(
        "bhij,bjhd->bihd", attn_probs, valued, preferred_element_type=jnp.float32
    )
    mixed_out = mixed_out.reshape(qkv_block.shape[0], WIN_ROWS, D).astype(jnp.bfloat16)
    return (mixed_out, row_max + jnp.log(row_total))


def attend_backward(bias_sum, block_items, bias_heads, masked):
    qkv_block, key_block, log_total, grad_block = block_items
    window_count = qkv_block.shape[0]
    scores, queries, key_part, valued = window_scores(qkv_block, key_block, bias_heads, masked)
    attn_probs = jnp.exp(scores - log_total)
    probs_low = attn_probs.astype(jnp.bfloat16)
    grad_heads = grad_block.reshape(window_count, WIN_ROWS, HEADS, HEAD_DIM)
    grad_value = jnp.einsum(
        "bhij,bihd->bjhd", probs_low, grad_heads, preferred_element_type=jnp.float32
    )
    grad_probs = jnp.einsum(
        "bihd,bjhd->bhij", grad_heads, valued, preferred_element_type=jnp.float32
    )
    grad_scores = attn_probs * (
        grad_probs - jnp.sum(attn_probs * grad_probs, axis=-1, keepdims=True)
    )
    scores_low = grad_scores.astype(jnp.bfloat16)
    scale_factor = HEAD_DIM ** (-0.5)
    grad_query = (
        jnp.einsum("bhij,bjhd->bihd", scores_low, key_part, preferred_element_type=jnp.float32)
        * scale_factor
    )
    grad_key = (
        jnp.einsum("bhij,bihd->bjhd", scores_low, queries, preferred_element_type=jnp.float32)
        * scale_factor
    )
    grad_qkv = (
        jnp.stack([grad_query, grad_key, grad_value], axis=2)
        .reshape(window_count, WIN_ROWS, 3 * D)
        .astype(jnp.bfloat16)
    )
    return (bias_sum + jnp.sum(scores_low, axis=0, dtype=jnp.float32), grad_qkv)


def run_forward(qkv_windows, key_windows, bias_heads, masked):
    window_count = qkv_windows.shape[0]
    paired = (
        qkv_windows.reshape(window_count // 2, 2, WIN_ROWS, 3 * D),
        key_windows.reshape(window_count // 2, 2, WIN_ROWS),
    )
    mixed_out, log_total = lax.map(
        partial(attend_forward, bias_heads=bias_heads, masked=masked), paired
    )
    return (mixed_out.reshape(window_count, WIN_ROWS, D), log_total)


def run_backward(qkv_windows, key_windows, log_total, grad_windows, bias_heads, masked):
    window_count = qkv_windows.shape[0]
    items = (
        qkv_windows.reshape(window_count // 2, 2, WIN_ROWS, 3 * D),
        key_windows.reshape(window_count // 2, 2, WIN_ROWS),
        log_total,
        grad_windows.reshape(window_count // 2, 2, WIN_ROWS, D),
    )
    start_sum = jnp.zeros((HEADS, WIN_ROWS, WIN_ROWS), jnp.float32)
    bias_grad, grad_qkv = lax.scan(
        partial(attend_backward, bias_heads=bias_heads, masked=masked), start_sum, items
    )
    return (grad_qkv.reshape(window_count, WIN_ROWS, 3 * D), bias_grad)


def layer_forward(current, clip_all, layer_weights, shifted):
    (
        gain_one,
        shift_one,
        weight_qkv,
        bias_query,
        bias_value,
        table_rows,
        weight_proj,
        bias_proj,
        gain_two,
        shift_two,
        weight_up,
        bias_up,
        weight_down,
        bias_down,
    ) = layer_weights
    token_rows = current.shape[0]
    frames = token_rows // (SIDE * SIDE)
    bias_heads = jnp.transpose(table_rows.astype(jnp.float32)[relative_index()], (2, 0, 1))
    normed_low = layer_norm(
        current, gain_one.astype(jnp.float32), shift_one.astype(jnp.float32)
    ).astype(jnp.bfloat16)
    qkv_bias = jnp.concatenate([bias_query, jnp.zeros_like(bias_query), bias_value]).astype(
        jnp.float32
    )
    qkv_low = (
        (product(normed_low, weight_qkv) + qkv_bias)
        .astype(jnp.bfloat16)
        .reshape(frames, SIDE, SIDE, 3 * D)
    )
    if shifted:
        ahead_qkv = passed_along(qkv_low[:SHIFT_T], "tm", -1)
        extended = jnp.roll(
            jnp.concatenate([qkv_low[SHIFT_T:], ahead_qkv]), (-SHIFT_S, -SHIFT_S), axis=(1, 2)
        )
        start_frame = lax.axis_index("tm") * frames + SHIFT_T
        wrapped = jnp.concatenate([clip_all, clip_all[:SHIFT_T]])
        moved_ids = lax.dynamic_slice_in_dim(wrapped, start_frame, frames)
        labels = region_labels()
        key_field = moved_ids[:, None, None] * 9 + labels[None, :, None] * 3 + labels[None, None, :]
        key_windows = split_windows(key_field[..., None])[..., 0]
    else:
        extended = qkv_low
        key_windows = jnp.zeros(
            (frames // WIN_T * (SIDE // WIN_S) * (SIDE // WIN_S), WIN_ROWS), jnp.int32
        )
    qkv_windows = split_windows(extended)
    mixed_windows, log_total = run_forward(qkv_windows, key_windows, bias_heads, shifted)
    mixed_out = merge_windows(mixed_windows, frames)
    if shifted:
        mixed_out = jnp.roll(mixed_out, (SHIFT_S, SHIFT_S), axis=(1, 2))
        behind = passed_along(mixed_out[frames - SHIFT_T :], "tm", 1)
        mixed_out = jnp.concatenate([behind, mixed_out[: frames - SHIFT_T]])
    mixed_out = mixed_out.reshape(token_rows, D)
    attended = current + product(mixed_out, weight_proj) + bias_proj.astype(jnp.float32)
    normed_two = layer_norm(
        attended, gain_two.astype(jnp.float32), shift_two.astype(jnp.float32)
    ).astype(jnp.bfloat16)
    hidden = product(normed_two, weight_up) + bias_up.astype(jnp.float32)
    active_low = jax.nn.gelu(hidden, approximate=False).astype(jnp.bfloat16)
    result = attended + product(active_low, weight_down) + bias_down.astype(jnp.float32)
    saved_state = (
        current,
        normed_low,
        qkv_windows,
        key_windows,
        log_total,
        mixed_out,
        attended,
        normed_two,
        hidden,
        active_low,
    )
    return (result, saved_state)


def layer_backward(upstream, saved_state, layer_weights, shifted):
    (
        gain_one,
        shift_one,
        weight_qkv,
        bias_query,
        bias_value,
        table_rows,
        weight_proj,
        bias_proj,
        gain_two,
        shift_two,
        weight_up,
        bias_up,
        weight_down,
        bias_down,
    ) = layer_weights
    (
        current,
        normed_low,
        qkv_windows,
        key_windows,
        log_total,
        mixed_out,
        attended,
        normed_two,
        hidden,
        active_low,
    ) = saved_state
    token_rows = current.shape[0]
    frames = token_rows // (SIDE * SIDE)
    table_index = relative_index()
    bias_heads = jnp.transpose(table_rows.astype(jnp.float32)[table_index], (2, 0, 1))
    grad_out_low = upstream.astype(jnp.bfloat16)
    grad_down = contract_rows(active_low, grad_out_low)
    grad_bias_down = jnp.sum(grad_out_low, axis=0, dtype=jnp.float32)
    grad_active = times_transpose(grad_out_low, weight_down)
    gelu_back = jax.vjp(partial(jax.nn.gelu, approximate=False), hidden)[1]
    grad_hidden_low = gelu_back(grad_active)[0].astype(jnp.bfloat16)
    grad_up = contract_rows(normed_two, grad_hidden_low)
    grad_bias_up = jnp.sum(grad_hidden_low, axis=0, dtype=jnp.float32)
    grad_normed_two = times_transpose(grad_hidden_low, weight_up)
    norm_back_two = jax.vjp(
        layer_norm, attended, gain_two.astype(jnp.float32), shift_two.astype(jnp.float32)
    )[1]
    grad_attended, grad_gain_two, grad_shift_two = norm_back_two(grad_normed_two)
    grad_attended = grad_attended + upstream
    grad_attn_low = grad_attended.astype(jnp.bfloat16)
    grad_proj = contract_rows(mixed_out, grad_attn_low)
    grad_bias_proj = jnp.sum(grad_attn_low, axis=0, dtype=jnp.float32)
    grad_mixed = (
        times_transpose(grad_attn_low, weight_proj)
        .astype(jnp.bfloat16)
        .reshape(frames, SIDE, SIDE, D)
    )
    if shifted:
        ahead_grad = passed_along(grad_mixed[:SHIFT_T], "tm", -1)
        grad_mixed = jnp.roll(
            jnp.concatenate([grad_mixed[SHIFT_T:], ahead_grad]), (-SHIFT_S, -SHIFT_S), axis=(1, 2)
        )
    grad_windows = split_windows(grad_mixed)
    grad_qkv_windows, grad_bias_heads = run_backward(
        qkv_windows, key_windows, log_total, grad_windows, bias_heads, shifted
    )
    grad_qkv = merge_windows(grad_qkv_windows, frames)
    if shifted:
        grad_qkv = jnp.roll(grad_qkv, (SHIFT_S, SHIFT_S), axis=(1, 2))
        behind_grad = passed_along(grad_qkv[frames - SHIFT_T :], "tm", 1)
        grad_qkv = jnp.concatenate([behind_grad, grad_qkv[: frames - SHIFT_T]])
    grad_qkv = grad_qkv.reshape(token_rows, 3 * D)
    grad_weight_qkv = contract_rows(normed_low, grad_qkv)
    column_sums = jnp.sum(grad_qkv, axis=0, dtype=jnp.float32)
    grad_normed = times_transpose(grad_qkv, weight_qkv)
    norm_back_one = jax.vjp(
        layer_norm, current, gain_one.astype(jnp.float32), shift_one.astype(jnp.float32)
    )[1]
    grad_current, grad_gain_one, grad_shift_one = norm_back_one(grad_normed)
    grad_table = jax.ops.segment_sum(
        grad_bias_heads.reshape(HEADS, -1).T, table_index.reshape(-1), num_segments=TABLE_ROWS
    )
    layer_grads = (
        grad_gain_one,
        grad_shift_one,
        grad_weight_qkv,
        column_sums[:D],
        column_sums[2 * D :],
        grad_table,
        grad_proj,
        grad_bias_proj,
        grad_gain_two,
        grad_shift_two,
        grad_up,
        grad_bias_up,
        grad_down,
        grad_bias_down,
    )
    return (grad_current + grad_attended, layer_grads)


def body(
    inputs,
    clip_ids,
    norm1_gain,
    norm1_bias,
    qkv_weight,
    q_bias,
    v_bias,
    bias_table,
    proj_weight,
    proj_bias,
    norm2_gain,
    norm2_bias,
    fc1_weight,
    fc1_bias,
    fc2_weight,
    fc2_bias,
    cotangent,
):
    weight_set = (
        norm1_gain,
        norm1_bias,
        qkv_weight,
        q_bias,
        v_bias,
        bias_table,
        proj_weight,
        proj_bias,
        norm2_gain,
        norm2_bias,
        fc1_weight,
        fc1_bias,
        fc2_weight,
        fc2_bias,
    )
    token_rows = inputs.shape[1] * SIDE * SIDE
    current = inputs[0].reshape(token_rows, D).astype(jnp.float32)
    saved_layers = []
    for layer_index in range(LAYERS):
        layer_weights = tuple((member[layer_index] for member in weight_set))
        current, saved_state = layer_forward(current, clip_ids[0], layer_weights, layer_index == 1)
        saved_layers.append(saved_state)
    upstream = cotangent[0].reshape(token_rows, D).astype(jnp.float32)
    grads_by_layer = [None] * LAYERS
    for layer_index in reversed(range(LAYERS)):
        layer_weights = tuple((member[layer_index] for member in weight_set))
        upstream, layer_grads = layer_backward(
            upstream, saved_layers[layer_index], layer_weights, layer_index == 1
        )
        grads_by_layer[layer_index] = layer_grads
    stacked = [
        jnp.stack([grads_by_layer[layer_index][position] for layer_index in range(LAYERS)])
        for position in range(len(weight_set))
    ]
    small_places = [0, 1, 3, 4, 5, 7, 8, 9, 11, 13]
    flat_small = jnp.concatenate([stacked[position].reshape(-1) for position in small_places])
    shard_qkv, shard_proj, shard_up, shard_down = (
        lax.psum_scatter(stacked[2], "tm", scatter_dimension=1, tiled=True),
        lax.psum_scatter(stacked[6], "tm", scatter_dimension=1, tiled=True),
        lax.psum_scatter(stacked[10], "tm", scatter_dimension=1, tiled=True),
        lax.psum_scatter(stacked[12], "tm", scatter_dimension=1, tiled=True),
    )
    shard_qkv, shard_proj, shard_up, shard_down = (
        lax.psum(shard_qkv.astype(jnp.bfloat16), "dp").astype(jnp.float32),
        lax.psum(shard_proj.astype(jnp.bfloat16), "dp").astype(jnp.float32),
        lax.psum(shard_up.astype(jnp.bfloat16), "dp").astype(jnp.float32),
        lax.psum(shard_down.astype(jnp.bfloat16), "dp").astype(jnp.float32),
    )
    small_total = lax.psum(flat_small, ("dp", "tm"))
    results = [None] * len(weight_set)
    results[2] = shard_qkv
    results[6] = shard_proj
    results[10] = shard_up
    results[12] = shard_down
    offset = 0
    for position in small_places:
        member = stacked[position]
        results[position] = small_total[offset : offset + member.size].reshape(member.shape)
        offset = offset + member.size
    return (
        current.astype(jnp.bfloat16).reshape(inputs.shape),
        upstream.astype(jnp.bfloat16).reshape(inputs.shape),
    ) + tuple(results)


def solution(mesh):
    placed = (
        P("dp", "tm", None, None, None),
        P("dp", None),
        P(),
        P(),
        P(),
        P(),
        P(),
        P(),
        P(),
        P(),
        P(),
        P(),
        P(),
        P(),
        P(),
        P(),
        P("dp", "tm", None, None, None),
    )
    return jax.shard_map(
        body,
        mesh=mesh,
        in_specs=placed,
        out_specs=(
            P("dp", "tm", None, None, None),
            P("dp", "tm", None, None, None),
            P(),
            P(),
            P(None, "tm", None),
            P(),
            P(),
            P(),
            P(None, "tm", None),
            P(),
            P(),
            P(),
            P(None, "tm", None),
            P(),
            P(None, "tm", None),
            P(),
        ),
        check_vma=False,
    )
```

profile of v0, /device:TPU:0, one launch (start us, length us, event | category | flops | bytes accessed | tf_op | source)
XLA Modules:
  0.0 3826.9 jit_solution(14328640126855807229)
XLA Ops:
  42.0 15.8 copy.270
  60.2 282.7 %gather_fusion = f32[153664,16]{1,0:T(8,128)} fusion(f32[2535,16]{1,0:T(8,128)S(1)} %bitcast_convert_fusion.1, s32[154624]{0:T(1024)S(1)} %pad_clamp_fusion), kind=kCustom, calls=%fused_computation | custom fusion | bytes 20283648 | tf_op jit(solution)/shard_map/gather | solution.py:195
  342.9 54.4 %copy.269 = f32[392,392,16]{0,1,2:T(8,128)} copy(f32[392,392,16]{2,1,0:T(8,128)} %bitcast.21) | data formatting | bytes 19668992 | tf_op jit(solution)/shard_map/gather | solution.py:195
  399.2 101.7 %while.50 = (s32[]{:T(128)}, bf16[2,2,392,512]{3,1,2,0:T(2,128)(2,1)}, f32[2,2,16,392,1]{3,2,1,4,0:T(8,128)S(1)}, bf16[2,2,392,1536]{2,3,1,0:T(8,128)(2,1)}, f32[16,392,392]{1,2,0:T(8,128)}, /*index=5*/s32[]{:T(128)}) while((s32[]{:T(128)}, bf16[2,2,392,512]{3,1,2,0:T(2,128)(2,1)}, f32[2,2,16,392,1]{3,2,1,4,0:T(8,128)S(1)}, ...), condition=%wide.region_5.6_spmd, body=%wide.region_2.5_spmd.sunk | while | flops 688803584 | bytes 100965960 | solution.py:155
  401.9 13.2 fusion.187
  415.0 14.9 fusion.188
  429.9 16.2 fusion.189
  452.4 13.2 fusion.187
  465.6 14.9 fusion.188
  480.5 16.2 fusion.189
  515.3 32.8 multiply_convert_fusion.7
  577.4 281.6 %gather_fusion.1 = f32[153664,16]{1,0:T(8,128)} fusion(f32[2535,16]{1,0:T(8,128)S(1)} %bitcast_convert_fusion, s32[154624]{0:T(1024)S(1)} %copy-done.32), kind=kCustom, calls=%fused_computation.1 | custom fusion | bytes 20283648 | tf_op jit(solution)/shard_map/gather | solution.py:195
  859.0 54.5 %copy.278 = f32[392,392,16]{0,1,2:T(8,128)} copy(f32[392,392,16]{2,1,0:T(8,128)} %bitcast.43) | data formatting | bytes 19668992 | tf_op jit(solution)/shard_map/gather | solution.py:195
  934.5 15.9 copy.279
  952.4 84.6 %while.51 = (s32[]{:T(128)}, bf16[2,2,392,512]{3,1,2,0:T(2,128)(2,1)}, f32[2,2,16,392,1]{3,2,1,4,0:T(8,128)S(1)}, bf16[2,2,392,1536]{2,3,1,0:T(8,128)(2,1)}, s32...) while((s32[]{:T(128)}, bf16[2,2,392,512]{3,1,2,0:T(2,128)(2,1)}, ...), condition=%wide.region_13.14_spmd, body=%wide.region_10.13_spmd.sunk | while | flops 674359168 | bytes 82015120 | solution.py:155
  954.8 14.6 fusion.190
  997.1 14.6 fusion.190
  1065.8 33.1 multiply_convert_fusion.6
  1098.9 16.6 convert_reduce_fusion.2
  1148.5 251.5 %while.52 = (s32[]{:T(128)}, f32[16,392,392]{1,2,0:T(8,128)}, bf16[2,2,392,1536]{3,1,2,0:T(2,128)(2,1)}, s32[2,2,392]{2,1,0:T(2,128)S(1)}, bf16[2,2,392,1536]{2,...) while((s32[]{:T(128)}, f32[16,392,392]{1,2,0:T(8,128)}, ...), condition=%wide.region_21.22_spmd.clone, body=%wide.region_18.21_spmd.clone.sunk | while | flops 1639695232 | bytes 288524544 | solution.py:170
  1156.4 13.4 fusion.198
  1171.7 21.1 multiply_reduce_fusion.16
  1192.8 28.6 convert_reduce_fusion.13
  1238.9 12.4 fusion.199
  1280.4 13.4 fusion.198
  1295.8 21.2 multiply_reduce_fusion.16
  1316.9 28.6 convert_reduce_fusion.13
  1386.7 13.2 select_add_fusion.4
  1412.0 27.1 collective-permute-done.3
  1466.8 17.8 convert_reduce_fusion.3
  1509.0 245.8 %while.53 = (s32[]{:T(128)}, f32[16,392,392]{1,2,0:T(8,128)}, bf16[2,2,392,1536]{3,1,2,0:T(2,128)(2,1)}, bf16[2,2,392,1536]{2,3,1,0:T(8,128)(2,1)}, f32[16,392,3...) while((s32[]{:T(128)}, f32[16,392,392]{1,2,0:T(8,128)}, ...), condition=%wide.region_29.30_spmd.clone, body=%wide.region_26.29_spmd.clone.sunk | while | flops 1634470656 | bytes 287900448 | solution.py:170
  1516.7 13.7 fusion.207
  1531.3 19.1 multiply_reduce_fusion.17
  1550.3 28.8 convert_reduce_fusion.14
  1638.1 13.4 fusion.207
  1652.4 19.0 multiply_reduce_fusion.17
  1671.4 28.8 convert_reduce_fusion.14
  1741.3 13.2 select_add_fusion.5
  1839.6 15.7 copy.302
  1855.3 17.1 reshape.924
  1872.5 36.4 copy.303
  1908.8 820.0 %scatter_custom_fusion.1 = f32[2535,16]{1,0:T(8,128)} fusion(s32[153664]{0:T(1024)} %reshape.983, f32[153664,16]{1,0:T(8,128)} %copy.303, f32[]{:T(128)} %constant.203.clone.1), kind=kCustom, calls=%fused_computation.220 | custom fusion | flops 2458624 | bytes 162752 | tf_op jit(solution)/shard_map/scatter-add | solution.py:330
  2729.0 15.9 copy.300
  2744.9 17.0 reshape.923
  2761.9 35.9 copy.301
  2797.8 820.5 %scatter_custom_fusion = f32[2535,16]{1,0:T(8,128)} fusion(s32[153664]{0:T(1024)} %reshape.983, f32[153664,16]{1,0:T(8,128)} %copy.301, f32[]{:T(128)} %constant.203.clone.1), kind=kCustom, calls=%fused_computation.222 | custom fusion | flops 2458624 | bytes 162752 | tf_op jit(solution)/shard_map/scatter-add | solution.py:330
  3672.6 103.4 %all-reduce.4.cloned.1.call-done = f32[93408]{0:T(1024)} async-done(((f32[93408]{0:T(1024)}), f32[93408]{0:T(1024)}) %all-reduce.4.cloned.1.call-update) | async-done | bytes 373648 | tf_op jit(solution)/shard_map/psum | solution.py:420
  3786.8 26.0 all-reduce.6.cloned.1.call-done
  (614 shorter events, 662.0 us)
Async XLA Ops:
  8.0 3648.7 %reduce-scatter.7.cloned.1.call-start = ((), (), s32[]{:S(2)}) async-start(), calls=%async_computation.6 | async-start | bytes 2228224 | tf_op jit(solution)/shard_map/reduce_scatter | solution.py:410
  8.1 49.7 %copy-start.67 = (s32[392]{0:T(512)}, s32[392]{0:T(512)S(1)}, u32[]{:S(2)}) copy-start(s32[392]{0:T(512)S(1)} %get-tuple-element.561) | copy-start | bytes 4708
  8.1 49.7 %copy-start.69 = (s32[392]{0:T(512)}, s32[392]{0:T(512)S(1)}, u32[]{:S(2)}) copy-start(s32[392]{0:T(512)S(1)} %get-tuple-element.562) | copy-start | bytes 4708
  8.1 49.6 %copy-start.71 = (s32[392]{0:T(512)}, s32[392]{0:T(512)S(1)}, u32[]{:S(2)}) copy-start(s32[392]{0:T(512)S(1)} %add_select_fusion.4) | copy-start | bytes 4708
  42.0 17.1 copy-start.48
  59.0 283.8 %copy-start.31 = (s32[154624]{0:T(1024)}, s32[154624]{0:T(1024)S(1)}, u32[]{:S(2)}) copy-start(s32[154624]{0:T(1024)S(1)} %pad_clamp_fusion) | copy-start | bytes 1855492
  511.2 37.0 copy-start.4
  511.2 36.9 copy-start.57
  512.9 35.2 copy-start.74
  513.5 34.6 copy-start.103
  514.1 34.0 copy-start.96
  514.7 33.4 copy-start.113
  515.3 32.9 copy-start.127
  566.3 347.9 %collective-permute-start = (bf16[4,14,14,1536]{3,0,2,1:T(4,128)(2,1)}, bf16[4,14,14,1536]{3,0,2,1:T(4,128)(2,1)}, u32[]{:S(2)}, u32[]{:S(2)}) collective-permute-start(bf16[4,14,14,1536]{3,0,2,1:T(4,128)(2,1)} %copy.273), channel_id=1, source_target_pairs={{0,15},{1,0},{2,1},{3,2},{4,3},{5,4},{6,5},{7,6},{8,7},{9,8},{10,9... | collective-permute-start | bytes 7225352 | tf_op jit(solution)/shard_map/ppermute | solution.py:27
  859.0 54.5 %copy-start.123 = (s32[1,128]{1,0:T(1,128)S(1)}, s32[1,128]{1,0:T(1,128)}, u32[]{:S(2)}) copy-start(s32[1,128]{1,0:T(1,128)} %param.26) | copy-start | bytes 1540
  859.0 54.9 %copy-start.30 = (bf16[4,14,14,1536]{3,2,1,0:T(8,128)(2,1)S(1)}, bf16[4,14,14,1536]{3,2,1,0:T(8,128)(2,1)}, u32[]{:S(2)}) copy-start(bf16[4,14,14,1536]{3,2,1,0:T(8,128)(2,1)} %slice.302) | copy-start | bytes 7225348
  1040.5 14.5 collective-permute-start.1
  1064.1 59.5 %copy-start.11 = (f32[1568,512]{1,0:T(8,128)}, f32[1568,512]{1,0:T(8,128)S(1)}, u32[]{:S(2)}) copy-start(f32[1568,512]{1,0:T(8,128)S(1)} %get-tuple-element.549) | copy-start | bytes 9633796
  1064.2 59.5 %copy-start.63 = (f32[1568]{0:T(1024)}, f32[1568]{0:T(1024)S(1)}, u32[]{:S(2)}) copy-start(f32[1568]{0:T(1024)S(1)} %broadcast_multiply_fusion.1) | copy-start | bytes 18820
  1064.9 58.8 %copy-start.80 = (f32[1568]{0:T(1024)}, f32[1568]{0:T(1024)S(1)}, u32[]{:S(2)}) copy-start(f32[1568]{0:T(1024)S(1)} %fusion.95) | copy-start | bytes 18820
  1065.8 33.1 copy-start.26
  1098.9 16.6 copy-start.126
  1129.2 9.7 collective-permute-start.2
  1156.4 15.3 slice-start.5
  1156.4 15.3 slice-start.6
  1156.4 15.3 slice-start.7
  1280.4 15.3 slice-start.6
  1280.4 15.3 slice-start.7
  1407.1 36.0 copy-start.22
  1407.1 32.0 collective-permute-start.3
  1466.8 28.0 copy-start.13
  1466.8 17.8 copy-start.5
  1466.8 17.8 copy-start.58
  1466.8 17.8 copy-start.75
  1466.8 17.8 copy-start.104
  1501.3 2157.0 %reduce-scatter.5.cloned.1.call-start = ((), (), s32[]{:S(2)}) async-start(), calls=%async_computation.5 | async-start | bytes 6684672 | tf_op jit(solution)/shard_map/reduce_scatter | solution.py:409
  1781.4 1878.5 %reduce-scatter.11.cloned.1.call-start = ((), (), s32[]{:S(2)}) async-start(), calls=%async_computation.8 | async-start | bytes 8912896 | tf_op jit(solution)/shard_map/reduce_scatter | solution.py:412
  1800.1 1861.6 %reduce-scatter.9.cloned.1.call-start = ((), (), s32[]{:S(2)}) async-start(), calls=%async_computation.7 | async-start | bytes 8912896 | tf_op jit(solution)/shard_map/reduce_scatter | solution.py:411
  1819.5 1956.4 %all-reduce.4.cloned.1.call-start = ((), (), s32[]{:S(2)}) async-start(), calls=%async_computation.4 | async-start | bytes 753664 | tf_op jit(solution)/shard_map/psum | solution.py:420
  1872.4 856.4 %copy-start.95 = (f32[2048]{0:T(1024)S(1)}, f32[2048]{0:T(1024)}, u32[]{:S(2)}) copy-start(f32[2048]{0:T(1024)} %get-tuple-element.555) | copy-start | bytes 24580
  1872.4 856.4 %copy-start.98 = (f32[2048]{0:T(1024)S(1)}, f32[2048]{0:T(1024)}, u32[]{:S(2)}) copy-start(f32[2048]{0:T(1024)} %get-tuple-element.557) | copy-start | bytes 24580
  1872.4 856.5 %copy-start.118 = (f32[512]{0:T(512)S(1)}, f32[512]{0:T(512)}, u32[]{:S(2)}) copy-start(f32[512]{0:T(512)} %get-tuple-element.410) | copy-start | bytes 6148
  1872.4 856.5 %copy-start.122 = (f32[512]{0:T(512)S(1)}, f32[512]{0:T(512)}, u32[]{:S(2)}) copy-start(f32[512]{0:T(512)} %get-tuple-element.409) | copy-start | bytes 6148
  1872.4 856.5 %copy-start.117 = (f32[512]{0:T(512)S(1)}, f32[512]{0:T(512)}, u32[]{:S(2)}) copy-start(f32[512]{0:T(512)} %get-tuple-element.403) | copy-start | bytes 6148
  1872.4 856.5 %copy-start.121 = (f32[512]{0:T(512)S(1)}, f32[512]{0:T(512)}, u32[]{:S(2)}) copy-start(f32[512]{0:T(512)} %get-tuple-element.401) | copy-start | bytes 6148
  1872.5 856.5 %copy-start.84 = (f32[512]{0:T(512)S(1)}, f32[512]{0:T(512)}, u32[]{:S(2)}) copy-start(f32[512]{0:T(512)} %get-tuple-element.481) | copy-start | bytes 6148
  1872.5 856.5 %copy-start.108 = (f32[512]{0:T(512)S(1)}, f32[512]{0:T(512)}, u32[]{:S(2)}) copy-start(f32[512]{0:T(512)} %get-tuple-element.479) | copy-start | bytes 6148
  3650.7 162.1 %all-reduce.6.cloned.1.call-start = ((), (), s32[]{:S(2)}) async-start(), calls=%async_computation.9 | async-start | bytes 1572864 | tf_op jit(solution)/shard_map/psum | solution.py:415
  (117 other events, 752.2 us)
Sparse Core Ops, SparseCore 0:
  1501.4 59.0 reduce-scatter.6
  1781.5 82.3 reduce-scatter.4
  1868.0 102.5 reduce-scatter.10
  1974.5 102.9 reduce-scatter.8
Sparse Core Ops, SparseCore 1:
  3650.7 125.2 all-reduce.3
  3778.9 33.9 all-reduce.5
where the time goes:
time: 3840 us; the launch traced here: 3830 us
  other arithmetic  1940 us (51%)
  local copies, waits for them, and re-layouts  1110 us (29%)
  matrix products  566 us (15%)
  waiting for transfers between devices  178 us (5%)
    scatter-add x2, other arithmetic, layer_backward(): jax.ops.segment_sum(grad_bias_heads.reshape(HEADS, -1).T, table_index.res...  1640 us
    gather x4, local copies, waits for them, and re-layouts, layer_forward(): table_rows.astype(jnp.float32)[relative_index()]  673 us
    dot_general x8, matrix products, window_scores(): jnp.einsum('bihd,bjhd->bhij', queries, key_part, preferred_element_type=j...  136 us
    reduce_sum x4, other arithmetic, attend_backward(): return (bias_sum + jnp.sum(scores_low, axis=0, dtype=jnp.float32), grad_qkv)  115 us
    psum x1, waiting for transfers between devices, body(): small_total = lax.psum(flat_small, ('dp', 'tm'))  103 us
    dot_general x8, matrix products, product(): return jnp.dot(left_side, right_side, preferred_element_type=jnp.float32)  92.8 us
  transfers between devices with their start and end apart: 10, of which 5 were waited for; matrix products, arithmetic and copies ran while one was open for 66% of the time, Pallas kernels for 0%

commit v1 on v0

v1 whole, which is shorter than its diff:
```python
from functools import partial
import math

import jax
import jax.numpy as jnp
from jax import lax
from jax.experimental import pallas as pl
from jax.experimental.pallas import tpu as pltpu
from jax.sharding import PartitionSpec as P

D = 512
HEADS = 16
HEAD_DIM = 32
FF = 2048
SIDE = 14
WIN_T = 8
WIN_S = 7
SHIFT_T = 4
SHIFT_S = 3
LAYERS = 2
WIN_ROWS = 392
TABLE_ROWS = 2535
WINDOWS = 4
GROUP = 4
GROUPS = HEADS // GROUP
GW = GROUP * HEAD_DIM
HS = 400
LANES = 1664
OT_LANES = 1792
CODE = 768
BASE = 1536
LOG2E = 1.4426950408889634
QSCALE = HEAD_DIM ** (-0.5) * LOG2E
BIG = 1e30
F32 = jnp.float32
BF16 = jnp.bfloat16
CHUNKS = [(256 * c, 256) for c in range(6)] + [(1536, 128)]


def dot_nn(a, b):
    return lax.dot_general(a, b, (((1,), (0,)), ((), ())), preferred_element_type=F32)


def dot_nt(a, b):
    return lax.dot_general(a, b, (((1,), (1,)), ((), ())), preferred_element_type=F32)


def dot_tn(a, b):
    return lax.dot_general(a, b, (((0,), (0,)), ((), ())), preferred_element_type=F32)


def code_shift(spot):
    return 8 * (84 - (spot // WIN_S * 13 + spot % WIN_S))


def head_lanes(rows):
    return lax.broadcasted_iota(jnp.int32, (rows, GW), 1) // HEAD_DIM


def stack_heads(stack_ref, block):
    lane_head = head_lanes(WIN_ROWS)
    zero = jnp.zeros((), block.dtype)
    for h in range(GROUP):
        stack_ref[HS * h : HS * h + WIN_ROWS, :GW] = jnp.where(lane_head == h, block, zero)


def clear_gaps(stack_ref):
    width = stack_ref.shape[1]
    for h in range(GROUP):
        stop = HS * (h + 1) if h < GROUP - 1 else LANES
        stack_ref[HS * h + 384 : stop, :] = jnp.zeros((stop - HS * h - 384, width), stack_ref.dtype)


def unstack(turned_ref):
    picked = []
    for h in range(GROUP):
        rows = turned_ref[HEAD_DIM * h : HEAD_DIM * (h + 1), 384 * h : 384 * h + 512 + 128]
        if h:
            rows = pltpu.roll(rows, 640 - 16 * h, axis=1)
        picked.append(rows[:, :512])
    return jnp.concatenate(picked, axis=0).T[:WIN_ROWS]


def build_bias(tab_ref, place_ref, bias_ref, rolled):
    bias_ref[0] = jnp.zeros((WIN_ROWS, LANES), F32)
    for h in range(GROUP):
        base = tab_ref[0, h]
        for spot in range(49):
            shift = code_shift(spot)
            rolled[8 * spot : 8 * spot + 8, :] = pltpu.roll(base, BASE - shift, axis=1)[:, :CODE]
        part = dot_nn(rolled[...].astype(BF16), place_ref[h])
        bias_ref[0, :, 384 * h : 384 * h + 512] += part * LOG2E


def forward_kernel(masked, *refs):
    if masked:
        (q_ref, k_ref, v_ref, tab_ref, place_ref, kaug_ref, qaug_ref, o_ref, lse_ref, bias_ref, stack, rolled, turned) = refs
    else:
        (q_ref, k_ref, v_ref, tab_ref, place_ref, o_ref, lse_ref, bias_ref, stack, rolled, turned) = refs

    @pl.when((pl.program_id(0) == 0) & (pl.program_id(1) == 0))
    def _():
        clear_gaps(stack)
        if masked:
            for h in range(GROUP):
                stack[HS * h : HS * h + WIN_ROWS, GW:] = qaug_ref[...]

    @pl.when(pl.program_id(1) == 0)
    def _():
        build_bias(tab_ref, place_ref, bias_ref, rolled)

    stack_heads(stack, q_ref[0])
    keys = k_ref[0]
    if masked:
        keys = jnp.concatenate([keys, kaug_ref[0]], axis=1)
    values = jnp.concatenate([v_ref[0].astype(F32).T, jnp.ones((8, WIN_ROWS), F32)], axis=0).astype(BF16)
    for start, width in CHUNKS:
        scores = dot_nt(keys, stack[start : start + width, :]) + bias_ref[0, :, start : start + width]
        top = jnp.max(scores, axis=0, keepdims=True)
        weights = jnp.exp2(scores - top).astype(BF16)
        mixed = dot_nn(values, weights)
        total = mixed[GW : GW + 1]
        turned[:, start : start + width] = mixed[:GW] * (1.0 / total)
        lse_ref[0, :, start : start + width] = jnp.broadcast_to(top + jnp.log2(total), (8, width))
    o_ref[0] = unstack(turned).astype(BF16)


def backward_kernel(masked, *refs):
    if masked:
        (q_ref, k_ref, v_ref, o_ref, do_ref, lse_ref, bias_ref, place_ref, kaug_ref, qaug_ref,
         dq_ref, dk_ref, dv_ref, dtab_ref, stack, dstack, probs, slopes, turned, bias_sum) = refs
    else:
        (q_ref, k_ref, v_ref, o_ref, do_ref, lse_ref, bias_ref, place_ref,
         dq_ref, dk_ref, dv_ref, dtab_ref, stack, dstack, probs, slopes, turned, bias_sum) = refs

    @pl.when((pl.program_id(0) == 0) & (pl.program_id(1) == 0))
    def _():
        clear_gaps(stack)
        clear_gaps(dstack)
        if masked:
            for h in range(GROUP):
                stack[HS * h : HS * h + WIN_ROWS, GW:] = qaug_ref[...]

    @pl.when(pl.program_id(1) == 0)
    def _():
        bias_sum[...] = jnp.zeros_like(bias_sum)

    stack_heads(stack, q_ref[0])
    stack_heads(dstack, do_ref[0])
    keys = k_ref[0]
    keys_turned = keys.astype(F32).T.astype(BF16)
    if masked:
        keys = jnp.concatenate([keys, kaug_ref[0]], axis=1)
    values = v_ref[0]
    product = do_ref[0].astype(F32) * o_ref[0].astype(F32)
    product = jnp.concatenate([product, jnp.zeros((8, GW), F32)], axis=0)
    product_high = product.astype(BF16)
    product_low = (product - product_high.astype(F32)).astype(BF16)
    head_rows = lax.broadcasted_iota(jnp.int32, (8, GW), 0) == lax.broadcasted_iota(jnp.int32, (8, GW), 1) // HEAD_DIM
    picker = head_rows.astype(F32).astype(BF16)
    deltas = dot_nt(picker, product_high) + dot_nt(picker, product_low)
    delta_row = jnp.concatenate([deltas[h : h + 1] for h in range(GROUP)] + [jnp.zeros((1, LANES - GROUP * HS), F32)], axis=1)
    for start, width in CHUNKS:
        scores = dot_nt(keys, stack[start : start + width, :]) + bias_ref[0, :, start : start + width]
        chances = jnp.exp2(scores - lse_ref[0, :1, start : start + width])
        slope = dot_nt(values, dstack[start : start + width, :])
        slope = chances * (slope - delta_row[:, start : start + width])
        probs[:, start : start + width] = chances.astype(BF16)
        slopes[:, start : start + width] = slope.astype(BF16)
        bias_sum[:, start : start + width] += slope
    dv_ref[0] = dot_nn(probs[...], dstack[...]).astype(BF16)
    dk_ref[0] = (dot_nn(slopes[...], stack[:, :GW]) * math.log(2.0)).astype(BF16)
    for start, width in CHUNKS:
        turned[:, start : start + width] = dot_nn(keys_turned, slopes[:, start : start + width])
    dq_ref[0] = (unstack(turned) * HEAD_DIM ** (-0.5)).astype(BF16)

    @pl.when(pl.program_id(1) == WINDOWS - 1)
    def _():
        dtab_ref[...] = jnp.zeros_like(dtab_ref)
        pad = jnp.zeros((8, BASE - CODE), F32)
        for h in range(GROUP):
            coded = dot_nt(bias_sum[:, 384 * h : 384 * h + 512].astype(BF16), place_ref[h])
            total = jnp.zeros((8, BASE), F32)
            for spot in range(49):
                piece = jnp.concatenate([coded[8 * spot : 8 * spot + 8], pad], axis=1)
                total = total + pltpu.roll(piece, code_shift(spot), axis=1)
            dtab_ref[0, h] = total


def head_block(part):
    return pl.BlockSpec((1, WIN_ROWS, GW), lambda g, w: (w, 0, part * GROUPS + g))


PLAIN = pl.BlockSpec((1, WIN_ROWS, GW), lambda g, w: (w, 0, g))
LSE = pl.BlockSpec((1, 8, LANES), lambda g, w: (g * WINDOWS + w, 0, 0))
BIAS = pl.BlockSpec((1, WIN_ROWS, LANES), lambda g, w: (g, 0, 0))
TABLE = pl.BlockSpec((1, GROUP, 8, BASE), lambda g, w: (g, 0, 0, 0))
PLACE = pl.BlockSpec((GROUP, CODE, 512), lambda g, w: (0, 0, 0), pipeline_mode=pl.Buffered(1))
KAUG = pl.BlockSpec((1, WIN_ROWS, GW), lambda g, w: (w, 0, 0))
QAUG = pl.BlockSpec((WIN_ROWS, GW), lambda g, w: (0, 0))
VMEM_LIMIT = 62 * 1024 * 1024


def attention_forward(qkv, table, place, aug):
    masked = aug is not None
    wide = 2 * GW if masked else GW
    return pl.pallas_call(
        partial(forward_kernel, masked),
        grid=(GROUPS, WINDOWS),
        in_specs=[head_block(0), head_block(1), head_block(2), TABLE, PLACE] + ([KAUG, QAUG] if masked else []),
        out_specs=[PLAIN, LSE, BIAS],
        out_shape=[
            jax.ShapeDtypeStruct((WINDOWS, WIN_ROWS, D), BF16),
            jax.ShapeDtypeStruct((GROUPS * WINDOWS, 8, LANES), F32),
            jax.ShapeDtypeStruct((GROUPS, WIN_ROWS, LANES), F32),
        ],
        scratch_shapes=[
            pltpu.VMEM((LANES, wide), BF16),
            pltpu.VMEM((WIN_ROWS, CODE), F32),
            pltpu.VMEM((GW, OT_LANES), F32),
        ],
        compiler_params=pltpu.CompilerParams(vmem_limit_bytes=VMEM_LIMIT),
        name="attention_forward",
    )(qkv, qkv, qkv, table, place, *(aug or ()))


def attention_backward(qkv, mixed, grad_mixed, lse, bias, place, aug):
    masked = aug is not None
    wide = 2 * GW if masked else GW
    return pl.pallas_call(
        partial(backward_kernel, masked),
        grid=(GROUPS, WINDOWS),
        in_specs=[head_block(0), head_block(1), head_block(2), PLAIN, PLAIN, LSE, BIAS, PLACE] + ([KAUG, QAUG] if masked else []),
        out_specs=[PLAIN, PLAIN, PLAIN, TABLE],
        out_shape=[jax.ShapeDtypeStruct((WINDOWS, WIN_ROWS, D), BF16)] * 3
        + [jax.ShapeDtypeStruct((GROUPS, GROUP, 8, BASE), F32)],
        scratch_shapes=[
            pltpu.VMEM((LANES, wide), BF16),
            pltpu.VMEM((LANES, GW), BF16),
            pltpu.VMEM((WIN_ROWS, LANES), BF16),
            pltpu.VMEM((WIN_ROWS, LANES), BF16),
            pltpu.VMEM((GW, OT_LANES), F32),
            pltpu.VMEM((WIN_ROWS, LANES), F32),
        ],
        compiler_params=pltpu.CompilerParams(vmem_limit_bytes=VMEM_LIMIT),
        name="attention_backward",
    )(qkv, qkv, qkv, mixed, grad_mixed, lse, bias, place, *(aug or ()))


def spread_table(table_rows):
    cube = table_rows.T.reshape(HEADS, 15, 169)
    rows = jnp.stack([cube[:, 7 - tj : 15 - tj] for tj in range(WIN_T)], axis=1)
    rows = rows.transpose(0, 1, 3, 2).reshape(HEADS, WIN_T, 169 * WIN_T)
    rows = jnp.pad(rows, ((0, 0), (0, 0), (0, BASE - 169 * WIN_T)))
    return rows.reshape(GROUPS, GROUP, WIN_T, BASE).astype(F32)


def gather_table(spread):
    rows = spread.reshape(HEADS, WIN_T, BASE)[:, :, : 169 * WIN_T].reshape(HEADS, WIN_T, 169, WIN_T)
    rows = rows.transpose(0, 1, 3, 2)
    total = sum(
        jnp.pad(rows[:, tj], ((0, 0), (7 - tj, tj), (0, 0))) for tj in range(WIN_T)
    )
    return total.reshape(HEADS, TABLE_ROWS).T


def place_codes():
    code = jnp.arange(CODE, dtype=jnp.int32)
    spot_h, spot_w = code // 8 // 13, code // 8 % 13
    lane = (spot_h * WIN_S + spot_w) * 8 + code % 8
    lane = jnp.where((spot_h < WIN_S) & (spot_w < WIN_S), lane, -1000)
    target = lane[None, :] + 16 * jnp.arange(GROUP, dtype=jnp.int32)[:, None]
    return (target[:, :, None] == jnp.arange(512, dtype=jnp.int32)).astype(BF16)


def mask_operands(clip_row, frames):
    index = lax.axis_index("tm")
    wrapped = jnp.concatenate([clip_row, clip_row[:1]])
    own = lax.dynamic_slice_in_dim(wrapped, index * frames + SHIFT_T, 1)
    following = lax.dynamic_slice_in_dim(jnp.concatenate([clip_row, clip_row[:SHIFT_T]]), (index + 1) * frames, 1)
    differs = (own != following).astype(F32)
    token = jnp.arange(WIN_ROWS, dtype=jnp.int32)
    late = (token % 8 >= SHIFT_T).astype(F32)
    low = (token // 8 // WIN_S >= WIN_S - SHIFT_S).astype(F32)
    right = (token // 8 % WIN_S >= WIN_S - SHIFT_S).astype(F32)
    sides = jnp.stack([late, low, right], axis=1)
    window = jnp.arange(WINDOWS)
    weight = jnp.stack(
        [jnp.broadcast_to(differs, (WINDOWS,)), (window // 2).astype(F32), (window % 2).astype(F32)], axis=1
    )
    queries = jnp.concatenate([sides, 1.0 - sides], axis=1)
    keys = -BIG * jnp.concatenate([weight, weight], axis=1)[:, None, :] * jnp.concatenate([1.0 - sides, sides], axis=1)
    queries = jnp.pad(queries, ((0, 0), (0, GW - 6))).astype(BF16)
    keys = jnp.pad(keys, ((0, 0), (0, 0), (0, GW - 6))).astype(BF16)
    return (keys, queries)


def passed_along(value, axis, steps):
    count = lax.axis_size(axis)
    pairs = [(source, (source + steps) % count) for source in range(count)]
    return lax.ppermute(value, axis, pairs)


def to_windows(field):
    channels = field.shape[-1]
    return field.reshape(2, WIN_S, 2, WIN_S, WIN_T, channels).transpose(0, 2, 1, 3, 4, 5).reshape(WINDOWS, WIN_ROWS, channels)


def from_windows(windows):
    channels = windows.shape[-1]
    return windows.reshape(2, 2, WIN_S, WIN_S, WIN_T, channels).transpose(0, 2, 1, 3, 4, 5).reshape(SIDE, SIDE, WIN_T, channels)


def shift_in(field):
    ahead = passed_along(field[:, :, :SHIFT_T], "tm", -1)
    moved = jnp.concatenate([field[:, :, SHIFT_T:], ahead], axis=2)
    return to_windows(jnp.roll(moved, (-SHIFT_S, -SHIFT_S), axis=(0, 1)))


def shift_out(windows):
    moved = jnp.roll(from_windows(windows), (SHIFT_S, SHIFT_S), axis=(0, 1))
    behind = passed_along(moved[:, :, SHIFT_T:], "tm", 1)
    return jnp.concatenate([behind, moved[:, :, :SHIFT_T]], axis=2)


def layer_norm(values, gain_row, shift_row):
    center = values - jnp.mean(values, axis=-1, keepdims=True)
    spread = jnp.mean(center * center, axis=-1, keepdims=True)
    return center * lax.rsqrt(spread + 1e-05) * gain_row + shift_row


def layer_forward(current, layer_weights, place, aug):
    (gain_one, shift_one, weight_qkv, bias_query, bias_value, table_rows, weight_proj, bias_proj,
     gain_two, shift_two, weight_up, bias_up, weight_down, bias_down) = layer_weights
    rows = WINDOWS * WIN_ROWS
    table = spread_table(table_rows)
    normed_one = layer_norm(current, gain_one.astype(F32), shift_one.astype(F32)).astype(BF16)
    qkv_bias = jnp.concatenate([bias_query, jnp.zeros_like(bias_query), bias_value]).astype(F32)
    scales = jnp.concatenate([jnp.full((D,), QSCALE, F32), jnp.ones((2 * D,), F32)])
    qkv = ((dot_nn(normed_one, weight_qkv) + qkv_bias) * scales).astype(BF16).reshape(WINDOWS, WIN_ROWS, 3 * D)
    mixed, lse, bias = attention_forward(qkv, table, place, aug)
    attended = current + dot_nn(mixed.reshape(rows, D), weight_proj) + bias_proj.astype(F32)
    normed_two = layer_norm(attended, gain_two.astype(F32), shift_two.astype(F32)).astype(BF16)
    hidden = dot_nn(normed_two, weight_up) + bias_up.astype(F32)
    active = jax.nn.gelu(hidden, approximate=False).astype(BF16)
    result = attended + dot_nn(active, weight_down) + bias_down.astype(F32)
    return result, (current, normed_one, qkv, mixed, lse, bias, attended, normed_two, hidden, active)


def layer_backward(upstream, saved, layer_weights, place, aug):
    (gain_one, shift_one, weight_qkv, bias_query, bias_value, table_rows, weight_proj, bias_proj,
     gain_two, shift_two, weight_up, bias_up, weight_down, bias_down) = layer_weights
    (current, normed_one, qkv, mixed, lse, bias, attended, normed_two, hidden, active) = saved
    rows = WINDOWS * WIN_ROWS
    grad_out = upstream.astype(BF16)
    grad_down = dot_tn(active, grad_out)
    grad_bias_down = jnp.sum(grad_out, axis=0, dtype=F32)
    grad_active = dot_nt(grad_out, weight_down)
    gelu_back = jax.vjp(partial(jax.nn.gelu, approximate=False), hidden)[1]
    grad_hidden = gelu_back(grad_active)[0].astype(BF16)
    grad_up = dot_tn(normed_two, grad_hidden)
    grad_bias_up = jnp.sum(grad_hidden, axis=0, dtype=F32)
    grad_normed = dot_nt(grad_hidden, weight_up)
    norm_back = jax.vjp(layer_norm, attended, gain_two.astype(F32), shift_two.astype(F32))[1]
    grad_attended, grad_gain_two, grad_shift_two = norm_back(grad_normed)
    grad_attended = grad_attended + upstream
    grad_attn = grad_attended.astype(BF16)
    grad_proj = dot_tn(mixed.reshape(rows, D), grad_attn)
    grad_bias_proj = jnp.sum(grad_attn, axis=0, dtype=F32)
    grad_mixed = dot_nt(grad_attn, weight_proj).astype(BF16).reshape(WINDOWS, WIN_ROWS, D)
    dq, dk, dv, spread = attention_backward(qkv, mixed, grad_mixed, lse, bias, place, aug)
    dq, dk, dv = (part.reshape(rows, D) for part in (dq, dk, dv))
    grad_weight_qkv = jnp.concatenate([dot_tn(normed_one, part) for part in (dq, dk, dv)], axis=1)
    grad_normed = sum(dot_nt(part, weight_qkv[:, i * D : (i + 1) * D]) for i, part in enumerate((dq, dk, dv)))
    norm_back = jax.vjp(layer_norm, current, gain_one.astype(F32), shift_one.astype(F32))[1]
    grad_current, grad_gain_one, grad_shift_one = norm_back(grad_normed)
    layer_grads = (
        grad_gain_one, grad_shift_one, grad_weight_qkv, jnp.sum(dq, axis=0, dtype=F32), jnp.sum(dv, axis=0, dtype=F32),
        gather_table(spread), grad_proj, grad_bias_proj, grad_gain_two, grad_shift_two,
        grad_up, grad_bias_up, grad_down, grad_bias_down,
    )
    return grad_current + grad_attended, layer_grads


def body(inputs, clip_ids, *rest):
    weight_set, cotangent = rest[:-1], rest[-1]
    frames = inputs.shape[1]
    rows = WINDOWS * WIN_ROWS
    place = place_codes()
    aug = mask_operands(clip_ids[0], frames)
    layers = [tuple(member[index] for member in weight_set) for index in range(LAYERS)]
    upstream = shift_in(cotangent[0].transpose(1, 2, 0, 3)).reshape(rows, D).astype(F32)
    current = to_windows(inputs[0].transpose(1, 2, 0, 3)).reshape(rows, D).astype(F32)
    current, saved_first = layer_forward(current, layers[0], place, None)
    current = shift_in(from_windows(current.reshape(WINDOWS, WIN_ROWS, D))).reshape(rows, D)
    current, saved_second = layer_forward(current, layers[1], place, aug)
    block_output = shift_out(current.astype(BF16).reshape(WINDOWS, WIN_ROWS, D)).transpose(2, 0, 1, 3)
    upstream, grads_second = layer_backward(upstream, saved_second, layers[1], place, aug)
    upstream = to_windows(shift_out(upstream.reshape(WINDOWS, WIN_ROWS, D))).reshape(rows, D)
    upstream, grads_first = layer_backward(upstream, saved_first, layers[0], place, None)
    input_grad = from_windows(upstream.astype(BF16).reshape(WINDOWS, WIN_ROWS, D)).transpose(2, 0, 1, 3)
    stacked = [jnp.stack(pair) for pair in zip(grads_first, grads_second)]
    small_places = [0, 1, 3, 4, 5, 7, 8, 9, 11, 13]
    flat_small = jnp.concatenate([stacked[position].reshape(-1) for position in small_places])
    results = [None] * len(weight_set)
    for position in (2, 6, 10, 12):
        shard = lax.psum_scatter(stacked[position], "tm", scatter_dimension=1, tiled=True)
        results[position] = lax.psum(shard.astype(BF16), "dp").astype(F32)
    small_total = lax.psum(flat_small, ("dp", "tm"))
    offset = 0
    for position in small_places:
        member = stacked[position]
        results[position] = small_total[offset : offset + member.size].reshape(member.shape)
        offset = offset + member.size
    return (block_output.reshape(inputs.shape), input_grad.reshape(inputs.shape)) + tuple(results)


def solution(mesh):
    tokens = P("dp", "tm", None, None, None)
    split = P(None, "tm", None)
    placed = (tokens, P("dp", None)) + (P(),) * 14 + (tokens,)
    outs = (tokens, tokens, P(), P(), split, P(), P(), P(), split, P(), P(), P(), split, P(), split, P())
    return jax.shard_map(body, mesh=mesh, in_specs=placed, out_specs=outs, check_vma=False)
```

time: 3840 us -> 975 us (0.25)
  other arithmetic: 1940 us -> 77.7 us
  local copies, waits for them, and re-layouts: 1110 us -> 124 us
  matrix products: 566 us -> 194 us
  Pallas kernels: 0 us -> 202 us
  blocking collectives: 0 us -> 166 us
    scatter-add x2 -> x0, other arithmetic: 1640 us -> none  [layer_backward(): jax.ops.segment_sum(grad_bias_heads.reshape(HEADS, -1).T, table_index.res...]
    gather x4 -> x0, local copies, waits for them, and re-layouts: 673 us -> none  [layer_forward(): table_rows.astype(jnp.float32)[relative_index()]]
    dot_general x52 -> x32, matrix products: 566 us -> 194 us  [the longest x8 93.6 us: dot_nn(): lax.dot_general(a, b, (((1,), (0,)), ((), ())), preferred_element_type=F32)]
    pallas_call x0 -> x4, Pallas kernels: none -> 202 us  [the longest x2 104 us: attention_forward(): pl.pallas_call(partial(forward_kernel, masked), grid=(GROUPS, WINDOWS), i...]
    reduce_sum x14 -> x10, other arithmetic: 184 us -> 9.58 us  [the longest x2 3.76 us: layer_norm(): return center * lax.rsqrt(spread + 1e-05) * gain_row + shift_row]
    unnamed x0 -> x1, blocking collectives: none -> 166 us
    transpose x10 -> x7, local copies, waits for them, and re-layouts: 107 us -> 14.4 us  [the longest x2 9.68 us: spread_table(): rows = rows.transpose(0, 1, 3, 2).reshape(HEADS, WIN_T, 169 * WIN_T)]
    while x60 -> x0, local copies, waits for them, and re-layouts: 64 us -> none  [the longest x2 31.7 us: run_forward(): lax.map(partial(attend_forward, bias_heads=bias_heads, masked=masked), pa...]
  transfers between devices with their start and end apart: 10 -> 9, of which waited for: 5 -> 5; matrix products, arithmetic and copies ran while one was open for 66% -> 18% of each run, Pallas kernels for 0% -> 5%
where the time goes in v1:
time: 975 us; the launch traced here: 966 us
  Pallas kernels  202 us (21%)
  matrix products  194 us (20%)
  waiting for transfers between devices  176 us (18%)
  blocking collectives  166 us (17%)
  local copies, waits for them, and re-layouts  124 us (13%)
  other arithmetic  77.7 us (8%)
  between operations  19.7 us (2%)
    unnamed x1, blocking collectives  166 us
    psum x1, waiting for transfers between devices, body(): small_total = lax.psum(flat_small, ('dp', 'tm'))  118 us
    pallas_call x2, Pallas kernels, attention_forward(): pl.pallas_call(partial(forward_kernel, masked), grid=(GROUPS, WINDOWS), i...  104 us
    pallas_call x2, Pallas kernels, attention_backward(): pl.pallas_call(partial(backward_kernel, masked), grid=(GROUPS, WINDOWS),...  98.4 us
    dot_general x8, matrix products, dot_nn(): lax.dot_general(a, b, (((1,), (0,)), ((), ())), preferred_element_type=F32)  93.6 us
    dot_general x12, matrix products, dot_nt(): lax.dot_general(a, b, (((1,), (1,)), ((), ())), preferred_element_type=F32)  63.6 us
    dot_general x12, matrix products, dot_tn(): lax.dot_general(a, b, (((0,), (0,)), ((), ())), preferred_element_type=F32)  37 us
    unnamed x308, local copies, waits for them, and re-layouts  36.1 us
  transfers between devices with their start and end apart: 9, of which 5 were waited for; matrix products, arithmetic and copies ran while one was open for 18% of the time, Pallas kernels for 5%

profile of v1, /device:TPU:0, one launch (start us, length us, event | category | flops | bytes accessed | tf_op | source)
XLA Modules:
  0.0 966.1 jit_solution(488346996214861068)
XLA Ops:
  14.4 4.8 copy.157
  19.2 3.7 copy.158
  31.6 4.4 multiply_convert_fusion.3
  36.0 56.5 %attention_forward.2 = (bf16[4,392,512]{2,1,0:T(8,128)(2,1)}, f32[16,8,1664]{2,1,0:T(8,128)}, f32[4,392,1664]{2,1,0:T(8,128)}) custom-call(bf16[4,392,1536]{2,1,0:T(8,128)(2,1)} %bitcast.386, bf16[4,392,1536]{2,1,0:T(8,128)(2,1)} %bitcast.387, bf16[4,392,1536]{2,1,0:T(8,128)(2,1)} %bitcast.388, f32[4,4,8,1536]{3,2,1,0:T(8,128)} %convert.48.refs_3_, ...), custom_call_target="tpu_custom_call" | custom-call | tf_op jit(solution)/shard_map/attention_forward/pallas_call | solution.py:207
  92.6 3.7 fusion.131
  100.3 33.3 %multiply_convert_fusion.1 = (bf16[1568,2048]{1,0:T(8,128)(2,1)S(1)}, f32[1568,2048]{1,0:T(8,128)}, f32[1568,2048]{1,0:T(8,128)}) fusion(f32[2048]{0:T(1024)S(1)} %bitcast.494, bf16[2,512,2048]{2,1,0:T(8,128)(2,1)S(1)} %copy-done.133, f32[1568,512]{1,0:T(8,128)S(1)} %get-tuple-element.239, f32[512]{0:T(512)S(1)} %bitcast.514, f32[512]{0:T(512)S(1)} %bitcast.500, ...), kind=kOutput, calls=%fused_computation.21 | convolution fusion | flops 3504291840 | bytes 37449728 | tf_op jit(solution)/shard_map/dot_general | solution.py:41
  133.6 3.8 add_add_fusion.5
  139.6 5.4 collective-permute-start
  149.0 4.8 copy.166
  153.9 3.8 copy.167
  164.3 3.8 slice_bitcast_fusion.1
  168.1 4.2 collective-permute-done.2
  188.0 4.4 multiply_convert_fusion.2
  192.4 47.5 %attention_forward.3 = (bf16[4,392,512]{2,1,0:T(8,128)(2,1)}, f32[16,8,1664]{2,1,0:T(8,128)}, f32[4,392,1664]{2,1,0:T(8,128)}) custom-call(bf16[4,392,1536]{2,1,0:T(8,128)(2,1)} %bitcast.392, bf16[4,392,1536]{2,1,0:T(8,128)(2,1)} %bitcast.393, bf16[4,392,1536]{2,1,0:T(8,128)(2,1)} %bitcast.394, f32[4,4,8,1536]{3,2,1,0:T(8,128)} %convert.49.refs_3_, ...), custom_call_target="tpu_custom_call" | custom-call | tf_op jit(solution)/shard_map/attention_forward/pallas_call | solution.py:207
  239.9 3.7 fusion.132
  245.2 33.2 %multiply_convert_fusion = (bf16[1568,2048]{1,0:T(8,128)(2,1)}, f32[1568,2048]{1,0:T(8,128)}, f32[1568,2048]{1,0:T(8,128)}) fusion(f32[2048]{0:T(1024)S(1)} %bitcast.497, bf16[2,512,2048]{2,1,0:T(8,128)(2,1)S(1)} %copy-done.134, f32[1568,512]{1,0:T(8,128)S(1)} %get-tuple-element.242, f32[512]{0:T(512)S(1)} %bitcast.517, f32[512]{0:T(512)S(1)} %bitcast.505, ...), kind=kOutput, calls=%fused_computation.8 | convolution fusion | flops 3504291840 | bytes 37449728 | tf_op jit(solution)/shard_map/dot_general | solution.py:41
  278.4 16.7 %convert_reduce_fusion = (f32[2048]{0:T(1024)}, bf16[1568,2048]{1,0:T(8,128)(2,1)}) fusion(f32[1568,2048]{1,0:T(8,128)} %get-tuple-element.173, bf16[1568,512]{1,0:T(8,128)(2,1)S(1)} %bitcast.413, bf16[2,2048,512]{2,1,0:T(8,128)(2,1)} %param.31, f32[1568,2048]{1,0:T(8,128)} %get-tuple-element.243, f32[2048]{0:T(1024)S(1)} %bitcast.498), kind=kOutput, calls=%fused_computation.4 | convolution fusion | flops 3342923776 | bytes 35831808 | tf_op jit(solution)/shard_map/dot_general | solution.py:45
  295.2 8.1 multiply_reduce_fusion
  307.6 2.2 convolution_convert_fusion.1
  312.0 49.4 %attention_backward.2 = (bf16[4,392,512]{2,1,0:T(8,128)(2,1)}, bf16[4,392,512]{2,1,0:T(8,128)(2,1)}, bf16[4,392,512]{2,1,0:T(8,128)(2,1)}, f32[4,4,8,1536]{3,2,1,0:T(8,128)}) custom-call(bf16[4,392,1536]{2,1,0:T(8,128)(2,1)} %bitcast.395, bf16[4,392,1536]{2,1,0:T(8,128)(2,1)} %bitcast.396, bf16[4,392,1536]{2,1,0:T(8,128)(2,1)} %bitcast.397, ...), custom_call_target="tpu_custom_call" | custom-call | tf_op jit(solution)/shard_map/attention_backward/pallas_call | solution.py:230
  361.4 2.6 fusion.50
  377.0 20.8 %collective-permute-done.3 = f32[14,14,4,512]{3,2,1,0:T(4,128)S(1)} collective-permute-done((f32[14,14,4,512]{3,2,1,0:T(4,128)S(1)}, f32[14,14,4,512]{3,2,1,0:T(4,128)S(1)}, u32[]{:S(2)}, u32[]{:S(2)}) %collective-permute-start.3) | collective-permute-done | bytes 1605664 | tf_op jit(solution)/shard_map/ppermute | solution.py:301
  400.4 16.7 %convert_reduce_fusion.1 = (f32[2048]{0:T(1024)}, bf16[1568,2048]{1,0:T(8,128)(2,1)}) fusion(f32[1568,2048]{1,0:T(8,128)} %get-tuple-element.175, bf16[1568,512]{1,0:T(8,128)(2,1)S(1)} %bitcast.452, bf16[2,2048,512]{2,1,0:T(8,128)(2,1)} %param.31, f32[1568,2048]{1,0:T(8,128)} %get-tuple-element.240, f32[2048]{0:T(1024)S(1)} %bitcast.495), kind=kOutput, calls=%fused_computation.5 | convolution fusion | flops 3342923776 | bytes 35831808 | tf_op jit(solution)/shard_map/dot_general | solution.py:45
  417.2 8.7 multiply_reduce_fusion.1
  432.6 6.8 convolution_bitcast_fusion
  439.7 6.2 convolution_bitcast_fusion.1
  445.9 4.3 pad_maximum_fusion.1
  456.8 7.3 add_convert_fusion.3
  466.3 5.3 copy.185
  471.6 6.6 convolution_bitcast_fusion.2
  478.3 6.4 convolution_bitcast_fusion.3
  484.7 3.9 pad_maximum_fusion
  488.7 2.9 slice_bitcast_fusion.9
  502.9 6.7 collective-permute-done.1
  511.5 2.2 convolution_convert_fusion
  513.7 49.0 %attention_backward.3 = (bf16[4,392,512]{2,1,0:T(8,128)(2,1)}, bf16[4,392,512]{2,1,0:T(8,128)(2,1)}, bf16[4,392,512]{2,1,0:T(8,128)(2,1)}, f32[4,4,8,1536]{3,2,1,0:T(8,128)}) custom-call(bf16[4,392,1536]{2,1,0:T(8,128)(2,1)} %bitcast.389, bf16[4,392,1536]{2,1,0:T(8,128)(2,1)} %bitcast.390, bf16[4,392,1536]{2,1,0:T(8,128)(2,1)} %bitcast.391, ...), custom_call_target="tpu_custom_call" | custom-call | tf_op jit(solution)/shard_map/attention_backward/pallas_call | solution.py:230
  562.8 2.7 fusion.133
  570.0 3.4 pad_maximum_fusion.2
  573.5 10.7 %copy.181 = f32[2,512,1536]{2,0,1:T(2,128)} copy(f32[2,512,1536]{1,2,0:T(8,128)} %pad_maximum_fusion.2) | data formatting | bytes 12582912 | tf_op jit(solution)/shard_map/stack | solution.py:402
  586.7 4.0 copy.184
  590.7 3.0 slice_bitcast_fusion.17
  595.8 2.3 copy.180
  598.1 2.4 reshape.897
  609.3 8.0 concatenate.124
  617.3 165.8 %all-reduce.29 = bf16[2,512,1536]{2,0,1:T(2,128)(2,1)} all-reduce(f32[2,512,1536]{2,0,1:T(2,128)} %copy.181), channel_id=2, replica_groups=mesh['dp'=2,'tm'=16] {'tm'}, use_global_device_ids=true, to_apply=%region_35.36.clone | all-reduce | flops 1572864 | bytes 9437184
  790.3 4.9 add_convert_fusion.2
  796.6 118.3 %all-reduce.26.cloned.1.call-done = f32[93408]{0:T(1024)} async-done(((f32[93408]{0:T(1024)}), f32[93408]{0:T(1024)}) %all-reduce.26.cloned.1.call-update) | async-done | bytes 373648 | tf_op jit(solution)/shard_map/psum | solution.py:409
  925.7 26.0 %all-reduce.28.cloned.1.call-done = (bf16[2,32,1536]{2,0,1:T(2,128)(2,1)}, bf16[2,32,512]{2,1,0:T(8,128)(2,1)}, bf16[2,32,2048]{2,1,0:T(8,128)(2,1)}, bf16[2,128,512]{2,1,0:T(8,128)(2,1)}) async-done(((bf16[2,32,1536]{2,0,1:T(2,128)(2,1)}, bf16[2,32,512]{2,1,0:T(8,128)(2,1)}, bf16[2,32,2048]{2,1,0:T(8,128)(2,1)}, bf16[2,128,512]{2,1,0:T(8,128)(2,1)}), (bf16[2,32,1536]{2,0,1:T(2,128)(2,1)}, ...) | async-done | bytes 786448 | tf_op jit(solution)/shard_map/psum | solution.py:408
  (495 shorter events, 141.2 us)
Async XLA Ops:
  8.0 777.1 %reduce-scatter.4.cloned.1.call-start = ((), (), s32[]{:S(2)}) async-start(), calls=%async_computation.4 | async-start | bytes 2228224 | tf_op jit(solution)/shard_map/reduce_scatter | solution.py:407
  36.0 56.5 %copy-start.54 = (bf16[2,512,512]{2,1,0:T(8,128)(2,1)S(1)}, bf16[2,512,512]{2,1,0:T(8,128)(2,1)}, u32[]{:S(2)}) copy-start(bf16[2,512,512]{2,1,0:T(8,128)(2,1)} %param.25) | copy-start | bytes 3145732
  92.5 7.8 copy-start.133
  96.3 37.4 %copy-start.9 = (f32[1568,512]{1,0:T(8,128)}, f32[1568,512]{1,0:T(8,128)S(1)}, u32[]{:S(2)}) copy-start(f32[1568,512]{1,0:T(8,128)S(1)} %get-tuple-element.239) | copy-start | bytes 9633796
  96.3 37.2 %copy-start.76 = (f32[1568]{0:T(1024)}, f32[1568]{0:T(1024)S(1)}, u32[]{:S(2)}) copy-start(f32[1568]{0:T(1024)S(1)} %broadcast_multiply_fusion.2) | copy-start | bytes 18820
  97.9 35.7 %copy-start.89 = (f32[1568]{0:T(1024)}, f32[1568]{0:T(1024)S(1)}, u32[]{:S(2)}) copy-start(f32[1568]{0:T(1024)S(1)} %fusion.82) | copy-start | bytes 18820
  98.5 35.1 %copy-start.118 = (f32[1,512]{1,0:T(1,128)}, f32[1,512]{1,0:T(1,128)S(1)}, u32[]{:S(2)}) copy-start(f32[1,512]{1,0:T(1,128)S(1)} %get-tuple-element.227) | copy-start | bytes 6148
  99.1 34.4 %copy-start.113 = (f32[1,2048]{1,0:T(1,128)}, f32[1,2048]{1,0:T(1,128)S(1)}, u32[]{:S(2)}) copy-start(f32[1,2048]{1,0:T(1,128)S(1)} %get-tuple-element.221) | copy-start | bytes 24580
  99.7 33.9 %copy-start.125 = (f32[1,512]{1,0:T(1,128)}, f32[1,512]{1,0:T(1,128)S(1)}, u32[]{:S(2)}) copy-start(f32[1,512]{1,0:T(1,128)S(1)} %get-tuple-element.229) | copy-start | bytes 6148
  100.3 33.3 %copy-start.135 = (bf16[2,2048,512]{2,1,0:T(8,128)(2,1)S(1)}, bf16[2,2048,512]{2,1,0:T(8,128)(2,1)}, u32[]{:S(2)}) copy-start(bf16[2,2048,512]{2,1,0:T(8,128)(2,1)} %param.31) | copy-start | bytes 12582916
  139.6 38.7 %copy-start.17 = (f32[14,14,4,512]{3,2,1,0:T(4,128)}, f32[14,14,4,512]{3,2,1,0:T(4,128)S(1)}, u32[]{:S(2)}) copy-start(f32[14,14,4,512]{3,2,1,0:T(4,128)S(1)} %get-tuple-element.195) | copy-start | bytes 4816900
  139.6 8.0 copy-start.66
  139.6 37.9 %collective-permute-start = (f32[14,14,4,512]{3,2,1,0:T(4,128)}, f32[14,14,4,512]{3,2,1,0:T(4,128)S(1)}, u32[]{:S(2)}, u32[]{:S(2)}) collective-permute-start(f32[14,14,4,512]{3,2,1,0:T(4,128)} %get-tuple-element.194), channel_id=1, source_target_pairs={{0,15},{1,0},{2,1},{3,2},{4,3},{5,4},{6,5},{7,6},{8,7},{9,8},{10,9... | collective-permute-start | bytes 4816904 | tf_op jit(solution)/shard_map/ppermute | solution.py:301
  146.7 25.5 %collective-permute-start.2 = (bf16[14,14,4,512]{3,2,1,0:T(4,128)(2,1)}, bf16[14,14,4,512]{3,2,1,0:T(4,128)(2,1)}, u32[]{:S(2)}, u32[]{:S(2)}) collective-permute-start(bf16[14,14,4,512]{3,2,1,0:T(4,128)(2,1)} %get-tuple-element.198), channel_id=1, source_target_pairs={{0,15},{1,0},{2,1},{3,2},{4,3},{5,4},{6,5},{7,6},{8,7},{9,8},{10,9... | collective-permute-start | bytes 2408456 | tf_op jit(solution)/shard_map/ppermute | solution.py:301
  163.6 8.6 copy-start.26
  192.3 47.5 %copy-start.55 = (bf16[2,512,512]{2,1,0:T(8,128)(2,1)S(1)}, bf16[2,512,512]{2,1,0:T(8,128)(2,1)}, u32[]{:S(2)}) copy-start(bf16[2,512,512]{2,1,0:T(8,128)(2,1)} %param.25) | copy-start | bytes 3145732
  192.3 47.5 %copy-start.122 = (f32[1,512]{1,0:T(1,128)S(1)}, f32[1,512]{1,0:T(1,128)}, u32[]{:S(2)}) copy-start(f32[1,512]{1,0:T(1,128)} %get-tuple-element.230) | copy-start | bytes 6148
  243.6 59.7 %copy-start.13 = (f32[1568,512]{1,0:T(8,128)}, f32[1568,512]{1,0:T(8,128)S(1)}, u32[]{:S(2)}) copy-start(f32[1568,512]{1,0:T(8,128)S(1)} %get-tuple-element.242) | copy-start | bytes 9633796
  243.6 59.6 %copy-start.79 = (f32[1568]{0:T(1024)}, f32[1568]{0:T(1024)S(1)}, u32[]{:S(2)}) copy-start(f32[1568]{0:T(1024)S(1)} %broadcast_multiply_fusion.1) | copy-start | bytes 18820
  244.3 59.0 %copy-start.92 = (f32[1568]{0:T(1024)}, f32[1568]{0:T(1024)S(1)}, u32[]{:S(2)}) copy-start(f32[1568]{0:T(1024)S(1)} %fusion.83) | copy-start | bytes 18820
  245.2 33.2 %copy-start.19 = (bf16[2,7,2,7,8,512]{5,4,3,1,2,0:T(8,128)(2,1)S(1)}, bf16[2,7,2,7,8,512]{5,4,3,1,2,0:T(8,128)(2,1)}, u32[]{:S(2)}) copy-start(bf16[2,7,2,7,8,512]{5,4,3,1,2,0:T(8,128)(2,1)} %copy.171) | copy-start | bytes 4816900
  295.2 8.1 copy-start.75
  312.0 49.4 %copy-start.38 = (bf16[512,1536]{1,0:T(8,128)(2,1)S(1)}, bf16[512,1536]{1,0:T(8,128)(2,1)}, u32[]{:S(2)}) copy-start(bf16[512,1536]{1,0:T(8,128)(2,1)} %get-tuple-element.197) | copy-start | bytes 4718596
  374.7 23.1 %collective-permute-start.3 = (f32[14,14,4,512]{3,2,1,0:T(4,128)S(1)}, f32[14,14,4,512]{3,2,1,0:T(4,128)S(1)}, u32[]{:S(2)}, u32[]{:S(2)}) collective-permute-start(f32[14,14,4,512]{3,2,1,0:T(4,128)S(1)} %get-tuple-element.192), channel_id=1, source_target_pairs={{0,1},{1,2},{2,3},{3,4},{4,5},{5,6},{6,7},{7,8},{8,9},{9,10},{10,1... | collective-permute-start | bytes 4816904 | tf_op jit(solution)/shard_map/ppermute | solution.py:301
  398.8 40.7 %copy-start.2 = (f32[2,2,7,7,8,512]{5,4,3,2,1,0:T(8,128)}, f32[2,2,7,7,8,512]{5,4,3,2,1,0:T(8,128)S(1)}, u32[]{:S(2)}) copy-start(f32[2,2,7,7,8,512]{5,4,3,2,1,0:T(8,128)S(1)} %copy.174) | copy-start | bytes 9633796
  400.4 16.7 %copy-start.10 = (f32[1568,512]{1,0:T(8,128)S(1)}, f32[1568,512]{1,0:T(8,128)}, u32[]{:S(2)}) copy-start(f32[1568,512]{1,0:T(8,128)} %copy-done.9) | copy-start | bytes 9633796
  400.4 16.7 %copy-start.77 = (f32[1568]{0:T(1024)S(1)}, f32[1568]{0:T(1024)}, u32[]{:S(2)}) copy-start(f32[1568]{0:T(1024)} %copy-done.76) | copy-start | bytes 18820
  400.4 16.7 %copy-start.90 = (f32[1568]{0:T(1024)S(1)}, f32[1568]{0:T(1024)}, u32[]{:S(2)}) copy-start(f32[1568]{0:T(1024)} %copy-done.89) | copy-start | bytes 18820
  400.4 16.7 %copy-start.119 = (f32[1,512]{1,0:T(1,128)S(1)}, f32[1,512]{1,0:T(1,128)}, u32[]{:S(2)}) copy-start(f32[1,512]{1,0:T(1,128)} %copy-done.118) | copy-start | bytes 6148
  417.1 8.7 copy-start.73
  432.6 354.1 %reduce-scatter.8.cloned.1.call-start = ((), (), s32[]{:S(2)}) async-start(), calls=%async_computation.6 | async-start | bytes 8912896 | tf_op jit(solution)/shard_map/reduce_scatter | solution.py:407
  450.3 338.2 %reduce-scatter.6.cloned.1.call-start = ((), (), s32[]{:S(2)}) async-start(), calls=%async_computation.5 | async-start | bytes 8912896 | tf_op jit(solution)/shard_map/reduce_scatter | solution.py:407
  488.6 426.3 %all-reduce.26.cloned.1.call-start = ((), (), s32[]{:S(2)}) async-start(), calls=%async_computation.3 | async-start | bytes 753664 | tf_op jit(solution)/shard_map/psum | solution.py:409
  495.1 14.5 %collective-permute-start.1 = (bf16[14,14,4,512]{3,2,1,0:T(4,128)(2,1)S(1)}, bf16[14,14,4,512]{3,2,1,0:T(4,128)(2,1)S(1)}, u32[]{:S(2)}, u32[]{:S(2)}) collective-permute-start(bf16[14,14,4,512]{3,2,1,0:T(4,128)(2,1)S(1)} %get-tuple-element.200), channel_id=1, source_target_pairs={{0,1},{1,2},{2,3},{3,4},{4,5},{5,6},{6,7},{7,8},{8,9},{9,10},{10,1... | collective-permute-start | bytes 2408456 | tf_op jit(solution)/shard_map/ppermute | solution.py:301
  500.8 10.7 %copy-start.36 = (bf16[1568,512]{1,0:T(8,128)(2,1)S(1)}, bf16[1568,512]{1,0:T(8,128)(2,1)}, u32[]{:S(2)}) copy-start(bf16[1568,512]{1,0:T(8,128)(2,1)} %copy-done.35) | copy-start | bytes 4816900
  500.9 10.7 %copy-start.57 = (bf16[2,512,512]{2,1,0:T(8,128)(2,1)S(1)}, bf16[2,512,512]{2,1,0:T(8,128)(2,1)}, u32[]{:S(2)}) copy-start(bf16[2,512,512]{2,1,0:T(8,128)(2,1)} %param.25) | copy-start | bytes 3145732
  513.7 49.0 %copy-start.50 = (bf16[2,2,7,7,8,512]{5,4,3,2,1,0:T(8,128)(2,1)S(1)}, bf16[2,2,7,7,8,512]{5,4,3,2,1,0:T(8,128)(2,1)}, u32[]{:S(2)}) copy-start(bf16[2,2,7,7,8,512]{5,4,3,2,1,0:T(8,128)(2,1)} %copy-done.49) | copy-start | bytes 4816900
  573.4 10.7 %copy-start.115 = (f32[2048]{0:T(1024)S(1)}, f32[2048]{0:T(1024)}, u32[]{:S(2)}) copy-start(f32[2048]{0:T(1024)} %get-tuple-element.248) | copy-start | bytes 24580
  573.4 10.7 %copy-start.117 = (f32[2048]{0:T(1024)S(1)}, f32[2048]{0:T(1024)}, u32[]{:S(2)}) copy-start(f32[2048]{0:T(1024)} %get-tuple-element.250) | copy-start | bytes 24580
  573.4 11.4 %copy-start.130 = (f32[512]{0:T(512)S(1)}, f32[512]{0:T(512)}, u32[]{:S(2)}) copy-start(f32[512]{0:T(512)} %get-tuple-element.149) | copy-start | bytes 6148
  573.4 11.4 %copy-start.132 = (f32[512]{0:T(512)S(1)}, f32[512]{0:T(512)}, u32[]{:S(2)}) copy-start(f32[512]{0:T(512)} %get-tuple-element.148) | copy-start | bytes 6148
  573.4 12.0 %copy-start.129 = (f32[512]{0:T(512)S(1)}, f32[512]{0:T(512)}, u32[]{:S(2)}) copy-start(f32[512]{0:T(512)} %get-tuple-element.142) | copy-start | bytes 6148
  573.4 12.0 %copy-start.131 = (f32[512]{0:T(512)S(1)}, f32[512]{0:T(512)}, u32[]{:S(2)}) copy-start(f32[512]{0:T(512)} %get-tuple-element.140) | copy-start | bytes 6148
  573.5 12.6 %copy-start.101 = (f32[512]{0:T(512)S(1)}, f32[512]{0:T(512)}, u32[]{:S(2)}) copy-start(f32[512]{0:T(512)} %get-tuple-element.166) | copy-start | bytes 6148
  573.5 12.5 %copy-start.123 = (f32[512]{0:T(512)S(1)}, f32[512]{0:T(512)}, u32[]{:S(2)}) copy-start(f32[512]{0:T(512)} %get-tuple-element.164) | copy-start | bytes 6148
  573.5 13.1 %copy-start.61 = (f32[4,4,8,1536]{3,2,1,0:T(8,128)S(1)}, f32[4,4,8,1536]{3,2,1,0:T(8,128)}, u32[]{:S(2)}) copy-start(f32[4,4,8,1536]{3,2,1,0:T(8,128)} %get-tuple-element.42) | copy-start | bytes 2359300
  617.3 167.8 %copy-start.86 = (f32[1568]{0:T(1024)S(1)}, f32[1568]{0:T(1024)}, u32[]{:S(2)}) copy-start(f32[1568]{0:T(1024)} %get-tuple-element.145) | copy-start | bytes 18820
  785.0 166.7 %all-reduce.28.cloned.1.call-start = ((), (), s32[]{:S(2)}) async-start(), calls=%async_computation.7 | async-start | bytes 1572864 | tf_op jit(solution)/shard_map/psum | solution.py:408
  (101 other events, 291.8 us)
Sparse Core Ops, SparseCore 0:
  432.7 59.0 reduce-scatter.3
  495.9 102.2 reduce-scatter.7
  602.3 143.9 reduce-scatter.5
Sparse Core Ops, SparseCore 1:
  785.1 129.7 all-reduce.25
  917.8 33.9 all-reduce.27

commit v2 on v1

v2 whole, which is shorter than its diff:
```python
from functools import partial
import math

import jax
import jax.numpy as jnp
from jax import lax
from jax.experimental import pallas as pl
from jax.experimental.pallas import tpu as pltpu
from jax.sharding import PartitionSpec as P

D = 512
HEADS = 16
HEAD_DIM = 32
FF = 2048
SIDE = 14
WIN_T = 8
WIN_S = 7
SHIFT_T = 4
SHIFT_S = 3
LAYERS = 2
WIN_ROWS = 392
TABLE_ROWS = 2535
WINDOWS = 4
GROUP = 4
GROUPS = HEADS // GROUP
GW = GROUP * HEAD_DIM
HS = 400
LANES = 1664
OT_LANES = 1792
CODE = 768
BASE = 1536
LOG2E = 1.4426950408889634
QSCALE = HEAD_DIM ** (-0.5) * LOG2E
BIG = 1e30
F32 = jnp.float32
BF16 = jnp.bfloat16
CHUNKS = [(256 * c, 256) for c in range(6)] + [(1536, 128)]


def dot_nn(a, b):
    return lax.dot_general(a, b, (((1,), (0,)), ((), ())), preferred_element_type=F32)


def dot_nt(a, b):
    return lax.dot_general(a, b, (((1,), (1,)), ((), ())), preferred_element_type=F32)


def dot_tn(a, b):
    return lax.dot_general(a, b, (((0,), (0,)), ((), ())), preferred_element_type=F32)


def code_shift(spot):
    return 8 * (84 - (spot // WIN_S * 13 + spot % WIN_S))


def head_lanes(rows):
    return lax.broadcasted_iota(jnp.int32, (rows, GW), 1) // HEAD_DIM


def stack_heads(stack_ref, block):
    lane_head = head_lanes(WIN_ROWS)
    zero = jnp.zeros((), block.dtype)
    for h in range(GROUP):
        stack_ref[HS * h : HS * h + WIN_ROWS, :GW] = jnp.where(lane_head == h, block, zero)


def clear_gaps(stack_ref):
    width = stack_ref.shape[1]
    for h in range(GROUP):
        stop = HS * (h + 1) if h < GROUP - 1 else LANES
        stack_ref[HS * h + 384 : stop, :] = jnp.zeros((stop - HS * h - 384, width), stack_ref.dtype)


def unstack(turned_ref):
    picked = []
    for h in range(GROUP):
        rows = turned_ref[HEAD_DIM * h : HEAD_DIM * (h + 1), 384 * h : 384 * h + 512 + 128]
        if h:
            rows = pltpu.roll(rows, 640 - 16 * h, axis=1)
        picked.append(rows[:, :512])
    return jnp.concatenate(picked, axis=0).T[:WIN_ROWS]


def build_bias(tab_ref, place_ref, bias_ref, rolled):
    bias_ref[...] = jnp.zeros((WIN_ROWS, LANES), F32)
    for h in range(GROUP):
        base = tab_ref[0, h]
        for spot in range(49):
            shift = code_shift(spot)
            rolled[8 * spot : 8 * spot + 8, :] = pltpu.roll(base, BASE - shift, axis=1)[:, :CODE]
        part = dot_nn(rolled[...].astype(BF16), place_ref[h])
        bias_ref[:, 384 * h : 384 * h + 512] += part * LOG2E


def forward_kernel(masked, *refs):
    if masked:
        (q_ref, k_ref, v_ref, tab_ref, place_ref, kaug_ref, qaug_ref, o_ref, inv_ref, e_ref, stack, rolled, turned, bias_sum) = refs
    else:
        (q_ref, k_ref, v_ref, tab_ref, place_ref, o_ref, inv_ref, e_ref, stack, rolled, turned, bias_sum) = refs

    @pl.when((pl.program_id(0) == 0) & (pl.program_id(1) == 0))
    def _():
        clear_gaps(stack)
        if masked:
            for h in range(GROUP):
                stack[HS * h : HS * h + WIN_ROWS, GW:] = qaug_ref[...]

    @pl.when(pl.program_id(1) == 0)
    def _():
        build_bias(tab_ref, place_ref, bias_sum, rolled)

    stack_heads(stack, q_ref[0])
    keys = k_ref[0]
    if masked:
        keys = jnp.concatenate([keys, kaug_ref[0]], axis=1)
    values = v_ref[0].astype(F32).T
    values = jnp.concatenate([values, jnp.ones((16, WIN_ROWS), F32)], axis=0).astype(BF16)
    for start, width in CHUNKS:
        scores = dot_nt(keys, stack[start : start + width, :]) + bias_sum[:, start : start + width]
        top = jnp.max(scores, axis=0, keepdims=True)
        e_ref[0, :, start : start + width] = jnp.exp2(scores - top).astype(BF16)
    for start, width in CHUNKS:
        mixed = dot_nn(values, e_ref[0, :, start : start + width])
        inverse = 1.0 / mixed[GW : GW + 8]
        turned[:, start : start + width] = mixed[:GW] * inverse[:1]
        inv_ref[0, :, start : start + width] = inverse
    o_ref[0] = unstack(turned).astype(BF16)


def backward_kernel(q_ref, k_ref, v_ref, do_ref, inv_ref, e_ref, place_ref,
                    dq_ref, dk_ref, dv_ref, dtab_ref, stack, dstack, probs, slopes, turned, bias_sum):
    @pl.when((pl.program_id(0) == 0) & (pl.program_id(1) == 0))
    def _():
        clear_gaps(stack)
        clear_gaps(dstack)

    @pl.when(pl.program_id(1) == 0)
    def _():
        bias_sum[...] = jnp.zeros_like(bias_sum)

    stack_heads(stack, q_ref[0])
    stack_heads(dstack, do_ref[0])
    keys_turned = k_ref[0].astype(F32).T.astype(BF16)
    values = v_ref[0]
    for start, width in CHUNKS:
        lanes = slice(start, start + width)
        chances = e_ref[0, :, lanes].astype(F32) * inv_ref[0, :1, lanes]
        slope = chances * dot_nt(values, dstack[lanes, :])
        slope = slope - chances * jnp.sum(slope, axis=0, keepdims=True)
        probs[:, lanes] = chances.astype(BF16)
        slopes[:, lanes] = slope.astype(BF16)
        bias_sum[:, lanes] += slope
    dv_ref[0] = dot_nn(probs[...], dstack[...]).astype(BF16)
    dk_ref[0] = (dot_nn(slopes[...], stack[...]) * math.log(2.0)).astype(BF16)
    for start, width in CHUNKS:
        turned[:, start : start + width] = dot_nn(keys_turned, slopes[:, start : start + width])
    dq_ref[0] = (unstack(turned) * HEAD_DIM ** (-0.5)).astype(BF16)

    @pl.when(pl.program_id(1) == WINDOWS - 1)
    def _():
        dtab_ref[...] = jnp.zeros_like(dtab_ref)
        pad = jnp.zeros((8, BASE - CODE), F32)
        for h in range(GROUP):
            coded = dot_nt(bias_sum[:, 384 * h : 384 * h + 512].astype(BF16), place_ref[h])
            total = jnp.zeros((8, BASE), F32)
            for spot in range(49):
                piece = jnp.concatenate([coded[8 * spot : 8 * spot + 8], pad], axis=1)
                total = total + pltpu.roll(piece, code_shift(spot), axis=1)
            dtab_ref[0, h] = total


def busy(microseconds):
    return pl.CostEstimate(flops=microseconds * 1_000_000_000, bytes_accessed=microseconds * 1_000_000, transcendentals=0)


def head_block(part):
    return pl.BlockSpec((1, WIN_ROWS, GW), lambda g, w: (w, 0, part * GROUPS + g))


PLAIN = pl.BlockSpec((1, WIN_ROWS, GW), lambda g, w: (w, 0, g))
INV = pl.BlockSpec((1, 8, LANES), lambda g, w: (g * WINDOWS + w, 0, 0))
EXPS = pl.BlockSpec((1, WIN_ROWS, LANES), lambda g, w: (g * WINDOWS + w, 0, 0))
TABLE = pl.BlockSpec((1, GROUP, 8, BASE), lambda g, w: (g, 0, 0, 0))
PLACE = pl.BlockSpec((GROUP, CODE, 512), lambda g, w: (0, 0, 0), pipeline_mode=pl.Buffered(1))
KAUG = pl.BlockSpec((1, WIN_ROWS, GW), lambda g, w: (w, 0, 0))
QAUG = pl.BlockSpec((WIN_ROWS, GW), lambda g, w: (0, 0))
VMEM_LIMIT = 62 * 1024 * 1024


def attention_forward(qkv, table, place, aug):
    masked = aug is not None
    wide = 2 * GW if masked else GW
    return pl.pallas_call(
        partial(forward_kernel, masked),
        grid=(GROUPS, WINDOWS),
        in_specs=[head_block(0), head_block(1), head_block(2), TABLE, PLACE] + ([KAUG, QAUG] if masked else []),
        out_specs=[PLAIN, INV, EXPS],
        out_shape=[
            jax.ShapeDtypeStruct((WINDOWS, WIN_ROWS, D), BF16),
            jax.ShapeDtypeStruct((GROUPS * WINDOWS, 8, LANES), F32),
            jax.ShapeDtypeStruct((GROUPS * WINDOWS, WIN_ROWS, LANES), BF16),
        ],
        scratch_shapes=[
            pltpu.VMEM((LANES, wide), BF16),
            pltpu.VMEM((WIN_ROWS, CODE), F32),
            pltpu.VMEM((GW, OT_LANES), F32),
            pltpu.VMEM((WIN_ROWS, LANES), F32),
        ],
        compiler_params=pltpu.CompilerParams(vmem_limit_bytes=VMEM_LIMIT),
        cost_estimate=busy(31),
        name="attention_forward",
    )(qkv, qkv, qkv, table, place, *(aug or ()))


def attention_backward(qkv, grad_mixed, inverse, exps, place):
    return pl.pallas_call(
        backward_kernel,
        grid=(GROUPS, WINDOWS),
        in_specs=[head_block(0), head_block(1), head_block(2), PLAIN, INV, EXPS, PLACE],
        out_specs=[PLAIN, PLAIN, PLAIN, TABLE],
        out_shape=[jax.ShapeDtypeStruct((WINDOWS, WIN_ROWS, D), BF16)] * 3
        + [jax.ShapeDtypeStruct((GROUPS, GROUP, 8, BASE), F32)],
        scratch_shapes=[
            pltpu.VMEM((LANES, GW), BF16),
            pltpu.VMEM((LANES, GW), BF16),
            pltpu.VMEM((WIN_ROWS, LANES), BF16),
            pltpu.VMEM((WIN_ROWS, LANES), BF16),
            pltpu.VMEM((GW, OT_LANES), F32),
            pltpu.VMEM((WIN_ROWS, LANES), F32),
        ],
        compiler_params=pltpu.CompilerParams(vmem_limit_bytes=VMEM_LIMIT),
        cost_estimate=busy(52),
        name="attention_backward",
    )(qkv, qkv, qkv, grad_mixed, inverse, exps, place)


def spread_table(table_rows):
    cube = table_rows.T.reshape(HEADS, 15, 169)
    rows = jnp.stack([cube[:, 7 - tj : 15 - tj] for tj in range(WIN_T)], axis=1)
    rows = rows.transpose(0, 1, 3, 2).reshape(HEADS, WIN_T, 169 * WIN_T)
    rows = jnp.pad(rows, ((0, 0), (0, 0), (0, BASE - 169 * WIN_T)))
    return rows.reshape(GROUPS, GROUP, WIN_T, BASE).astype(F32)


def gather_table(spread):
    rows = spread.reshape(HEADS, WIN_T, BASE)[:, :, : 169 * WIN_T].reshape(HEADS, WIN_T, 169, WIN_T)
    rows = rows.transpose(0, 1, 3, 2)
    total = sum(
        jnp.pad(rows[:, tj], ((0, 0), (7 - tj, tj), (0, 0))) for tj in range(WIN_T)
    )
    return total.reshape(HEADS, TABLE_ROWS).T


def place_codes():
    code = jnp.arange(CODE, dtype=jnp.int32)
    spot_h, spot_w = code // 8 // 13, code // 8 % 13
    lane = (spot_h * WIN_S + spot_w) * 8 + code % 8
    lane = jnp.where((spot_h < WIN_S) & (spot_w < WIN_S), lane, -1000)
    target = lane[None, :] + 16 * jnp.arange(GROUP, dtype=jnp.int32)[:, None]
    return (target[:, :, None] == jnp.arange(512, dtype=jnp.int32)).astype(BF16)


def mask_operands(clip_row, frames):
    index = lax.axis_index("tm")
    wrapped = jnp.concatenate([clip_row, clip_row[:1]])
    own = lax.dynamic_slice_in_dim(wrapped, index * frames + SHIFT_T, 1)
    following = lax.dynamic_slice_in_dim(jnp.concatenate([clip_row, clip_row[:SHIFT_T]]), (index + 1) * frames, 1)
    differs = (own != following).astype(F32)
    token = jnp.arange(WIN_ROWS, dtype=jnp.int32)
    late = (token % 8 >= SHIFT_T).astype(F32)
    low = (token // 8 // WIN_S >= WIN_S - SHIFT_S).astype(F32)
    right = (token // 8 % WIN_S >= WIN_S - SHIFT_S).astype(F32)
    sides = jnp.stack([late, low, right], axis=1)
    window = jnp.arange(WINDOWS)
    weight = jnp.stack(
        [jnp.broadcast_to(differs, (WINDOWS,)), (window // 2).astype(F32), (window % 2).astype(F32)], axis=1
    )
    queries = jnp.concatenate([sides, 1.0 - sides], axis=1)
    keys = -BIG * jnp.concatenate([weight, weight], axis=1)[:, None, :] * jnp.concatenate([1.0 - sides, sides], axis=1)
    queries = jnp.pad(queries, ((0, 0), (0, GW - 6))).astype(BF16)
    keys = jnp.pad(keys, ((0, 0), (0, 0), (0, GW - 6))).astype(BF16)
    return (keys, queries)


TAIL_SLOPE = 0.21
TAIL_POLY = (
    -0.07194446913289963, 0.2849435841958524, -0.3329670889498132, 0.35241963260033626, -0.09596225895564263,
    0.12572571978855923, 0.06897590427205952, 0.0850992002684089, 0.08370977184002107,
)


def gelu_and_slope(u):
    t = 1.0 / (1.0 + TAIL_SLOPE * jnp.abs(u))
    tail = TAIL_POLY[0] * t + TAIL_POLY[1]
    for coefficient in TAIL_POLY[2:]:
        tail = tail * t + coefficient
    bell = jnp.exp2(u * u * (-0.5 * LOG2E))
    tail = tail * t * bell
    chance = jnp.where(u >= 0.0, 1.0 - tail, tail)
    return u * chance, chance + u * bell * (1.0 / math.sqrt(2.0 * math.pi))


def normalized(values):
    center = values - jnp.mean(values, axis=1, keepdims=True)
    scale = lax.rsqrt(jnp.mean(center * center, axis=1, keepdims=True) + 1e-05)
    return center * scale, scale


def norm_backward(grad_normed, gain, shape, scale):
    e = grad_normed * gain
    return scale * (e - jnp.mean(e, axis=1, keepdims=True) - shape * jnp.mean(e * shape, axis=1, keepdims=True))


def turned_low(block):
    return block.astype(F32).T.astype(BF16)


def column_sum(block):
    return jnp.sum(block, axis=0, keepdims=True)


def project_in_kernel(layer, x_ref, gain_ref, shift_ref, w_ref, qb_ref, vb_ref, n_ref, qkv_ref):
    row = slice(layer, layer + 1)
    shape, _ = normalized(x_ref[0].astype(F32))
    n = (shape * gain_ref[row].astype(F32) + shift_ref[row].astype(F32)).astype(BF16)
    n_ref[0] = n
    qkv_ref[0, :, :D] = ((dot_nn(n, w_ref[0, :, :D]) + qb_ref[row].astype(F32)) * QSCALE).astype(BF16)
    qkv_ref[0, :, D : 2 * D] = dot_nn(n, w_ref[0, :, D : 2 * D]).astype(BF16)
    qkv_ref[0, :, 2 * D :] = (dot_nn(n, w_ref[0, :, 2 * D :]) + vb_ref[row].astype(F32)).astype(BF16)


def feed_forward_kernel(layer, x_ref, o_ref, wp_ref, wu_ref, wd_ref, bp_ref, gain_ref, shift_ref, bu_ref, bd_ref,
                        x1_ref, n_ref, act_ref, slope_ref, x2_ref):
    row = slice(layer, layer + 1)
    x1 = x_ref[0].astype(F32) + dot_nn(o_ref[0], wp_ref[0]) + bp_ref[row].astype(F32)
    x1_ref[0] = x1
    shape, _ = normalized(x1)
    n = (shape * gain_ref[row].astype(F32) + shift_ref[row].astype(F32)).astype(BF16)
    n_ref[0] = n
    total = x1 + bd_ref[row].astype(F32)
    for c in range(4):
        for part in (0, 1):
            cols = slice(512 * c + 256 * part, 512 * c + 256 * part + 256)
            g, slope = gelu_and_slope(dot_nn(n, wu_ref[0, :, cols]) + bu_ref[row, cols].astype(F32))
            act_ref[0, :, cols] = g.astype(BF16)
            slope_ref[0, :, cols] = slope.astype(BF16)
        wide = slice(512 * c, 512 * c + 512)
        total = total + dot_nn(act_ref[0, :, wide], wd_ref[0, wide, :])
    x2_ref[0] = total.astype(x2_ref.dtype)


def feed_backward_kernel(layer, shards, dz_ref, x1_ref, n_ref, o_ref, act_ref, slope_ref, wp_ref, wu_ref, wd_ref, gain_ref,
                         dx1_ref, do_ref, sums_ref, *rest):
    grads, (du, acc_up, acc_down, acc_proj) = rest[:-4], rest[-4:]
    row = slice(layer, layer + 1)
    step = pl.program_id(0)

    @pl.when(step == 0)
    def _():
        sums_ref[...] = jnp.zeros_like(sums_ref)
        acc_up[...] = jnp.zeros_like(acc_up)
        acc_down[...] = jnp.zeros_like(acc_down)
        acc_proj[...] = jnp.zeros_like(acc_proj)

    dz = dz_ref[0].astype(F32)
    dm = dz.astype(BF16)
    dm_turned = turned_low(dm)
    n_turned = turned_low(n_ref[0])
    dn = jnp.zeros((WIN_ROWS, D), F32)
    for c in range(4):
        for part in (0, 1):
            cols = slice(512 * c + 256 * part, 512 * c + 256 * part + 256)
            grad = dot_nt(dm, wd_ref[0, cols, :]) * slope_ref[0, :, cols].astype(F32)
            low = grad.astype(BF16)
            du[:, cols] = low
            sums_ref[0:1, cols] += column_sum(low.astype(F32))
        wide = slice(512 * c, 512 * c + 512)
        acc_down[:, wide] += dot_nn(dm_turned, act_ref[0, :, wide])
        acc_up[:, wide] += dot_nn(n_turned, du[:, wide])
        dn = dn + dot_nt(du[:, wide], wu_ref[0, :, wide])
    shape, scale = normalized(x1_ref[0])
    dx1 = dz + norm_backward(dn, gain_ref[row].astype(F32), shape, scale)
    dx1_ref[0] = dx1
    da = dx1.astype(BF16)
    do_ref[0] = dot_nt(da, wp_ref[0]).astype(BF16)
    acc_proj[...] += dot_nn(turned_low(o_ref[0]), da)
    sums_ref[1:2, :] += jnp.concatenate(
        [column_sum(dm.astype(F32)), column_sum(da.astype(F32)), column_sum(dn * shape), column_sum(dn)], axis=1
    )

    @pl.when(step == WINDOWS - 1)
    def _():
        if shards == 16:
            (packed,) = grads
            for s in range(16):
                for c in range(16):
                    packed[s, 32 * c : 32 * c + 32, :] = acc_up[32 * s : 32 * s + 32, 128 * c : 128 * c + 128].astype(BF16)
                packed[s, 512:1024, :] = acc_down[:, 128 * s : 128 * s + 128].astype(BF16)
                for c in range(4):
                    packed[s, 1024 + 32 * c : 1056 + 32 * c, :] = acc_proj[32 * s : 32 * s + 32, 128 * c : 128 * c + 128].astype(BF16)
        else:
            for target, source in zip(grads, (acc_up, acc_down, acc_proj)):
                target[...] = source[...].astype(BF16)


def project_back_kernel(layer, shards, dq_ref, dk_ref, dv_ref, n_ref, x_ref, dx1_ref, w_ref, gain_ref, dx_ref, sums_ref, grad_ref, acc):
    row = slice(layer, layer + 1)
    step = pl.program_id(0)

    @pl.when(step == 0)
    def _():
        sums_ref[...] = jnp.zeros_like(sums_ref)
        acc[...] = jnp.zeros_like(acc)

    n_turned = turned_low(n_ref[0])
    dn = jnp.zeros((WIN_ROWS, D), F32)
    for i, part in enumerate((dq_ref, dk_ref, dv_ref)):
        cols = slice(D * i, D * i + D)
        dn = dn + dot_nt(part[0], w_ref[0, :, cols])
        acc[:, cols] += dot_nn(n_turned, part[0])
    shape, scale = normalized(x_ref[0].astype(F32))
    dx_ref[0] = (dx1_ref[0] + norm_backward(dn, gain_ref[row].astype(F32), shape, scale)).astype(dx_ref.dtype)
    sums_ref[0:1, :] += jnp.concatenate(
        [column_sum(dq_ref[0].astype(F32)), column_sum(dv_ref[0].astype(F32)), column_sum(dn * shape), column_sum(dn)], axis=1
    )

    @pl.when(step == WINDOWS - 1)
    def _():
        if shards == 16:
            for s in range(16):
                for c in range(12):
                    grad_ref[s, 32 * c : 32 * c + 32, :] = acc[32 * s : 32 * s + 32, 128 * c : 128 * c + 128].astype(BF16)
        else:
            grad_ref[...] = acc[...].astype(BF16)


def window_block(width):
    return pl.BlockSpec((1, WIN_ROWS, width), lambda w: (w, 0, 0))


def window_shape(width, dtype):
    return jax.ShapeDtypeStruct((WINDOWS, WIN_ROWS, width), dtype)


def weight_block(layer, rows, columns):
    return pl.BlockSpec((1, rows, columns), lambda w: (layer, 0, 0), pipeline_mode=pl.Buffered(1))


def whole_block(*shape):
    return pl.BlockSpec(shape, lambda w: (0,) * len(shape))


DENSE_PARAMS = pltpu.CompilerParams(vmem_limit_bytes=VMEM_LIMIT)
ROW = whole_block(LAYERS, D)


def project_in(layer, x, gain, shift, weight, q_bias, v_bias):
    return pl.pallas_call(
        partial(project_in_kernel, layer),
        grid=(WINDOWS,),
        in_specs=[window_block(D), ROW, ROW, weight_block(layer, D, 3 * D), ROW, ROW],
        out_specs=[window_block(D), window_block(3 * D)],
        out_shape=[window_shape(D, BF16), window_shape(3 * D, BF16)],
        compiler_params=DENSE_PARAMS,
        cost_estimate=busy(8),
        name="project_in",
    )(x, gain, shift, weight, q_bias, v_bias)


def feed_forward(layer, x, mixed, wp, wu, wd, bp, gain, shift, bu, bd, out_dtype):
    return pl.pallas_call(
        partial(feed_forward_kernel, layer),
        grid=(WINDOWS,),
        in_specs=[window_block(D), window_block(D), weight_block(layer, D, D), weight_block(layer, D, FF),
                  weight_block(layer, FF, D), ROW, ROW, ROW, whole_block(LAYERS, FF), ROW],
        out_specs=[window_block(D), window_block(D), window_block(FF), window_block(FF), window_block(D)],
        out_shape=[window_shape(D, F32), window_shape(D, BF16), window_shape(FF, BF16), window_shape(FF, BF16),
                   window_shape(D, out_dtype)],
        compiler_params=DENSE_PARAMS,
        cost_estimate=busy(28),
        name="feed_forward",
    )(x, mixed, wp, wu, wd, bp, gain, shift, bu, bd)


def feed_backward(layer, shards, dz, x1, normed, mixed, act, slope, wp, wu, wd, gain):
    if shards == 16:
        grad_shapes = [(16, 1152, 128)]
    else:
        grad_shapes = [(D, FF), (D, FF), (D, D)]
    return pl.pallas_call(
        partial(feed_backward_kernel, layer, shards),
        grid=(WINDOWS,),
        in_specs=[window_block(D), window_block(D), window_block(D), window_block(D), window_block(FF), window_block(FF),
                  weight_block(layer, D, D), weight_block(layer, D, FF), weight_block(layer, FF, D), ROW],
        out_specs=[window_block(D), window_block(D), whole_block(8, FF)] + [whole_block(*shape) for shape in grad_shapes],
        out_shape=[window_shape(D, F32), window_shape(D, BF16), jax.ShapeDtypeStruct((8, FF), F32)]
        + [jax.ShapeDtypeStruct(shape, BF16) for shape in grad_shapes],
        scratch_shapes=[pltpu.VMEM((WIN_ROWS, FF), BF16), pltpu.VMEM((D, FF), F32), pltpu.VMEM((D, FF), F32), pltpu.VMEM((D, D), F32)],
        compiler_params=DENSE_PARAMS,
        cost_estimate=busy(28),
        name="feed_backward",
    )(dz, x1, normed, mixed, act, slope, wp, wu, wd, gain)


def project_back(layer, shards, dq, dk, dv, normed, x, dx1, weight, gain, out_dtype):
    grad_shape = (16, 384, 128) if shards == 16 else (D, 3 * D)
    return pl.pallas_call(
        partial(project_back_kernel, layer, shards),
        grid=(WINDOWS,),
        in_specs=[window_block(D)] * 6 + [weight_block(layer, D, 3 * D), ROW],
        out_specs=[window_block(D), whole_block(8, FF), whole_block(*grad_shape)],
        out_shape=[window_shape(D, out_dtype), jax.ShapeDtypeStruct((8, FF), F32), jax.ShapeDtypeStruct(grad_shape, BF16)],
        scratch_shapes=[pltpu.VMEM((D, 3 * D), F32)],
        compiler_params=DENSE_PARAMS,
        cost_estimate=busy(13),
        name="project_back",
    )(dq, dk, dv, normed, x, dx1, weight, gain)


def passed_along(value, axis, steps):
    count = lax.axis_size(axis)
    pairs = [(source, (source + steps) % count) for source in range(count)]
    return lax.ppermute(value, axis, pairs)


def to_windows(field):
    channels = field.shape[-1]
    return field.reshape(2, WIN_S, 2, WIN_S, WIN_T, channels).transpose(0, 2, 1, 3, 4, 5).reshape(WINDOWS, WIN_ROWS, channels)


def from_windows(windows):
    channels = windows.shape[-1]
    return windows.reshape(2, 2, WIN_S, WIN_S, WIN_T, channels).transpose(0, 2, 1, 3, 4, 5).reshape(SIDE, SIDE, WIN_T, channels)


def shift_in(field):
    ahead = passed_along(field[:, :, :SHIFT_T], "tm", -1)
    moved = jnp.concatenate([field[:, :, SHIFT_T:], ahead], axis=2)
    return to_windows(jnp.roll(moved, (-SHIFT_S, -SHIFT_S), axis=(0, 1)))


def shift_out(windows):
    moved = jnp.roll(from_windows(windows), (SHIFT_S, SHIFT_S), axis=(0, 1))
    behind = passed_along(moved[:, :, SHIFT_T:], "tm", 1)
    return jnp.concatenate([behind, moved[:, :, :SHIFT_T]], axis=2)


def layer_forward(layer, current, weights, place, aug, out_dtype):
    (gain_one, shift_one, weight_qkv, bias_query, bias_value, table_rows, weight_proj, bias_proj,
     gain_two, shift_two, weight_up, bias_up, weight_down, bias_down) = weights
    table = spread_table(table_rows[layer])
    normed_one, qkv = project_in(layer, current, gain_one, shift_one, weight_qkv, bias_query, bias_value)
    mixed, inverse, exps = attention_forward(qkv, table, place, aug)
    attended, normed_two, act, slope, result = feed_forward(
        layer, current, mixed, weight_proj, weight_up, weight_down, bias_proj, gain_two, shift_two, bias_up, bias_down, out_dtype
    )
    return result, (current, normed_one, qkv, mixed, inverse, exps, attended, normed_two, act, slope)


def over_groups(value):
    count = lax.axis_size("dp")
    if count != 2:
        return lax.psum(value, "dp")
    return value.astype(F32) + passed_along(value, "dp", 1).astype(F32)


def scattered(grad):
    shard = lax.psum_scatter(grad, "tm", scatter_dimension=0, tiled=True)
    return over_groups(shard.reshape(shard.shape[-2:])).astype(F32)


def halved(grad):
    count = lax.axis_size("tm")
    index = lax.axis_index("tm")
    kept = grad.reshape((count, -1) + grad.shape[-1:])
    reach = 1
    while reach < count:
        pairs = kept.reshape((kept.shape[0] // 2, 2) + kept.shape[1:])
        bit = index // reach % 2
        mine = lax.dynamic_index_in_dim(pairs, bit, 1, keepdims=False)
        sent = lax.dynamic_index_in_dim(pairs, 1 - bit, 1, keepdims=False).astype(BF16)
        swap = [(source, source ^ reach) for source in range(count)]
        kept = mine.astype(F32) + lax.ppermute(sent, "tm", swap).astype(F32)
        reach = 2 * reach
    return over_groups(kept[0].astype(BF16))


def unpack(packed, start, columns):
    rows = columns // 128 * 32
    return packed[start : start + rows].reshape(columns // 128, 32, 128).transpose(1, 0, 2).reshape(32, columns)


def layer_backward(layer, upstream, saved, weights, place, aug, out_dtype, after):
    (gain_one, shift_one, weight_qkv, bias_query, bias_value, table_rows, weight_proj, bias_proj,
     gain_two, shift_two, weight_up, bias_up, weight_down, bias_down) = weights
    (current, normed_one, qkv, mixed, inverse, exps, attended, normed_two, act, slope) = saved
    shards = lax.axis_size("tm")
    grad_attended, grad_mixed, sums_two, *feed_grads = feed_backward(
        layer, shards, upstream, attended, normed_two, mixed, act, slope, weight_proj, weight_up, weight_down, gain_two
    )
    if shards == 16:
        feed_sums = (scattered(feed_grads[0]),)
    else:
        feed_sums = (scattered(feed_grads[0]), scattered(feed_grads[1].T), scattered(feed_grads[2]))
    dq, dk, dv, spread = attention_backward(qkv, grad_mixed, inverse, exps, place)
    if after is not None:
        dq, after = lax.optimization_barrier((dq, after))
    result, sums_one, grad_qkv = project_back(
        layer, shards, dq, dk, dv, normed_one, current, grad_attended, weight_qkv, gain_one, out_dtype
    )
    grad_qkv = halved(grad_qkv)
    small = jnp.concatenate([sums_two[:2].reshape(-1), sums_one[:1].reshape(-1), gather_table(spread).reshape(-1)])
    if after is not None:
        small, feed_sums = lax.optimization_barrier((small, feed_sums))
    return result, (feed_sums, grad_qkv, lax.psum(small, ("dp", "tm"))), after


def layer_totals(sums):
    feed_sums, grad_qkv, small = sums
    if len(feed_sums) == 1:
        packed = feed_sums[0]
        grad_up = unpack(packed, 0, FF)
        grad_down = packed[512:1024].T
        grad_proj = unpack(packed, 1024, D)
        grad_qkv = unpack(grad_qkv, 0, 3 * D)
    else:
        grad_up, grad_down, grad_proj = feed_sums
    rest = small[FF : 3 * FF].reshape(8, D)
    return (
        rest[6], rest[7], grad_qkv, rest[4], rest[5], small[3 * FF :].reshape(TABLE_ROWS, HEADS), grad_proj, rest[1],
        rest[2], rest[3], grad_up, small[:FF], grad_down, rest[0],
    )


def body(inputs, clip_ids, *rest):
    weights, cotangent = rest[:-1], rest[-1]
    frames = inputs.shape[1]
    place = place_codes()
    aug = mask_operands(clip_ids[0], frames)
    upstream = shift_in(cotangent[0].transpose(1, 2, 0, 3))
    current = to_windows(inputs[0].transpose(1, 2, 0, 3))
    current, saved_first = layer_forward(0, current, weights, place, None, F32)
    current = shift_in(from_windows(current))
    current, saved_second = layer_forward(1, current, weights, place, aug, BF16)
    block_output = shift_out(current).transpose(2, 0, 1, 3)
    upstream, (feed_second, qkv_second, small_second), _ = layer_backward(
        1, upstream, saved_second, weights, place, aug, F32, None
    )
    upstream = to_windows(shift_out(upstream))
    upstream, feed_second = lax.optimization_barrier((upstream, feed_second))
    upstream, first, (qkv_second, small_second) = layer_backward(
        0, upstream, saved_first, weights, place, None, BF16, (qkv_second, small_second)
    )
    totals_first = layer_totals(first)
    totals_second = layer_totals((feed_second, qkv_second, small_second))
    input_grad = from_windows(upstream).transpose(2, 0, 1, 3)
    results = [jnp.stack(pair) for pair in zip(totals_first, totals_second)]
    return (block_output.reshape(inputs.shape), input_grad.reshape(inputs.shape)) + tuple(results)


def solution(mesh):
    tokens = P("dp", "tm", None, None, None)
    split = P(None, "tm", None)
    placed = (tokens, P("dp", None)) + (P(),) * 14 + (tokens,)
    outs = (tokens, tokens, P(), P(), split, P(), P(), P(), split, P(), P(), P(), split, P(), split, P())
    return jax.shard_map(body, mesh=mesh, in_specs=placed, out_specs=outs, check_vma=False)
```

time: 975 us -> 713 us (0.73)
  matrix products: 194 us -> 0 us
  blocking collectives: 166 us -> 0 us
  Pallas kernels: 202 us -> 320 us
  waiting for transfers between devices: 176 us -> 223 us
  other arithmetic: 77.7 us -> 35.4 us
  local copies, waits for them, and re-layouts: 124 us -> 87.4 us
  starting transfers between devices: 6.76 us -> 18.1 us
    dot_general x32 -> x0, matrix products: 194 us -> none  [the longest x8 93.6 us: dot_nn(): lax.dot_general(a, b, (((1,), (0,)), ((), ())), preferred_element_type=F32)]
    unnamed x1 -> x0, blocking collectives: 166 us -> none
    pallas_call x2 -> x10, Pallas kernels: 98.4 us -> 257 us  [the longest x2 105 us: attention_backward(): pl.pallas_call(backward_kernel, grid=(GROUPS, WINDOWS), in_specs=[head_bl...]
    ppermute x0 -> x8, waiting for transfers between devices: none -> 42.7 us  [halved(): kept = mine.astype(F32) + lax.ppermute(sent, 'tm', swap).astype(F32)]
    pallas_call x2, Pallas kernels: 104 us -> 62.3 us  [attention_forward(): pl.pallas_call(partial(forward_kernel, masked), grid=(GROUPS, WINDOWS), i...]
    psum x2, waiting for transfers between devices: 144 us -> 168 us  [layer_backward(): return (result, (feed_sums, grad_qkv, lax.psum(small, ('dp', 'tm'))), after)]
    ppermute x4 -> x8, waiting for transfers between devices: 31.7 us -> 12 us  [passed_along(): return lax.ppermute(value, axis, pairs)]
    convert_element_type x12 -> x2, other arithmetic: 19.2 us -> 0.94 us  [halved(): return over_groups(kept[0].astype(BF16))]
  transfers between devices with their start and end apart: 9 -> 20, of which waited for: 5 -> 11; matrix products, arithmetic and copies ran while one was open for 18% -> 13% of each run, Pallas kernels for 5% -> 23%
where the time goes in v2:
time: 713 us; the launch traced here: 702 us
  Pallas kernels  320 us (45%)
  waiting for transfers between devices  223 us (31%)
  local copies, waits for them, and re-layouts  87.4 us (12%)
  other arithmetic  35.4 us (5%)
  between operations  18.3 us (3%)
  starting transfers between devices  18.1 us (3%)
    psum x2, waiting for transfers between devices, layer_backward(): return (result, (feed_sums, grad_qkv, lax.psum(small, ('dp', 'tm'))), after)  168 us
    pallas_call x2, Pallas kernels, attention_backward(): pl.pallas_call(backward_kernel, grid=(GROUPS, WINDOWS), in_specs=[head_bl...  105 us
    pallas_call x2, Pallas kernels, attention_forward(): pl.pallas_call(partial(forward_kernel, masked), grid=(GROUPS, WINDOWS), i...  62.3 us
    pallas_call x2, Pallas kernels, feed_backward(): pl.pallas_call(partial(feed_backward_kernel, layer, shards), grid=(WINDOW...  56.9 us
    pallas_call x2, Pallas kernels, feed_forward(): pl.pallas_call(partial(feed_forward_kernel, layer), grid=(WINDOWS,), in_s...  55.1 us
    ppermute x8, waiting for transfers between devices, halved(): kept = mine.astype(F32) + lax.ppermute(sent, 'tm', swap).astype(F32)  42.7 us
    pallas_call x2, Pallas kernels, project_back(): pl.pallas_call(partial(project_back_kernel, layer, shards), grid=(WINDOWS...  25.2 us
    unnamed x61, local copies, waits for them, and re-layouts  20.4 us
  transfers between devices with their start and end apart: 20, of which 11 were waited for; matrix products, arithmetic and copies ran while one was open for 13% of the time, Pallas kernels for 23%

profile of v2, /device:TPU:0, one launch (start us, length us, event | category | flops | bytes accessed | tf_op | source)
XLA Modules:
  0.0 702.0 jit_solution(15039246162338113556)
XLA Ops:
  8.1 2.7 copy.169
  11.5 3.4 copy.170
  14.9 1.8 copy.171
  17.9 2.1 fusion.refs_4_.place_ref
  20.0 7.2 %project_in.2 = (bf16[4,392,512]{2,1,0:T(8,128)(2,1)}, bf16[4,392,1536]{2,1,0:T(8,128)(2,1)}) custom-call(bf16[4,392,512]{2,1,0:T(8,128)(2,1)} %bitcast.300, bf16[2,512]{1,0:T(2,128)(2,1)} %gain_ref.15, bf16[2,512]{1,0:T(2,128)(2,1)} %shift_ref.6, bf16[2,512,1536]{2,1,0:T(8,128)(2,1)} %w_ref.7, bf16[2,512]{1,0:T(2,128)(2,1)} %qb_ref.3, bf16[2,512]{1,0:T(2,128)(2,1)} %vb_ref.3), custom_call_target="tpu_custom_call" | custom-call | flops 8000000000 | bytes 8000000 | tf_op jit(solution)/shard_map/project_in/pallas_call | solution.py:458
  27.2 30.8 %attention_forward.2 = (bf16[4,392,512]{2,1,0:T(8,128)(2,1)}, f32[16,8,1664]{2,1,0:T(8,128)}, bf16[16,392,1664]{2,1,0:T(8,128)(2,1)}) custom-call(bf16[4,392,1536]{2,1,0:T(8,128)(2,1)} %get-tuple-element.65.refs_0_.refs_1_.refs_2_.q_ref.k_ref.v_ref, bf16[4,392,1536]{2,1,0:T(8,128)(2,1)} %get-tuple-element.65.refs_0_.refs_1_.refs_2_.q_ref.k_ref.v_ref, ...), custom_call_target="tpu_custom_call" | custom-call | flops 31000000512 | bytes 31000000 | tf_op jit(solution)/shard_map/attention_forward/pallas_call | solution.py:193
  58.0 27.2 %feed_forward.2 = (f32[4,392,512]{2,1,0:T(8,128)}, bf16[4,392,512]{2,1,0:T(8,128)(2,1)}, bf16[4,392,2048]{2,1,0:T(8,128)(2,1)}, bf16[4,392,2048]{2,1,0:T(8,128)(2,1)}, f32[4,392,512]{2,1,0:T(8,128)}) custom-call(bf16[4,392,512]{2,1,0:T(8,128)(2,1)} %bitcast.301, bf16[4,392,512]{2,1,0:T(8,128)(2,1)} %get-tuple-element.66.o_ref, bf16[2,512,512]{2,1,0:T(8,128)(2,1)} %wp_ref.7, ...), custom_call_target="tpu_custom_call" | custom-call | flops 28000000000 | bytes 28000000 | tf_op jit(solution)/shard_map/feed_forward/pallas_call | solution.py:471
  85.2 2.2 copy.172
  87.5 1.9 fusion.62
  89.4 5.6 collective-permute-start
  95.0 1.7 fusion.63
  103.1 4.9 copy.174
  108.0 3.7 copy.175
  118.3 4.0 collective-permute-done.2
  122.2 1.9 fusion.8
  129.2 2.0 copy.173
  131.3 7.7 %project_in.3 = (bf16[4,392,512]{2,1,0:T(8,128)(2,1)}, bf16[4,392,1536]{2,1,0:T(8,128)(2,1)}) custom-call(f32[4,392,512]{2,1,0:T(8,128)} %bitcast.288, bf16[2,512]{1,0:T(2,128)(2,1)} %gain_ref.15, bf16[2,512]{1,0:T(2,128)(2,1)} %shift_ref.6, bf16[2,512,1536]{2,1,0:T(8,128)(2,1)} %w_ref.7, bf16[2,512]{1,0:T(2,128)(2,1)} %qb_ref.3, bf16[2,512]{1,0:T(2,128)(2,1)} %vb_ref.3), custom_call_target="tpu_custom_call" | custom-call | flops 8000000000 | bytes 8000000 | tf_op jit(solution)/shard_map/project_in/pallas_call | solution.py:458
  139.0 31.5 %attention_forward.3 = (bf16[4,392,512]{2,1,0:T(8,128)(2,1)}, f32[16,8,1664]{2,1,0:T(8,128)}, bf16[16,392,1664]{2,1,0:T(8,128)(2,1)}) custom-call(bf16[4,392,1536]{2,1,0:T(8,128)(2,1)} %get-tuple-element.68.refs_0_.refs_1_.refs_2_.q_ref.k_ref.v_ref, bf16[4,392,1536]{2,1,0:T(8,128)(2,1)} %get-tuple-element.68.refs_0_.refs_1_.refs_2_.q_ref.k_ref.v_ref, ...), custom_call_target="tpu_custom_call" | custom-call | flops 31000000512 | bytes 31000000 | tf_op jit(solution)/shard_map/attention_forward/pallas_call | solution.py:193
  170.5 27.9 %feed_forward.3 = (f32[4,392,512]{2,1,0:T(8,128)}, bf16[4,392,512]{2,1,0:T(8,128)(2,1)}, bf16[4,392,2048]{2,1,0:T(8,128)(2,1)}, bf16[4,392,2048]{2,1,0:T(8,128)(2,1)}, bf16[4,392,512]{2,1,0:T(8,128)(2,1)}) custom-call(f32[4,392,512]{2,1,0:T(8,128)} %bitcast.289, bf16[4,392,512]{2,1,0:T(8,128)(2,1)} %get-tuple-element.69.o_ref, bf16[2,512,512]{2,1,0:T(8,128)(2,1)} %wp_ref.7, ...), custom_call_target="tpu_custom_call" | custom-call | flops 28000000000 | bytes 28000000 | tf_op jit(solution)/shard_map/feed_forward/pallas_call | solution.py:471
  198.4 28.4 %feed_backward.2 = (f32[4,392,512]{2,1,0:T(8,128)}, bf16[4,392,512]{2,1,0:T(8,128)(2,1)}, f32[8,2048]{1,0:T(8,128)}, bf16[16,1152,128]{2,1,0:T(8,128)(2,1)}) custom-call(bf16[4,392,512]{2,1,0:T(8,128)(2,1)} %bitcast.306, f32[4,392,512]{2,1,0:T(8,128)} %get-tuple-element.71.x1_ref, bf16[4,392,512]{2,1,0:T(8,128)(2,1)} %get-tuple-element.72.n_ref, ...), custom_call_target="tpu_custom_call" | custom-call | flops 28000000000 | bytes 28000000 | tf_op jit(solution)/shard_map/feed_backward/pallas_call | solution.py:490
  226.8 52.5 %attention_backward.2 = (bf16[4,392,512]{2,1,0:T(8,128)(2,1)}, bf16[4,392,512]{2,1,0:T(8,128)(2,1)}, bf16[4,392,512]{2,1,0:T(8,128)(2,1)}, f32[4,4,8,1536]{3,2,1,0:T(8,128)}) custom-call(bf16[4,392,1536]{2,1,0:T(8,128)(2,1)} %get-tuple-element.68.refs_0_.refs_1_.refs_2_.q_ref.k_ref.v_ref, ...), custom_call_target="tpu_custom_call" | custom-call | flops 51999997952 | bytes 52000000 | tf_op jit(solution)/shard_map/attention_backward/pallas_call | solution.py:216
  279.3 12.8 %project_back.2 = (f32[4,392,512]{2,1,0:T(8,128)}, f32[8,2048]{1,0:T(8,128)}, bf16[16,384,128]{2,1,0:T(8,128)(2,1)}) custom-call(bf16[4,392,512]{2,1,0:T(8,128)(2,1)} %get-tuple-element.78.dq_ref, bf16[4,392,512]{2,1,0:T(8,128)(2,1)} %get-tuple-element.79.dk_ref, bf16[4,392,512]{2,1,0:T(8,128)(2,1)} %get-tuple-element.80.dv_ref, ...), custom_call_target="tpu_custom_call" | custom-call | flops 12999999488 | bytes 13000000 | tf_op jit(solution)/shard_map/project_back/pallas_call | solution.py:507
  294.1 1.8 copy-done.1
  296.8 1.7 fusion.64
  302.0 1.9 fusion.61
  305.1 4.8 copy.201
  309.9 2.9 slice_bitcast_fusion.15
  312.8 26.1 %collective-permute-done.6 = bf16[4,384,128]{2,1,0:T(8,128)(2,1)} collective-permute-done((bf16[4,384,128]{2,1,0:T(8,128)(2,1)}, bf16[4,384,128]{2,1,0:T(8,128)(2,1)}, u32[]{:S(2)}, u32[]{:S(2)}) %collective-permute-start.6) | collective-permute-done | bytes 393248 | tf_op jit(solution)/shard_map/ppermute | solution.py:583
  341.5 5.4 collective-permute-done.7
  352.9 1.9 collective-permute-done.8
  358.7 1.9 collective-permute-done.9
  361.3 2.1 pad_maximum_fusion.5
  363.3 2.0 copy.181
  365.3 1.7 collective-permute-done.4
  367.1 28.5 %feed_backward.3 = (f32[4,392,512]{2,1,0:T(8,128)}, bf16[4,392,512]{2,1,0:T(8,128)(2,1)}, f32[8,2048]{1,0:T(8,128)}, bf16[16,1152,128]{2,1,0:T(8,128)(2,1)}) custom-call(f32[4,392,512]{2,1,0:T(8,128)} %bitcast.291, f32[4,392,512]{2,1,0:T(8,128)} %get-tuple-element.86.x1_ref, bf16[4,392,512]{2,1,0:T(8,128)(2,1)} %get-tuple-element.87.n_ref, ...), custom_call_target="tpu_custom_call" | custom-call | flops 28000000000 | bytes 28000000 | tf_op jit(solution)/shard_map/feed_backward/pallas_call | solution.py:490
  395.7 52.7 %attention_backward.3 = (bf16[4,392,512]{2,1,0:T(8,128)(2,1)}, bf16[4,392,512]{2,1,0:T(8,128)(2,1)}, bf16[4,392,512]{2,1,0:T(8,128)(2,1)}, f32[4,4,8,1536]{3,2,1,0:T(8,128)}) custom-call(bf16[4,392,1536]{2,1,0:T(8,128)(2,1)} %get-tuple-element.65.refs_0_.refs_1_.refs_2_.q_ref.k_ref.v_ref, ...), custom_call_target="tpu_custom_call" | custom-call | flops 51999997952 | bytes 52000000 | tf_op jit(solution)/shard_map/attention_backward/pallas_call | solution.py:216
  448.4 47.0 %all-reduce.23.cloned.1.call-done = f32[46704]{0:T(1024)} async-done(((f32[46704]{0:T(1024)}), f32[46704]{0:T(1024)}) %all-reduce.23.cloned.1.call-update) | async-done | bytes 186832 | tf_op jit(solution)/shard_map/psum | solution.py:615
  495.4 12.5 %project_back.3 = (bf16[4,392,512]{2,1,0:T(8,128)(2,1)}, f32[8,2048]{1,0:T(8,128)}, bf16[16,384,128]{2,1,0:T(8,128)(2,1)}) custom-call(bf16[4,392,512]{2,1,0:T(8,128)(2,1)} %get-tuple-element.98.dq_ref, bf16[4,392,512]{2,1,0:T(8,128)(2,1)} %get-tuple-element.99.dk_ref, bf16[4,392,512]{2,1,0:T(8,128)(2,1)} %get-tuple-element.100.dv_ref, ...), custom_call_target="tpu_custom_call" | custom-call | flops 12999999488 | bytes 13000000 | tf_op jit(solution)/shard_map/project_back/pallas_call | solution.py:507
  509.3 3.2 maximum_bitcast_fusion
  512.5 4.0 copy.202
  520.4 2.9 slice_bitcast_fusion.7
  525.9 1.8 reshape.533
  532.9 3.4 collective-permute-start.13
  537.0 4.7 collective-permute-done.13
  542.7 1.8 collective-permute-start.14
  545.3 4.8 collective-permute-done.14
  556.8 4.5 collective-permute-done.10
  564.9 121.3 %all-reduce.25.cloned.1.call-done = f32[46704]{0:T(1024)} async-done(((f32[46704]{0:T(1024)}), f32[46704]{0:T(1024)}) %all-reduce.25.cloned.1.call-update) | async-done | bytes 186832 | tf_op jit(solution)/shard_map/psum | solution.py:615
  (216 shorter events, 72.6 us)
Async XLA Ops:
  8.0 350.1 %reduce-scatter.3.cloned.1.call-start = ((), (), s32[]{:S(2)}) async-start(), calls=%async_computation.2 | async-start | bytes 5013504 | tf_op jit(solution)/shard_map/reduce_scatter | solution.py:568
  8.1 2.8 copy-start.17
  87.5 7.5 %copy-start.4 = (bf16[1,8,14,14,512]{4,1,3,2,0:T(8,128)(2,1)S(1)}, bf16[1,8,14,14,512]{4,1,3,2,0:T(8,128)(2,1)}, u32[]{:S(2)}) copy-start(bf16[1,8,14,14,512]{4,1,3,2,0:T(8,128)(2,1)} %param.33) | copy-start | bytes 4816900
  89.4 38.2 %collective-permute-start = (f32[14,14,4,512]{3,2,1,0:T(4,128)}, f32[14,14,4,512]{3,2,1,0:T(4,128)S(1)}, u32[]{:S(2)}, u32[]{:S(2)}) collective-permute-start(f32[14,14,4,512]{3,2,1,0:T(4,128)} %get-tuple-element.228), channel_id=1, source_target_pairs={{0,15},{1,0},{2,1},{3,2},{4,3},{5,4},{6,5},{7,6},{8,7},{9,8},{10,9... | collective-permute-start | bytes 4816904 | tf_op jit(solution)/shard_map/ppermute | solution.py:523
  95.0 7.3 %copy-start.19 = (s32[1,128]{1,0:T(1,128)S(1)}, s32[1,128]{1,0:T(1,128)}, u32[]{:S(2)}) copy-start(s32[1,128]{1,0:T(1,128)} %param.18) | copy-start | bytes 1540
  96.7 25.5 %collective-permute-start.2 = (bf16[14,14,4,512]{3,2,1,0:T(4,128)(2,1)}, bf16[14,14,4,512]{3,2,1,0:T(4,128)(2,1)}, u32[]{:S(2)}, u32[]{:S(2)}) collective-permute-start(bf16[14,14,4,512]{3,2,1,0:T(4,128)(2,1)} %get-tuple-element.230), channel_id=1, source_target_pairs={{0,15},{1,0},{2,1},{3,2},{4,3},{5,4},{6,5},{7,6},{8,7},{9,8},{10,9... | collective-permute-start | bytes 2408456 | tf_op jit(solution)/shard_map/ppermute | solution.py:523
  118.3 5.8 copy-start
  226.8 268.6 %all-reduce.23.cloned.1.call-start = ((), (), s32[]{:S(2)}) async-start(), calls=%async_computation.3 | async-start | bytes 376832 | tf_op jit(solution)/shard_map/psum | solution.py:615
  292.1 1.7 copy-start.5
  293.4 5.6 collective-permute-start.5
  293.9 1.9 copy-start.1
  298.4 1.4 copy-start.7
  298.4 210.8 %collective-permute-start.1 = (bf16[14,14,4,512]{3,2,1,0:T(4,128)(2,1)}, bf16[14,14,4,512]{3,2,1,0:T(4,128)(2,1)}, u32[]{:S(2)}, u32[]{:S(2)}) collective-permute-start(bf16[14,14,4,512]{3,2,1,0:T(4,128)(2,1)} %get-tuple-element.232), channel_id=1, source_target_pairs={{0,1},{1,2},{2,3},{3,4},{4,5},{5,6},{6,7},{7,8},{8,9},{9,10},{10,1... | collective-permute-start | bytes 2408456 | tf_op jit(solution)/shard_map/ppermute | solution.py:523
  302.0 2.1 copy-start.11
  302.0 36.9 %collective-permute-start.6 = (bf16[4,384,128]{2,1,0:T(8,128)(2,1)}, bf16[4,384,128]{2,1,0:T(8,128)(2,1)}, u32[]{:S(2)}, u32[]{:S(2)}) collective-permute-start(bf16[4,384,128]{2,1,0:T(8,128)(2,1)} %fusion.9), channel_id=1, source_target_pairs={{0,2},{1,3},{2,0},{3,1},{4,6},{5,7},{6,4},{7,5},{8,10},{9,11},{10,... | collective-permute-start | bytes 1179656 | tf_op jit(solution)/shard_map/ppermute | solution.py:583
  303.9 57.4 %collective-permute-start.3 = (f32[14,14,4,512]{3,2,1,0:T(4,128)}, f32[14,14,4,512]{3,2,1,0:T(4,128)}, u32[]{:S(2)}, u32[]{:S(2)}) collective-permute-start(f32[14,14,4,512]{3,2,1,0:T(4,128)} %get-tuple-element.226), channel_id=1, source_target_pairs={{0,1},{1,2},{2,3},{3,4},{4,5},{5,6},{6,7},{7,8},{8,9},{9,10},{10,1... | collective-permute-start | bytes 4816904 | tf_op jit(solution)/shard_map/ppermute | solution.py:523
  340.0 6.9 collective-permute-start.7
  347.6 7.2 %collective-permute-start.8 = (bf16[1,384,128]{2,1,0:T(8,128)(2,1)}, bf16[1,384,128]{2,1,0:T(8,128)(2,1)}, u32[]{:S(2)}, u32[]{:S(2)}) collective-permute-start(bf16[1,384,128]{2,1,0:T(8,128)(2,1)} %dynamic-slice_convert_fusion.5), channel_id=1, source_target_pairs={{0,8},{1,9},{2,10},{3,11},{4,12},{5,13},{6,14},{7,15},{8,0},{9,1},... | collective-permute-start | bytes 294920 | tf_op jit(solution)/shard_map/ppermute | solution.py:583
  350.2 2.8 copy-start.18
  355.7 4.9 collective-permute-start.9
  358.0 196.3 %reduce-scatter.5.cloned.1.call-start = ((), (), s32[]{:S(2)}) async-start(), calls=%async_computation.4 | async-start | bytes 5013504 | tf_op jit(solution)/shard_map/reduce_scatter | solution.py:568
  358.1 8.9 %collective-permute-start.4 = (bf16[1152,128]{1,0:T(8,128)(2,1)}, bf16[1152,128]{1,0:T(8,128)(2,1)S(1)}, u32[]{:S(2)}, u32[]{:S(2)}) collective-permute-start(bf16[1152,128]{1,0:T(8,128)(2,1)} %bitcast.323), channel_id=1, source_target_pairs={{0,16},{16,0},{1,17},{17,1},{2,18},{18,2},{3,19},{19,3},{4,20},{20... | collective-permute-start | bytes 884744 | tf_op jit(solution)/shard_map/ppermute | solution.py:523
  363.3 3.7 copy-start.14
  367.1 184.4 %copy-start.3 = (f32[1152,128]{1,0:T(8,128)}, f32[1152,128]{1,0:T(8,128)S(1)}, u32[]{:S(2)}) copy-start(f32[1152,128]{1,0:T(8,128)S(1)} %convert_add_fusion.3) | copy-start | bytes 1769476
  395.6 290.5 %all-reduce.25.cloned.1.call-start = ((), (), s32[]{:S(2)}) async-start(), calls=%async_computation.5 | async-start | bytes 376832 | tf_op jit(solution)/shard_map/psum | solution.py:615
  507.9 1.4 copy-start.2
  509.2 7.4 %collective-permute-start.11 = (bf16[8,384,128]{2,1,0:T(8,128)(2,1)S(1)}, bf16[8,384,128]{2,1,0:T(8,128)(2,1)}, u32[]{:S(2)}, u32[]{:S(2)}) collective-permute-start(bf16[8,384,128]{2,1,0:T(8,128)(2,1)S(1)} %dynamic-slice_bitcast_fusion), channel_id=1, source_target_pairs={{0,1},{1,0},{2,3},{3,2},{4,5},{5,4},{6,7},{7,6},{8,9},{9,8},{10,11... | collective-permute-start | bytes 2359304 | tf_op jit(solution)/shard_map/ppermute | solution.py:583
  509.3 3.2 copy-start.12
  519.0 12.8 %collective-permute-start.12 = (bf16[4,384,128]{2,1,0:T(8,128)(2,1)}, bf16[4,384,128]{2,1,0:T(8,128)(2,1)}, u32[]{:S(2)}, u32[]{:S(2)}) collective-permute-start(bf16[4,384,128]{2,1,0:T(8,128)(2,1)} %fusion.10), channel_id=1, source_target_pairs={{0,2},{1,3},{2,0},{3,1},{4,6},{5,7},{6,4},{7,5},{8,10},{9,11},{10,... | collective-permute-start | bytes 1179656 | tf_op jit(solution)/shard_map/ppermute | solution.py:583
  530.0 6.3 copy-start.13
  532.9 8.8 %collective-permute-start.13 = (bf16[2,384,128]{2,1,0:T(8,128)(2,1)S(1)}, bf16[2,384,128]{2,1,0:T(8,128)(2,1)}, u32[]{:S(2)}, u32[]{:S(2)}) collective-permute-start(bf16[2,384,128]{2,1,0:T(8,128)(2,1)S(1)} %fusion.12), channel_id=1, source_target_pairs={{0,4},{1,5},{2,6},{3,7},{4,0},{5,1},{6,2},{7,3},{8,12},{9,13},{10,... | collective-permute-start | bytes 589832 | tf_op jit(solution)/shard_map/ppermute | solution.py:583
  537.0 14.5 %copy-start.6 = (bf16[4,392,512]{2,1,0:T(8,128)(2,1)S(1)}, bf16[4,392,512]{2,1,0:T(8,128)(2,1)}, u32[]{:S(2)}) copy-start(bf16[4,392,512]{2,1,0:T(8,128)(2,1)} %get-tuple-element.103) | copy-start | bytes 4816900
  542.7 7.4 %collective-permute-start.14 = (bf16[1,384,128]{2,1,0:T(8,128)(2,1)S(1)}, bf16[1,384,128]{2,1,0:T(8,128)(2,1)S(1)}, u32[]{:S(2)}, u32[]{:S(2)}) collective-permute-start(bf16[1,384,128]{2,1,0:T(8,128)(2,1)S(1)} %dynamic-slice_convert_fusion.4), channel_id=1, source_target_pairs={{0,8},{1,9},{2,10},{3,11},{4,12},{5,13},{6,14},{7,15},{8,0},{9,1},... | collective-permute-start | bytes 294920 | tf_op jit(solution)/shard_map/ppermute | solution.py:583
  550.1 5.7 collective-permute-start.15
  551.5 1.4 copy-start.10
  551.5 1.6 slice-start.1
  553.0 0.8 slice-start
  553.1 1.0 copy-start.8
  554.3 7.0 copy-start.15
  554.3 7.0 collective-permute-start.10
  561.4 1.0 copy-start.9
  686.1 1.8 copy-start.16
  687.1 5.7 slice-start.2
  687.1 5.7 slice-start.3
Sparse Core Ops, SparseCore 0:
  226.9 76.9 reduce-scatter.2
  395.8 72.9 reduce-scatter.4
Sparse Core Ops, SparseCore 1:
  358.1 137.2 all-reduce.22
  561.6 124.5 all-reduce.24

commit v3 on v2

--- a/solution.py
+++ b/solution.py
@@ -7,6 +7,7 @@
 from jax.experimental import pallas as pl
 from jax.experimental.pallas import tpu as pltpu
 from jax.sharding import PartitionSpec as P
+
 
 D = 512
 HEADS = 16
@@ -36,26 +37,18 @@
 BF16 = jnp.bfloat16
 CHUNKS = [(256 * c, 256) for c in range(6)] + [(1536, 128)]
 
-
 def dot_nn(a, b):
     return lax.dot_general(a, b, (((1,), (0,)), ((), ())), preferred_element_type=F32)
 
-
 def dot_nt(a, b):
     return lax.dot_general(a, b, (((1,), (1,)), ((), ())), preferred_element_type=F32)
 
 
-def dot_tn(a, b):
-    return lax.dot_general(a, b, (((0,), (0,)), ((), ())), preferred_element_type=F32)
-
-
 def code_shift(spot):
     return 8 * (84 - (spot // WIN_S * 13 + spot % WIN_S))
 
-
 def head_lanes(rows):
     return lax.broadcasted_iota(jnp.int32, (rows, GW), 1) // HEAD_DIM
-
 
 def stack_heads(stack_ref, block):
     lane_head = head_lanes(WIN_ROWS)
@@ -63,13 +56,11 @@
     for h in range(GROUP):
         stack_ref[HS * h : HS * h + WIN_ROWS, :GW] = jnp.where(lane_head == h, block, zero)
 
-
 def clear_gaps(stack_ref):
     width = stack_ref.shape[1]
     for h in range(GROUP):
         stop = HS * (h + 1) if h < GROUP - 1 else LANES
         stack_ref[HS * h + 384 : stop, :] = jnp.zeros((stop - HS * h - 384, width), stack_ref.dtype)
-
 
 def unstack(turned_ref):
     picked = []
@@ -79,7 +70,6 @@
             rows = pltpu.roll(rows, 640 - 16 * h, axis=1)
         picked.append(rows[:, :512])
     return jnp.concatenate(picked, axis=0).T[:WIN_ROWS]
-
 
 def build_bias(tab_ref, place_ref, bias_ref, rolled):
     bias_ref[...] = jnp.zeros((WIN_ROWS, LANES), F32)
@@ -90,7 +80,6 @@
             rolled[8 * spot : 8 * spot + 8, :] = pltpu.roll(base, BASE - shift, axis=1)[:, :CODE]
         part = dot_nn(rolled[...].astype(BF16), place_ref[h])
         bias_ref[:, 384 * h : 384 * h + 512] += part * LOG2E
-
 
 def forward_kernel(masked, *refs):
     if masked:
@@ -125,7 +114,6 @@
         turned[:, start : start + width] = mixed[:GW] * inverse[:1]
         inv_ref[0, :, start : start + width] = inverse
     o_ref[0] = unstack(turned).astype(BF16)
-
 
 def backward_kernel(q_ref, k_ref, v_ref, do_ref, inv_ref, e_ref, place_ref,
                     dq_ref, dk_ref, dv_ref, dtab_ref, stack, dstack, probs, slopes, turned, bias_sum):
@@ -168,14 +156,11 @@
                 total = total + pltpu.roll(piece, code_shift(spot), axis=1)
             dtab_ref[0, h] = total
 
-
 def busy(microseconds):
     return pl.CostEstimate(flops=microseconds * 1_000_000_000, bytes_accessed=microseconds * 1_000_000, transcendentals=0)
 
-
 def head_block(part):
     return pl.BlockSpec((1, WIN_ROWS, GW), lambda g, w: (w, 0, part * GROUPS + g))
-
 
 PLAIN = pl.BlockSpec((1, WIN_ROWS, GW), lambda g, w: (w, 0, g))
 INV = pl.BlockSpec((1, 8, LANES), lambda g, w: (g * WINDOWS + w, 0, 0))
@@ -185,7 +170,6 @@
 KAUG = pl.BlockSpec((1, WIN_ROWS, GW), lambda g, w: (w, 0, 0))
 QAUG = pl.BlockSpec((WIN_ROWS, GW), lambda g, w: (0, 0))
 VMEM_LIMIT = 62 * 1024 * 1024
-
 
 def attention_forward(qkv, table, place, aug):
     masked = aug is not None
@@ -211,7 +195,6 @@
         name="attention_forward",
     )(qkv, qkv, qkv, table, place, *(aug or ()))
 
-
 def attention_backward(qkv, grad_mixed, inverse, exps, place):
     return pl.pallas_call(
         backward_kernel,
@@ -241,7 +224,6 @@
     rows = jnp.pad(rows, ((0, 0), (0, 0), (0, BASE - 169 * WIN_T)))
     return rows.reshape(GROUPS, GROUP, WIN_T, BASE).astype(F32)
 
-
 def gather_table(spread):
     rows = spread.reshape(HEADS, WIN_T, BASE)[:, :, : 169 * WIN_T].reshape(HEADS, WIN_T, 169, WIN_T)
     rows = rows.transpose(0, 1, 3, 2)
@@ -249,7 +231,6 @@
         jnp.pad(rows[:, tj], ((0, 0), (7 - tj, tj), (0, 0))) for tj in range(WIN_T)
     )
     return total.reshape(HEADS, TABLE_ROWS).T
-
 
 def place_codes():
     code = jnp.arange(CODE, dtype=jnp.int32)
@@ -258,7 +239,6 @@
     lane = jnp.where((spot_h < WIN_S) & (spot_w < WIN_S), lane, -1000)
     target = lane[None, :] + 16 * jnp.arange(GROUP, dtype=jnp.int32)[:, None]
     return (target[:, :, None] == jnp.arange(512, dtype=jnp.int32)).astype(BF16)
-
 
 def mask_operands(clip_row, frames):
     index = lax.axis_index("tm")
@@ -288,7 +268,6 @@
     0.12572571978855923, 0.06897590427205952, 0.0850992002684089, 0.08370977184002107,
 )
 
-
 def gelu_and_slope(u):
     t = 1.0 / (1.0 + TAIL_SLOPE * jnp.abs(u))
     tail = TAIL_POLY[0] * t + TAIL_POLY[1]
@@ -299,25 +278,20 @@
     chance = jnp.where(u >= 0.0, 1.0 - tail, tail)
     return u * chance, chance + u * bell * (1.0 / math.sqrt(2.0 * math.pi))
 
-
 def normalized(values):
     center = values - jnp.mean(values, axis=1, keepdims=True)
     scale = lax.rsqrt(jnp.mean(center * center, axis=1, keepdims=True) + 1e-05)
     return center * scale, scale
 
-
 def norm_backward(grad_normed, gain, shape, scale):
     e = grad_normed * gain
     return scale * (e - jnp.mean(e, axis=1, keepdims=True) - shape * jnp.mean(e * shape, axis=1, keepdims=True))
 
-
 def turned_low(block):
     return block.astype(F32).T.astype(BF16)
 
-
 def column_sum(block):
     return jnp.sum(block, axis=0, keepdims=True)
-
 
 def project_in_kernel(layer, x_ref, gain_ref, shift_ref, w_ref, qb_ref, vb_ref, n_ref, qkv_ref):
     row = slice(layer, layer + 1)
@@ -327,7 +301,6 @@
     qkv_ref[0, :, :D] = ((dot_nn(n, w_ref[0, :, :D]) + qb_ref[row].astype(F32)) * QSCALE).astype(BF16)
     qkv_ref[0, :, D : 2 * D] = dot_nn(n, w_ref[0, :, D : 2 * D]).astype(BF16)
     qkv_ref[0, :, 2 * D :] = (dot_nn(n, w_ref[0, :, 2 * D :]) + vb_ref[row].astype(F32)).astype(BF16)
-
 
 def feed_forward_kernel(layer, x_ref, o_ref, wp_ref, wu_ref, wd_ref, bp_ref, gain_ref, shift_ref, bu_ref, bd_ref,
                         x1_ref, n_ref, act_ref, slope_ref, x2_ref):
@@ -347,7 +320,6 @@
         wide = slice(512 * c, 512 * c + 512)
         total = total + dot_nn(act_ref[0, :, wide], wd_ref[0, wide, :])
     x2_ref[0] = total.astype(x2_ref.dtype)
-
 
 def feed_backward_kernel(layer, shards, dz_ref, x1_ref, n_ref, o_ref, act_ref, slope_ref, wp_ref, wu_ref, wd_ref, gain_ref,
                          dx1_ref, do_ref, sums_ref, *rest):
@@ -402,7 +374,6 @@
             for target, source in zip(grads, (acc_up, acc_down, acc_proj)):
                 target[...] = source[...].astype(BF16)
 
-
 def project_back_kernel(layer, shards, dq_ref, dk_ref, dv_ref, n_ref, x_ref, dx1_ref, w_ref, gain_ref, dx_ref, sums_ref, grad_ref, acc):
     row = slice(layer, layer + 1)
     step = pl.program_id(0)
@@ -433,26 +404,20 @@
         else:
             grad_ref[...] = acc[...].astype(BF16)
 
-
 def window_block(width):
     return pl.BlockSpec((1, WIN_ROWS, width), lambda w: (w, 0, 0))
 
-
 def window_shape(width, dtype):
     return jax.ShapeDtypeStruct((WINDOWS, WIN_ROWS, width), dtype)
 
-
 def weight_block(layer, rows, columns):
     return pl.BlockSpec((1, rows, columns), lambda w: (layer, 0, 0), pipeline_mode=pl.Buffered(1))
 
-
 def whole_block(*shape):
     return pl.BlockSpec(shape, lambda w: (0,) * len(shape))
 
-
 DENSE_PARAMS = pltpu.CompilerParams(vmem_limit_bytes=VMEM_LIMIT)
 ROW = whole_block(LAYERS, D)
-
 
 def project_in(layer, x, gain, shift, weight, q_bias, v_bias):
     return pl.pallas_call(
@@ -465,7 +430,6 @@
         cost_estimate=busy(8),
         name="project_in",
     )(x, gain, shift, weight, q_bias, v_bias)
-
 
 def feed_forward(layer, x, mixed, wp, wu, wd, bp, gain, shift, bu, bd, out_dtype):
     return pl.pallas_call(
@@ -480,7 +444,6 @@
         cost_estimate=busy(28),
         name="feed_forward",
     )(x, mixed, wp, wu, wd, bp, gain, shift, bu, bd)
-
 
 def feed_backward(layer, shards, dz, x1, normed, mixed, act, slope, wp, wu, wd, gain):
     if shards == 16:
@@ -501,7 +464,6 @@
         name="feed_backward",
     )(dz, x1, normed, mixed, act, slope, wp, wu, wd, gain)
 
-
 def project_back(layer, shards, dq, dk, dv, normed, x, dx1, weight, gain, out_dtype):
     grad_shape = (16, 384, 128) if shards == 16 else (D, 3 * D)
     return pl.pallas_call(
@@ -522,28 +484,23 @@
     pairs = [(source, (source + steps) % count) for source in range(count)]
     return lax.ppermute(value, axis, pairs)
 
-
 def to_windows(field):
     channels = field.shape[-1]
     return field.reshape(2, WIN_S, 2, WIN_S, WIN_T, channels).transpose(0, 2, 1, 3, 4, 5).reshape(WINDOWS, WIN_ROWS, channels)
 
-
 def from_windows(windows):
     channels = windows.shape[-1]
     return windows.reshape(2, 2, WIN_S, WIN_S, WIN_T, channels).transpose(0, 2, 1, 3, 4, 5).reshape(SIDE, SIDE, WIN_T, channels)
-
 
 def shift_in(field):
     ahead = passed_along(field[:, :, :SHIFT_T], "tm", -1)
     moved = jnp.concatenate([field[:, :, SHIFT_T:], ahead], axis=2)
     return to_windows(jnp.roll(moved, (-SHIFT_S, -SHIFT_S), axis=(0, 1)))
 
-
 def shift_out(windows):
     moved = jnp.roll(from_windows(windows), (SHIFT_S, SHIFT_S), axis=(0, 1))
     behind = passed_along(moved[:, :, SHIFT_T:], "tm", 1)
     return jnp.concatenate([behind, moved[:, :, :SHIFT_T]], axis=2)
-
 
 def layer_forward(layer, current, weights, place, aug, out_dtype):
     (gain_one, shift_one, weight_qkv, bias_query, bias_value, table_rows, weight_proj, bias_proj,
@@ -556,43 +513,67 @@
     )
     return result, (current, normed_one, qkv, mixed, inverse, exps, attended, normed_two, act, slope)
 
-
 def over_groups(value):
     count = lax.axis_size("dp")
     if count != 2:
         return lax.psum(value, "dp")
     return value.astype(F32) + passed_along(value, "dp", 1).astype(F32)
 
-
 def scattered(grad):
     shard = lax.psum_scatter(grad, "tm", scatter_dimension=0, tiled=True)
     return over_groups(shard.reshape(shard.shape[-2:])).astype(F32)
 
-
-def halved(grad):
+def swapped(value, reach):
+    count = lax.axis_size("tm")
+    return lax.ppermute(value, "tm", [(source, source ^ reach) for source in range(count)])
+
+def halved(kept, after):
     count = lax.axis_size("tm")
     index = lax.axis_index("tm")
-    kept = grad.reshape((count, -1) + grad.shape[-1:])
     reach = 1
     while reach < count:
         pairs = kept.reshape((kept.shape[0] // 2, 2) + kept.shape[1:])
         bit = index // reach % 2
         mine = lax.dynamic_index_in_dim(pairs, bit, 1, keepdims=False)
         sent = lax.dynamic_index_in_dim(pairs, 1 - bit, 1, keepdims=False).astype(BF16)
-        swap = [(source, source ^ reach) for source in range(count)]
-        kept = mine.astype(F32) + lax.ppermute(sent, "tm", swap).astype(F32)
+        kept = mine.astype(F32) + swapped(sent, reach).astype(F32)
         reach = 2 * reach
-    return over_groups(kept[0].astype(BF16))
-
+        if reach == 4:
+            kept, after = lax.optimization_barrier((kept, after))
+    return over_groups(kept[0].astype(BF16)).astype(F32), after
+
+def gathered(shard):
+    index = lax.axis_index("tm")
+    whole = shard[None]
+    reach = 1
+    while reach < lax.axis_size("tm"):
+        other = swapped(whole, reach)
+        upper = index // reach % 2 == 1
+        whole = jnp.concatenate([jnp.where(upper, other, whole), jnp.where(upper, whole, other)], axis=0)
+        reach = 2 * reach
+    return whole
+
+def reduce_last(qkv_grads, smalls, after):
+    count = lax.axis_size("tm")
+    flat = jnp.stack(smalls)
+    size = flat.shape[1]
+    rows = -(-size // (128 * count))
+    flat = jnp.pad(flat, ((0, 0), (0, rows * 128 * count - size))).reshape(LAYERS, count, rows, 128)
+    parts = [grad.reshape(count, -1, 128) for grad in qkv_grads]
+    height = parts[0].shape[1]
+    shard, after = halved(jnp.concatenate(parts + [flat[0].astype(BF16), flat[1].astype(BF16)], axis=1), after)
+    whole = gathered(shard[LAYERS * height :]).reshape(count, LAYERS, rows * 128)
+    whole = whole.transpose(1, 0, 2).reshape(LAYERS, -1)[:, :size]
+    qkv = [shard[height * layer : height * (layer + 1)] for layer in range(LAYERS)]
+    return qkv, whole, after
 
 def unpack(packed, start, columns):
     rows = columns // 128 * 32
     return packed[start : start + rows].reshape(columns // 128, 32, 128).transpose(1, 0, 2).reshape(32, columns)
 
-
-def layer_backward(layer, upstream, saved, weights, place, aug, out_dtype, after):
-    (gain_one, shift_one, weight_qkv, bias_query, bias_value, table_rows, weight_proj, bias_proj,
-     gain_two, shift_two, weight_up, bias_up, weight_down, bias_down) = weights
+def layer_backward(layer, upstream, saved, weights, place, out_dtype):
+    (gain_one, _, weight_qkv, _, _, _, weight_proj, _,
+     gain_two, _, weight_up, _, weight_down, _) = weights
     (current, normed_one, qkv, mixed, inverse, exps, attended, normed_two, act, slope) = saved
     shards = lax.axis_size("tm")
     grad_attended, grad_mixed, sums_two, *feed_grads = feed_backward(
@@ -603,17 +584,11 @@
     else:
         feed_sums = (scattered(feed_grads[0]), scattered(feed_grads[1].T), scattered(feed_grads[2]))
     dq, dk, dv, spread = attention_backward(qkv, grad_mixed, inverse, exps, place)
-    if after is not None:
-        dq, after = lax.optimization_barrier((dq, after))
     result, sums_one, grad_qkv = project_back(
         layer, shards, dq, dk, dv, normed_one, current, grad_attended, weight_qkv, gain_one, out_dtype
     )
-    grad_qkv = halved(grad_qkv)
     small = jnp.concatenate([sums_two[:2].reshape(-1), sums_one[:1].reshape(-1), gather_table(spread).reshape(-1)])
-    if after is not None:
-        small, feed_sums = lax.optimization_barrier((small, feed_sums))
-    return result, (feed_sums, grad_qkv, lax.psum(small, ("dp", "tm"))), after
-
+    return result, feed_sums, grad_qkv, small
 
 def layer_totals(sums):
     feed_sums, grad_qkv, small = sums
@@ -625,12 +600,12 @@
         grad_qkv = unpack(grad_qkv, 0, 3 * D)
     else:
         grad_up, grad_down, grad_proj = feed_sums
+        grad_qkv = grad_qkv.reshape(-1, 3 * D)
     rest = small[FF : 3 * FF].reshape(8, D)
     return (
         rest[6], rest[7], grad_qkv, rest[4], rest[5], small[3 * FF :].reshape(TABLE_ROWS, HEADS), grad_proj, rest[1],
         rest[2], rest[3], grad_up, small[:FF], grad_down, rest[0],
     )
-
 
 def body(inputs, clip_ids, *rest):
     weights, cotangent = rest[:-1], rest[-1]
@@ -643,20 +618,16 @@
     current = shift_in(from_windows(current))
     current, saved_second = layer_forward(1, current, weights, place, aug, BF16)
     block_output = shift_out(current).transpose(2, 0, 1, 3)
-    upstream, (feed_second, qkv_second, small_second), _ = layer_backward(
-        1, upstream, saved_second, weights, place, aug, F32, None
-    )
+    upstream, feed_second, qkv_second, small_second = layer_backward(1, upstream, saved_second, weights, place, F32)
     upstream = to_windows(shift_out(upstream))
-    upstream, feed_second = lax.optimization_barrier((upstream, feed_second))
-    upstream, first, (qkv_second, small_second) = layer_backward(
-        0, upstream, saved_first, weights, place, None, BF16, (qkv_second, small_second)
-    )
-    totals_first = layer_totals(first)
-    totals_second = layer_totals((feed_second, qkv_second, small_second))
+
+    upstream, feed_first, qkv_first, small_first = layer_backward(0, upstream, saved_first, weights, place, BF16)
+    qkv, small, feed_first = reduce_last((qkv_first, qkv_second), (small_first, small_second), feed_first)
+    totals_first = layer_totals((feed_first, qkv[0], small[0]))
+    totals_second = layer_totals((feed_second, qkv[1], small[1]))
     input_grad = from_windows(upstream).transpose(2, 0, 1, 3)
     results = [jnp.stack(pair) for pair in zip(totals_first, totals_second)]
     return (block_output.reshape(inputs.shape), input_grad.reshape(inputs.shape)) + tuple(results)
-
 
 def solution(mesh):
     tokens = P("dp", "tm", None, None, None)

time: 713 us -> 591 us (0.83)
  waiting for transfers between devices: 223 us -> 126 us
  local copies, waits for them, and re-layouts: 87.4 us -> 77.5 us
  other arithmetic: 35.4 us -> 25.7 us
    psum x2 -> x0, waiting for transfers between devices: 168 us -> none  [layer_backward(): return (result, (feed_sums, grad_qkv, lax.psum(small, ('dp', 'tm'))), after)]
    ppermute x8 -> x7, waiting for transfers between devices: 12 us -> 56.5 us  [passed_along(): return lax.ppermute(value, axis, pairs)]
    reduce_scatter x2, waiting for transfers between devices: 0.04 us -> 24.8 us  [scattered(): shard = lax.psum_scatter(grad, 'tm', scatter_dimension=0, tiled=True)]
    unnamed x61 -> x47, local copies, waits for them, and re-layouts: 20.4 us -> 13.4 us
  transfers between devices with their start and end apart: 20 -> 17, of which waited for: 11 -> 13; matrix products, arithmetic and copies ran while one was open for 13% -> 12% of each run, Pallas kernels for 23% -> 11%
where the time goes in v3:
time: 591 us; the launch traced here: 581 us
  Pallas kernels  320 us (54%)
  waiting for transfers between devices  126 us (21%)
  local copies, waits for them, and re-layouts  77.5 us (13%)
  other arithmetic  25.7 us (4%)
  between operations  16.6 us (3%)
  starting transfers between devices  16.1 us (3%)
    pallas_call x2, Pallas kernels, attention_backward(): pl.pallas_call(backward_kernel, grid=(GROUPS, WINDOWS), in_specs=[head_bl...  105 us
    pallas_call x2, Pallas kernels, attention_forward(): pl.pallas_call(partial(forward_kernel, masked), grid=(GROUPS, WINDOWS), i...  62.4 us
    pallas_call x2, Pallas kernels, feed_backward(): pl.pallas_call(partial(feed_backward_kernel, layer, shards), grid=(WINDOW...  56.8 us
    ppermute x7, waiting for transfers between devices, passed_along(): return lax.ppermute(value, axis, pairs)  56.5 us
    pallas_call x2, Pallas kernels, feed_forward(): pl.pallas_call(partial(feed_forward_kernel, layer), grid=(WINDOWS,), in_s...  54.9 us
    ppermute x8, waiting for transfers between devices, swapped(): lax.ppermute(value, 'tm', [(source, source ^ reach) for source in range(c...  44.2 us
    pallas_call x2, Pallas kernels, project_back(): pl.pallas_call(partial(project_back_kernel, layer, shards), grid=(WINDOWS...  25.3 us
    reduce_scatter x2, waiting for transfers between devices, scattered(): shard = lax.psum_scatter(grad, 'tm', scatter_dimension=0, tiled=True)  24.8 us
  transfers between devices with their start and end apart: 17, of which 13 were waited for; matrix products, arithmetic and copies ran while one was open for 12% of the time, Pallas kernels for 11%

profile of v3, /device:TPU:0, one launch (start us, length us, event | category | flops | bytes accessed | tf_op | source)
XLA Modules:
  0.0 581.1 jit_solution(13734242661448795870)
XLA Ops:
  7.3 2.7 copy.173
  10.6 3.4 copy.174
  14.0 1.8 copy.175
  17.0 2.1 fusion.refs_4_.place_ref
  19.1 7.2 %project_in.2 = (bf16[4,392,512]{2,1,0:T(8,128)(2,1)}, bf16[4,392,1536]{2,1,0:T(8,128)(2,1)}) custom-call(bf16[4,392,512]{2,1,0:T(8,128)(2,1)} %bitcast.269, bf16[2,512]{1,0:T(2,128)(2,1)} %gain_ref.15, bf16[2,512]{1,0:T(2,128)(2,1)} %shift_ref.6, bf16[2,512,1536]{2,1,0:T(8,128)(2,1)} %w_ref.7, bf16[2,512]{1,0:T(2,128)(2,1)} %qb_ref.3, bf16[2,512]{1,0:T(2,128)(2,1)} %vb_ref.3), custom_call_target="tpu_custom_call" | custom-call | flops 8000000000 | bytes 8000000 | tf_op jit(solution)/shard_map/project_in/pallas_call | solution.py:423
  26.3 30.8 %attention_forward.2 = (bf16[4,392,512]{2,1,0:T(8,128)(2,1)}, f32[16,8,1664]{2,1,0:T(8,128)}, bf16[16,392,1664]{2,1,0:T(8,128)(2,1)}) custom-call(bf16[4,392,1536]{2,1,0:T(8,128)(2,1)} %get-tuple-element.60.refs_0_.refs_1_.refs_2_.q_ref.k_ref.v_ref, bf16[4,392,1536]{2,1,0:T(8,128)(2,1)} %get-tuple-element.60.refs_0_.refs_1_.refs_2_.q_ref.k_ref.v_ref, ...), custom_call_target="tpu_custom_call" | custom-call | flops 31000000512 | bytes 31000000 | tf_op jit(solution)/shard_map/attention_forward/pallas_call | solution.py:177
  57.1 27.3 %feed_forward.2 = (f32[4,392,512]{2,1,0:T(8,128)}, bf16[4,392,512]{2,1,0:T(8,128)(2,1)}, bf16[4,392,2048]{2,1,0:T(8,128)(2,1)}, bf16[4,392,2048]{2,1,0:T(8,128)(2,1)}, f32[4,392,512]{2,1,0:T(8,128)}) custom-call(bf16[4,392,512]{2,1,0:T(8,128)(2,1)} %bitcast.270, bf16[4,392,512]{2,1,0:T(8,128)(2,1)} %get-tuple-element.61.o_ref, bf16[2,512,512]{2,1,0:T(8,128)(2,1)} %wp_ref.7, ...), custom_call_target="tpu_custom_call" | custom-call | flops 28000000000 | bytes 28000000 | tf_op jit(solution)/shard_map/feed_forward/pallas_call | solution.py:435
  84.4 2.2 copy.176
  86.6 1.9 fusion.60
  88.5 5.9 %collective-permute-start = (f32[14,14,4,512]{3,2,1,0:T(4,128)}, f32[14,14,4,512]{3,2,1,0:T(4,128)S(1)}, u32[]{:S(2)}, u32[]{:S(2)}) collective-permute-start(f32[14,14,4,512]{3,2,1,0:T(4,128)} %get-tuple-element.222), channel_id=1, source_target_pairs={{0,15},{1,0},{2,1},{3,2},{4,3},{5,4},{6,5},{7,6},{8,7},{9,8},{10,9... | collective-permute-start | bytes 4816904 | tf_op jit(solution)/shard_map/ppermute | solution.py:485
  94.4 1.7 fusion.61
  98.3 4.9 copy.178
  103.2 3.7 copy.179
  113.5 8.1 %collective-permute-done.2 = bf16[14,14,4,512]{3,2,1,0:T(4,128)(2,1)} collective-permute-done((bf16[14,14,4,512]{3,2,1,0:T(4,128)(2,1)}, bf16[14,14,4,512]{3,2,1,0:T(4,128)(2,1)}, u32[]{:S(2)}, u32[]{:S(2)}) %collective-permute-start.2) | collective-permute-done | bytes 802848 | tf_op jit(solution)/shard_map/ppermute | solution.py:485
  121.6 1.9 fusion.8
  128.6 2.0 copy.177
  130.6 7.7 %project_in.3 = (bf16[4,392,512]{2,1,0:T(8,128)(2,1)}, bf16[4,392,1536]{2,1,0:T(8,128)(2,1)}) custom-call(f32[4,392,512]{2,1,0:T(8,128)} %bitcast.261, bf16[2,512]{1,0:T(2,128)(2,1)} %gain_ref.15, bf16[2,512]{1,0:T(2,128)(2,1)} %shift_ref.6, bf16[2,512,1536]{2,1,0:T(8,128)(2,1)} %w_ref.7, bf16[2,512]{1,0:T(2,128)(2,1)} %qb_ref.3, bf16[2,512]{1,0:T(2,128)(2,1)} %vb_ref.3), custom_call_target="tpu_custom_call" | custom-call | flops 8000000000 | bytes 8000000 | tf_op jit(solution)/shard_map/project_in/pallas_call | solution.py:423
  138.3 31.6 %attention_forward.3 = (bf16[4,392,512]{2,1,0:T(8,128)(2,1)}, f32[16,8,1664]{2,1,0:T(8,128)}, bf16[16,392,1664]{2,1,0:T(8,128)(2,1)}) custom-call(bf16[4,392,1536]{2,1,0:T(8,128)(2,1)} %get-tuple-element.63.refs_0_.refs_1_.refs_2_.q_ref.k_ref.v_ref, bf16[4,392,1536]{2,1,0:T(8,128)(2,1)} %get-tuple-element.63.refs_0_.refs_1_.refs_2_.q_ref.k_ref.v_ref, ...), custom_call_target="tpu_custom_call" | custom-call | flops 31000000512 | bytes 31000000 | tf_op jit(solution)/shard_map/attention_forward/pallas_call | solution.py:177
  169.9 27.7 %feed_forward.3 = (f32[4,392,512]{2,1,0:T(8,128)}, bf16[4,392,512]{2,1,0:T(8,128)(2,1)}, bf16[4,392,2048]{2,1,0:T(8,128)(2,1)}, bf16[4,392,2048]{2,1,0:T(8,128)(2,1)}, bf16[4,392,512]{2,1,0:T(8,128)(2,1)}) custom-call(f32[4,392,512]{2,1,0:T(8,128)} %bitcast.262, bf16[4,392,512]{2,1,0:T(8,128)(2,1)} %get-tuple-element.64.o_ref, bf16[2,512,512]{2,1,0:T(8,128)(2,1)} %wp_ref.7, ...), custom_call_target="tpu_custom_call" | custom-call | flops 28000000000 | bytes 28000000 | tf_op jit(solution)/shard_map/feed_forward/pallas_call | solution.py:435
  197.5 28.5 %feed_backward.2 = (f32[4,392,512]{2,1,0:T(8,128)}, bf16[4,392,512]{2,1,0:T(8,128)(2,1)}, f32[8,2048]{1,0:T(8,128)}, bf16[16,1152,128]{2,1,0:T(8,128)(2,1)}) custom-call(bf16[4,392,512]{2,1,0:T(8,128)(2,1)} %bitcast.275, f32[4,392,512]{2,1,0:T(8,128)} %get-tuple-element.66.x1_ref, bf16[4,392,512]{2,1,0:T(8,128)(2,1)} %get-tuple-element.67.n_ref, ...), custom_call_target="tpu_custom_call" | custom-call | flops 28000000000 | bytes 28000000 | tf_op jit(solution)/shard_map/feed_backward/pallas_call | solution.py:453
  226.0 52.7 %attention_backward.2 = (bf16[4,392,512]{2,1,0:T(8,128)(2,1)}, bf16[4,392,512]{2,1,0:T(8,128)(2,1)}, bf16[4,392,512]{2,1,0:T(8,128)(2,1)}, f32[4,4,8,1536]{3,2,1,0:T(8,128)}) custom-call(bf16[4,392,1536]{2,1,0:T(8,128)(2,1)} %get-tuple-element.63.refs_0_.refs_1_.refs_2_.q_ref.k_ref.v_ref, ...), custom_call_target="tpu_custom_call" | custom-call | flops 51999997952 | bytes 52000000 | tf_op jit(solution)/shard_map/attention_backward/pallas_call | solution.py:199
  278.7 12.7 %project_back.2 = (f32[4,392,512]{2,1,0:T(8,128)}, f32[8,2048]{1,0:T(8,128)}, bf16[16,384,128]{2,1,0:T(8,128)(2,1)}) custom-call(bf16[4,392,512]{2,1,0:T(8,128)(2,1)} %get-tuple-element.73.dq_ref, bf16[4,392,512]{2,1,0:T(8,128)(2,1)} %get-tuple-element.74.dk_ref, bf16[4,392,512]{2,1,0:T(8,128)(2,1)} %get-tuple-element.75.dv_ref, ...), custom_call_target="tpu_custom_call" | custom-call | flops 12999999488 | bytes 13000000 | tf_op jit(solution)/shard_map/project_back/pallas_call | solution.py:469
  291.4 2.3 copy.184
  295.1 23.0 %collective-permute-done.3 = f32[14,14,4,512]{3,2,1,0:T(4,128)S(1)} collective-permute-done((f32[14,14,4,512]{3,2,1,0:T(4,128)S(1)}, f32[14,14,4,512]{3,2,1,0:T(4,128)S(1)}, u32[]{:S(2)}, u32[]{:S(2)}) %collective-permute-start.3) | collective-permute-done | bytes 1605664 | tf_op jit(solution)/shard_map/ppermute | solution.py:485
  318.8 2.0 copy.185
  320.8 28.3 %feed_backward.3 = (f32[4,392,512]{2,1,0:T(8,128)}, bf16[4,392,512]{2,1,0:T(8,128)(2,1)}, f32[8,2048]{1,0:T(8,128)}, bf16[16,1152,128]{2,1,0:T(8,128)(2,1)}) custom-call(f32[4,392,512]{2,1,0:T(8,128)} %bitcast.264, f32[4,392,512]{2,1,0:T(8,128)} %get-tuple-element.79.x1_ref, bf16[4,392,512]{2,1,0:T(8,128)(2,1)} %get-tuple-element.80.n_ref, ...), custom_call_target="tpu_custom_call" | custom-call | flops 28000000000 | bytes 28000000 | tf_op jit(solution)/shard_map/feed_backward/pallas_call | solution.py:453
  350.3 4.0 copy.208
  354.4 3.2 slice_bitcast_fusion.7
  362.4 52.6 %attention_backward.3 = (bf16[4,392,512]{2,1,0:T(8,128)(2,1)}, bf16[4,392,512]{2,1,0:T(8,128)(2,1)}, bf16[4,392,512]{2,1,0:T(8,128)(2,1)}, f32[4,4,8,1536]{3,2,1,0:T(8,128)}) custom-call(bf16[4,392,1536]{2,1,0:T(8,128)(2,1)} %get-tuple-element.60.refs_0_.refs_1_.refs_2_.q_ref.k_ref.v_ref, ...), custom_call_target="tpu_custom_call" | custom-call | flops 51999997952 | bytes 52000000 | tf_op jit(solution)/shard_map/attention_backward/pallas_call | solution.py:199
  416.1 3.9 copy.207
  420.0 3.0 slice_bitcast_fusion.15
  425.8 12.6 %project_back.3 = (bf16[4,392,512]{2,1,0:T(8,128)(2,1)}, f32[8,2048]{1,0:T(8,128)}, bf16[16,384,128]{2,1,0:T(8,128)(2,1)}) custom-call(bf16[4,392,512]{2,1,0:T(8,128)(2,1)} %get-tuple-element.86.dq_ref, bf16[4,392,512]{2,1,0:T(8,128)(2,1)} %get-tuple-element.87.dk_ref, bf16[4,392,512]{2,1,0:T(8,128)(2,1)} %get-tuple-element.88.dv_ref, ...), custom_call_target="tpu_custom_call" | custom-call | flops 12999999488 | bytes 13000000 | tf_op jit(solution)/shard_map/project_back/pallas_call | solution.py:469
  441.8 2.4 pad_maximum_fusion
  444.4 1.6 copy.215
  446.0 1.6 copy.182
  447.9 1.7 fusion.62
  450.3 1.7 convert_add_fusion
  455.4 17.0 %collective-permute-done.1 = bf16[14,14,4,512]{3,2,1,0:T(4,128)(2,1)} collective-permute-done((bf16[14,14,4,512]{3,2,1,0:T(4,128)(2,1)}, bf16[14,14,4,512]{3,2,1,0:T(4,128)(2,1)}, u32[]{:S(2)}, u32[]{:S(2)}) %collective-permute-start.1) | collective-permute-done | bytes 802848 | tf_op jit(solution)/shard_map/ppermute | solution.py:485
  472.4 3.2 maximum_bitcast_fusion
  477.0 17.8 %collective-permute-done.5 = bf16[4,814,128]{2,0,1:T(4,128)(2,1)S(1)} collective-permute-done((bf16[4,814,128]{2,0,1:T(4,128)(2,1)}, bf16[4,814,128]{2,0,1:T(4,128)(2,1)S(1)}, u32[]{:S(2)}, u32[]{:S(2)}) %collective-permute-start.5) | collective-permute-done | bytes 833568 | tf_op jit(solution)/shard_map/ppermute | solution.py:528
  495.0 24.8 %reduce-scatter.5.cloned.1.call-done = bf16[1,1152,128]{2,1,0:T(8,128)(2,1)} async-done(((bf16[16,1152,128]{2,1,0:T(8,128)(2,1)}), bf16[1,1152,128]{2,1,0:T(8,128)(2,1)}) %reduce-scatter.5.cloned.1.call-update) | async-done | bytes 294928 | tf_op jit(solution)/shard_map/reduce_scatter | solution.py:523
  523.1 3.9 collective-permute-done.14
  528.1 3.8 collective-permute-done.7
  534.7 7.8 %collective-permute-done.8 = bf16[1,814,128]{2,1,0:T(8,128)(2,1)S(1)} collective-permute-done((bf16[1,814,128]{2,1,0:T(8,128)(2,1)S(1)}, bf16[1,814,128]{2,1,0:T(8,128)(2,1)S(1)}, u32[]{:S(2)}, u32[]{:S(2)}) %collective-permute-start.8) | collective-permute-done | bytes 208416 | tf_op jit(solution)/shard_map/ppermute | solution.py:528
  543.9 4.5 collective-permute-done.9
  549.8 2.7 collective-permute-start.11
  555.0 4.2 collective-permute-done.12
  560.1 9.2 %collective-permute-done.13 = f32[8,46,128]{2,1,0:T(8,128)S(1)} collective-permute-done((f32[8,46,128]{2,1,0:T(8,128)S(1)}, f32[8,46,128]{2,1,0:T(8,128)S(1)}, u32[]{:S(2)}, u32[]{:S(2)}) %collective-permute-start.13) | collective-permute-done | bytes 188448 | tf_op jit(solution)/shard_map/ppermute | solution.py:528
  (189 shorter events, 53.2 us)
Async XLA Ops:
  7.2 2.8 copy-start.11
  7.2 446.7 %reduce-scatter.3.cloned.1.call-start = ((), (), s32[]{:S(2)}) async-start(), calls=%async_computation.2 | async-start | bytes 5013504 | tf_op jit(solution)/shard_map/reduce_scatter | solution.py:523
  86.6 7.8 %copy-start.4 = (bf16[1,8,14,14,512]{4,1,3,2,0:T(8,128)(2,1)S(1)}, bf16[1,8,14,14,512]{4,1,3,2,0:T(8,128)(2,1)}, u32[]{:S(2)}) copy-start(bf16[1,8,14,14,512]{4,1,3,2,0:T(8,128)(2,1)} %param.33) | copy-start | bytes 4816900
  88.5 38.4 %collective-permute-start = (f32[14,14,4,512]{3,2,1,0:T(4,128)}, f32[14,14,4,512]{3,2,1,0:T(4,128)S(1)}, u32[]{:S(2)}, u32[]{:S(2)}) collective-permute-start(f32[14,14,4,512]{3,2,1,0:T(4,128)} %get-tuple-element.222), channel_id=1, source_target_pairs={{0,15},{1,0},{2,1},{3,2},{4,3},{5,4},{6,5},{7,6},{8,7},{9,8},{10,9... | collective-permute-start | bytes 4816904 | tf_op jit(solution)/shard_map/ppermute | solution.py:485
  94.4 3.1 copy-start.12
  96.1 25.5 %collective-permute-start.2 = (bf16[14,14,4,512]{3,2,1,0:T(4,128)(2,1)}, bf16[14,14,4,512]{3,2,1,0:T(4,128)(2,1)}, u32[]{:S(2)}, u32[]{:S(2)}) collective-permute-start(bf16[14,14,4,512]{3,2,1,0:T(4,128)(2,1)} %get-tuple-element.224), channel_id=1, source_target_pairs={{0,15},{1,0},{2,1},{3,2},{4,3},{5,4},{6,5},{7,6},{8,7},{9,8},{10,9... | collective-permute-start | bytes 2408456 | tf_op jit(solution)/shard_map/ppermute | solution.py:485
  97.5 0.8 copy-start.7
  112.9 10.6 %copy-start = (bf16[14,14,4,512]{3,2,1,0:T(4,128)(2,1)S(1)}, bf16[14,14,4,512]{3,2,1,0:T(4,128)(2,1)}, u32[]{:S(2)}) copy-start(bf16[14,14,4,512]{3,2,1,0:T(4,128)(2,1)} %get-tuple-element.225) | copy-start | bytes 2408452
  295.1 23.1 %collective-permute-start.3 = (f32[14,14,4,512]{3,2,1,0:T(4,128)S(1)}, f32[14,14,4,512]{3,2,1,0:T(4,128)S(1)}, u32[]{:S(2)}, u32[]{:S(2)}) collective-permute-start(f32[14,14,4,512]{3,2,1,0:T(4,128)S(1)} %get-tuple-element.220), channel_id=1, source_target_pairs={{0,1},{1,2},{2,3},{3,4},{4,5},{5,6},{6,7},{7,8},{8,9},{9,10},{10,1... | collective-permute-start | bytes 4816904 | tf_op jit(solution)/shard_map/ppermute | solution.py:485
  349.2 1.1 copy-start.8
  349.2 170.6 %reduce-scatter.5.cloned.1.call-start = ((), (), s32[]{:S(2)}) async-start(), calls=%async_computation.3 | async-start | bytes 5013504 | tf_op jit(solution)/shard_map/reduce_scatter | solution.py:523
  446.0 4.3 collective-permute-start.4
  449.6 22.8 %collective-permute-start.1 = (bf16[14,14,4,512]{3,2,1,0:T(4,128)(2,1)}, bf16[14,14,4,512]{3,2,1,0:T(4,128)(2,1)}, u32[]{:S(2)}, u32[]{:S(2)}) collective-permute-start(bf16[14,14,4,512]{3,2,1,0:T(4,128)(2,1)} %get-tuple-element.226), channel_id=1, source_target_pairs={{0,1},{1,2},{2,3},{3,4},{4,5},{5,6},{6,7},{7,8},{8,9},{9,10},{10,1... | collective-permute-start | bytes 2408456 | tf_op jit(solution)/shard_map/ppermute | solution.py:485
  452.0 1.9 copy-start.1
  452.0 20.4 %copy-start.3 = (bf16[14,14,4,512]{3,2,1,0:T(4,128)(2,1)S(1)}, bf16[14,14,4,512]{3,2,1,0:T(4,128)(2,1)}, u32[]{:S(2)}) copy-start(bf16[14,14,4,512]{3,2,1,0:T(4,128)(2,1)} %get-tuple-element.227) | copy-start | bytes 2408452
  453.9 21.7 %copy-start.5 = (bf16[4,392,512]{2,1,0:T(8,128)(2,1)S(1)}, bf16[4,392,512]{2,1,0:T(8,128)(2,1)}, u32[]{:S(2)}) copy-start(bf16[4,392,512]{2,1,0:T(8,128)(2,1)} %get-tuple-element.91) | copy-start | bytes 4816900
  453.9 40.9 %collective-permute-start.5 = (bf16[4,814,128]{2,0,1:T(4,128)(2,1)}, bf16[4,814,128]{2,0,1:T(4,128)(2,1)S(1)}, u32[]{:S(2)}, u32[]{:S(2)}) collective-permute-start(bf16[4,814,128]{2,0,1:T(4,128)(2,1)} %copy.196), channel_id=1, source_target_pairs={{0,2},{1,3},{2,0},{3,1},{4,6},{5,7},{6,4},{7,5},{8,10},{9,11},{10,... | collective-permute-start | bytes 2500616 | tf_op jit(solution)/shard_map/ppermute | solution.py:528
  453.9 67.4 %collective-permute-start.6 = (bf16[1152,128]{1,0:T(8,128)(2,1)}, bf16[1152,128]{1,0:T(8,128)(2,1)S(1)}, u32[]{:S(2)}, u32[]{:S(2)}) collective-permute-start(bf16[1152,128]{1,0:T(8,128)(2,1)} %bitcast.291), channel_id=1, source_target_pairs={{0,16},{16,0},{1,17},{17,1},{2,18},{18,2},{3,19},{19,3},{4,20},{20... | collective-permute-start | bytes 884744 | tf_op jit(solution)/shard_map/ppermute | solution.py:485
  472.4 22.4 %copy-start.2 = (f32[8,814,128]{2,1,0:T(8,128)S(1)}, f32[8,814,128]{2,1,0:T(8,128)}, u32[]{:S(2)}) copy-start(f32[8,814,128]{2,1,0:T(8,128)} %copy-done.1) | copy-start | bytes 10002436
  477.0 44.3 %copy-start.9 = (bf16[1,1152,128]{2,1,0:T(8,128)(2,1)S(1)}, bf16[1,1152,128]{2,1,0:T(8,128)(2,1)}, u32[]{:S(2)}) copy-start(bf16[1,1152,128]{2,1,0:T(8,128)(2,1)} %reduce-scatter.3.cloned.1.call-done) | copy-start | bytes 884740
  519.8 7.2 %copy-start.10 = (bf16[1,1152,128]{2,1,0:T(8,128)(2,1)S(1)}, bf16[1,1152,128]{2,1,0:T(8,128)(2,1)}, u32[]{:S(2)}) copy-start(bf16[1,1152,128]{2,1,0:T(8,128)(2,1)} %reduce-scatter.5.cloned.1.call-done) | copy-start | bytes 884740
  519.8 7.2 %collective-permute-start.14 = (bf16[1152,128]{1,0:T(8,128)(2,1)}, bf16[1152,128]{1,0:T(8,128)(2,1)S(1)}, u32[]{:S(2)}, u32[]{:S(2)}) collective-permute-start(bf16[1152,128]{1,0:T(8,128)(2,1)} %bitcast.292), channel_id=1, source_target_pairs={{0,16},{16,0},{1,17},{17,1},{2,18},{18,2},{3,19},{19,3},{4,20},{20... | collective-permute-start | bytes 884744 | tf_op jit(solution)/shard_map/ppermute | solution.py:485
  522.2 9.7 %collective-permute-start.7 = (bf16[2,814,128]{2,1,0:T(8,128)(2,1)}, bf16[2,814,128]{2,1,0:T(8,128)(2,1)}, u32[]{:S(2)}, u32[]{:S(2)}) collective-permute-start(bf16[2,814,128]{2,1,0:T(8,128)(2,1)} %fusion.10), channel_id=1, source_target_pairs={{0,4},{1,5},{2,6},{3,7},{4,0},{5,1},{6,2},{7,3},{8,12},{9,13},{10,... | collective-permute-start | bytes 1250312 | tf_op jit(solution)/shard_map/ppermute | solution.py:528
  533.0 9.5 %collective-permute-start.8 = (bf16[1,814,128]{2,1,0:T(8,128)(2,1)S(1)}, bf16[1,814,128]{2,1,0:T(8,128)(2,1)S(1)}, u32[]{:S(2)}, u32[]{:S(2)}) collective-permute-start(bf16[1,814,128]{2,1,0:T(8,128)(2,1)S(1)} %dynamic-slice_convert_fusion.2), channel_id=1, source_target_pairs={{0,8},{1,9},{2,10},{3,11},{4,12},{5,13},{6,14},{7,15},{8,0},{9,1},... | collective-permute-start | bytes 625160 | tf_op jit(solution)/shard_map/ppermute | solution.py:528
  534.6 13.9 %copy-start.6 = (f32[1,128,512]{1,2,0:T(8,128)S(1)}, f32[1,128,512]{1,2,0:T(8,128)}, u32[]{:S(2)}) copy-start(f32[1,128,512]{1,2,0:T(8,128)} %get-tuple-element.230) | copy-start | bytes 786436
  542.5 5.9 %collective-permute-start.9 = (bf16[814,128]{1,0:T(8,128)(2,1)S(1)}, bf16[814,128]{1,0:T(8,128)(2,1)S(1)}, u32[]{:S(2)}, u32[]{:S(2)}) collective-permute-start(bf16[814,128]{1,0:T(8,128)(2,1)S(1)} %fusion.12), channel_id=1, source_target_pairs={{0,16},{16,0},{1,17},{17,1},{2,18},{18,2},{3,19},{19,3},{4,20},{20... | collective-permute-start | bytes 625160 | tf_op jit(solution)/shard_map/ppermute | solution.py:485
  548.5 1.3 collective-permute-start.10
  549.8 4.8 collective-permute-start.11
  554.5 4.7 collective-permute-start.12
  559.3 10.0 %collective-permute-start.13 = (f32[8,46,128]{2,1,0:T(8,128)S(1)}, f32[8,46,128]{2,1,0:T(8,128)S(1)}, u32[]{:S(2)}, u32[]{:S(2)}) collective-permute-start(f32[8,46,128]{2,1,0:T(8,128)S(1)} %pad_maximum_fusion.17), channel_id=1, source_target_pairs={{0,8},{1,9},{2,10},{3,11},{4,12},{5,13},{6,14},{7,15},{8,0},{9,1},... | collective-permute-start | bytes 565256 | tf_op jit(solution)/shard_map/ppermute | solution.py:528
Sparse Core Ops, SparseCore 0:
  349.3 72.8 reduce-scatter.2
  426.1 93.7 reduce-scatter.4

commit v4 on v3

--- a/solution.py
+++ b/solution.py
@@ -493,13 +493,13 @@
     return windows.reshape(2, 2, WIN_S, WIN_S, WIN_T, channels).transpose(0, 2, 1, 3, 4, 5).reshape(SIDE, SIDE, WIN_T, channels)
 
 def shift_in(field):
-    ahead = passed_along(field[:, :, :SHIFT_T], "tm", -1)
+    ahead = passed_along(field[:, :, :SHIFT_T].astype(BF16), "tm", -1).astype(field.dtype)
     moved = jnp.concatenate([field[:, :, SHIFT_T:], ahead], axis=2)
     return to_windows(jnp.roll(moved, (-SHIFT_S, -SHIFT_S), axis=(0, 1)))
 
 def shift_out(windows):
     moved = jnp.roll(from_windows(windows), (SHIFT_S, SHIFT_S), axis=(0, 1))
-    behind = passed_along(moved[:, :, SHIFT_T:], "tm", 1)
+    behind = passed_along(moved[:, :, SHIFT_T:].astype(BF16), "tm", 1).astype(moved.dtype)
     return jnp.concatenate([behind, moved[:, :, :SHIFT_T]], axis=2)
 
 def layer_forward(layer, current, weights, place, aug, out_dtype):
@@ -543,15 +543,28 @@
     return over_groups(kept[0].astype(BF16)).astype(F32), after
 
 def gathered(shard):
+    count = lax.axis_size("tm")
     index = lax.axis_index("tm")
     whole = shard[None]
     reach = 1
-    while reach < lax.axis_size("tm"):
-        other = swapped(whole, reach)
-        upper = index // reach % 2 == 1
-        whole = jnp.concatenate([jnp.where(upper, other, whole), jnp.where(upper, whole, other)], axis=0)
-        reach = 2 * reach
+    while reach < count:
+        low = index // reach % 2 == 1
+        if count // reach >= 4:
+            high = index // (2 * reach) % 2 == 1
+            one, two, three = (swapped(whole, reach * step) for step in (1, 2, 3))
+            first, second = jnp.where(low, one, whole), jnp.where(low, whole, one)
+            third, fourth = jnp.where(low, three, two), jnp.where(low, two, three)
+            whole = jnp.concatenate(
+                [jnp.where(high, third, first), jnp.where(high, fourth, second),
+                 jnp.where(high, first, third), jnp.where(high, second, fourth)], axis=0
+            )
+            reach = 4 * reach
+        else:
+            other = swapped(whole, reach)
+            whole = jnp.concatenate([jnp.where(low, other, whole), jnp.where(low, whole, other)], axis=0)
+            reach = 2 * reach
     return whole
+
 
 def reduce_last(qkv_grads, smalls, after):
     count = lax.axis_size("tm")
@@ -571,7 +584,7 @@
     rows = columns // 128 * 32
     return packed[start : start + rows].reshape(columns // 128, 32, 128).transpose(1, 0, 2).reshape(32, columns)
 
-def layer_backward(layer, upstream, saved, weights, place, out_dtype):
+def layer_backward(layer, upstream, saved, weights, place, out_dtype, after):
     (gain_one, _, weight_qkv, _, _, _, weight_proj, _,
      gain_two, _, weight_up, _, weight_down, _) = weights
     (current, normed_one, qkv, mixed, inverse, exps, attended, normed_two, act, slope) = saved
@@ -584,11 +597,13 @@
     else:
         feed_sums = (scattered(feed_grads[0]), scattered(feed_grads[1].T), scattered(feed_grads[2]))
     dq, dk, dv, spread = attention_backward(qkv, grad_mixed, inverse, exps, place)
+    if after is not None:
+        dq, after = lax.optimization_barrier((dq, after))
     result, sums_one, grad_qkv = project_back(
         layer, shards, dq, dk, dv, normed_one, current, grad_attended, weight_qkv, gain_one, out_dtype
     )
     small = jnp.concatenate([sums_two[:2].reshape(-1), sums_one[:1].reshape(-1), gather_table(spread).reshape(-1)])
-    return result, feed_sums, grad_qkv, small
+    return result, feed_sums, grad_qkv, small, after
 
 def layer_totals(sums):
     feed_sums, grad_qkv, small = sums
@@ -615,13 +630,19 @@
     upstream = shift_in(cotangent[0].transpose(1, 2, 0, 3))
     current = to_windows(inputs[0].transpose(1, 2, 0, 3))
     current, saved_first = layer_forward(0, current, weights, place, None, F32)
+    current, upstream = lax.optimization_barrier((current, upstream))
     current = shift_in(from_windows(current))
     current, saved_second = layer_forward(1, current, weights, place, aug, BF16)
     block_output = shift_out(current).transpose(2, 0, 1, 3)
-    upstream, feed_second, qkv_second, small_second = layer_backward(1, upstream, saved_second, weights, place, F32)
+    upstream, feed_second, qkv_second, small_second, _ = layer_backward(
+        1, upstream, saved_second, weights, place, F32, None
+    )
+    upstream, block_output = lax.optimization_barrier((upstream, block_output))
     upstream = to_windows(shift_out(upstream))
 
-    upstream, feed_first, qkv_first, small_first = layer_backward(0, upstream, saved_first, weights, place, BF16)
+    upstream, feed_first, qkv_first, small_first, feed_second = layer_backward(
+        0, upstream, saved_first, weights, place, BF16, feed_second
+    )
     qkv, small, feed_first = reduce_last((qkv_first, qkv_second), (small_first, small_second), feed_first)
     totals_first = layer_totals((feed_first, qkv[0], small[0]))
     totals_second = layer_totals((feed_second, qkv[1], small[1]))

time: 591 us -> 570 us (0.964)
  waiting for transfers between devices: 126 us -> 90.9 us
  local copies, waits for them, and re-layouts: 77.5 us -> 83.6 us
    ppermute x7, waiting for transfers between devices: 56.5 us -> 23.2 us  [passed_along(): return lax.ppermute(value, axis, pairs)]
    ppermute x8 -> x10, waiting for transfers between devices: 44.2 us -> 22.9 us  [swapped(): lax.ppermute(value, 'tm', [(source, source ^ reach) for source in range(c...]
    reduce_scatter x2, waiting for transfers between devices: 24.8 us -> 44.8 us  [scattered(): shard = lax.psum_scatter(grad, 'tm', scatter_dimension=0, tiled=True)]
    unnamed x47 -> x51, local copies, waits for them, and re-layouts: 13.4 us -> 20.1 us
  transfers between devices with their start and end apart: 17 -> 19, of which waited for: 13 -> 11; matrix products, arithmetic and copies ran while one was open for 12% -> 15% of each run, Pallas kernels for 11% -> 45%
where the time goes in v4:
time: 570 us; the launch traced here: 560 us
  Pallas kernels  320 us (56%)
  waiting for transfers between devices  90.9 us (16%)
  local copies, waits for them, and re-layouts  83.6 us (15%)
  other arithmetic  31.2 us (5%)
  starting transfers between devices  17.7 us (3%)
  between operations  16.5 us (3%)
    pallas_call x2, Pallas kernels, attention_backward(): pl.pallas_call(backward_kernel, grid=(GROUPS, WINDOWS), in_specs=[head_bl...  105 us
    pallas_call x2, Pallas kernels, attention_forward(): pl.pallas_call(partial(forward_kernel, masked), grid=(GROUPS, WINDOWS), i...  62.5 us
    pallas_call x2, Pallas kernels, feed_backward(): pl.pallas_call(partial(feed_backward_kernel, layer, shards), grid=(WINDOW...  56.8 us
    pallas_call x2, Pallas kernels, feed_forward(): pl.pallas_call(partial(feed_forward_kernel, layer), grid=(WINDOWS,), in_s...  55.3 us
    reduce_scatter x2, waiting for transfers between devices, scattered(): shard = lax.psum_scatter(grad, 'tm', scatter_dimension=0, tiled=True)  44.8 us
    pallas_call x2, Pallas kernels, project_back(): pl.pallas_call(partial(project_back_kernel, layer, shards), grid=(WINDOWS...  25.4 us
    ppermute x7, waiting for transfers between devices, passed_along(): return lax.ppermute(value, axis, pairs)  23.2 us
    ppermute x10, waiting for transfers between devices, swapped(): lax.ppermute(value, 'tm', [(source, source ^ reach) for source in range(c...  22.9 us
  transfers between devices with their start and end apart: 19, of which 11 were waited for; matrix products, arithmetic and copies ran while one was open for 15% of the time, Pallas kernels for 45%

profile of v4, /device:TPU:0, one launch (start us, length us, event | category | flops | bytes accessed | tf_op | source)
XLA Modules:
  0.0 559.7 jit_solution(7429251781208975900)
XLA Ops:
  7.2 3.4 fusion.60
  10.7 5.4 collective-permute-start
  16.8 3.2 copy.174
  20.0 3.1 copy.175
  26.2 2.1 fusion.refs_4_.place_ref
  32.0 7.2 %project_in.2 = (bf16[4,392,512]{2,1,0:T(8,128)(2,1)}, bf16[4,392,1536]{2,1,0:T(8,128)(2,1)}) custom-call(bf16[4,392,512]{2,1,0:T(8,128)(2,1)} %bitcast.276, bf16[2,512]{1,0:T(2,128)(2,1)} %gain_ref.15, bf16[2,512]{1,0:T(2,128)(2,1)} %shift_ref.6, bf16[2,512,1536]{2,1,0:T(8,128)(2,1)} %w_ref.7, bf16[2,512]{1,0:T(2,128)(2,1)} %qb_ref.3, bf16[2,512]{1,0:T(2,128)(2,1)} %vb_ref.3), custom_call_target="tpu_custom_call" | custom-call | flops 8000000000 | bytes 8000000 | tf_op jit(solution)/shard_map/project_in/pallas_call | solution.py:423
  39.2 30.9 %attention_forward.2 = (bf16[4,392,512]{2,1,0:T(8,128)(2,1)}, f32[16,8,1664]{2,1,0:T(8,128)}, bf16[16,392,1664]{2,1,0:T(8,128)(2,1)}) custom-call(bf16[4,392,1536]{2,1,0:T(8,128)(2,1)} %get-tuple-element.66.refs_0_.refs_1_.refs_2_.q_ref.k_ref.v_ref, bf16[4,392,1536]{2,1,0:T(8,128)(2,1)} %get-tuple-element.66.refs_0_.refs_1_.refs_2_.q_ref.k_ref.v_ref, ...), custom_call_target="tpu_custom_call" | custom-call | flops 31000000512 | bytes 31000000 | tf_op jit(solution)/shard_map/attention_forward/pallas_call | solution.py:177
  70.1 27.7 %feed_forward.2 = (f32[4,392,512]{2,1,0:T(8,128)}, bf16[4,392,512]{2,1,0:T(8,128)(2,1)}, bf16[4,392,2048]{2,1,0:T(8,128)(2,1)}, bf16[4,392,2048]{2,1,0:T(8,128)(2,1)}, f32[4,392,512]{2,1,0:T(8,128)}) custom-call(bf16[4,392,512]{2,1,0:T(8,128)(2,1)} %bitcast.277, bf16[4,392,512]{2,1,0:T(8,128)(2,1)} %get-tuple-element.67.o_ref, bf16[2,512,512]{2,1,0:T(8,128)(2,1)} %wp_ref.7, ...), custom_call_target="tpu_custom_call" | custom-call | flops 28000000000 | bytes 28000000 | tf_op jit(solution)/shard_map/feed_forward/pallas_call | solution.py:435
  103.9 1.7 copy-done.1
  107.6 5.2 copy.179
  112.8 1.8 copy.180
  123.9 2.1 copy.178
  126.0 7.7 %project_in.3 = (bf16[4,392,512]{2,1,0:T(8,128)(2,1)}, bf16[4,392,1536]{2,1,0:T(8,128)(2,1)}) custom-call(f32[4,392,512]{2,1,0:T(8,128)} %bitcast.265, bf16[2,512]{1,0:T(2,128)(2,1)} %gain_ref.15, bf16[2,512]{1,0:T(2,128)(2,1)} %shift_ref.6, bf16[2,512,1536]{2,1,0:T(8,128)(2,1)} %w_ref.7, bf16[2,512]{1,0:T(2,128)(2,1)} %qb_ref.3, bf16[2,512]{1,0:T(2,128)(2,1)} %vb_ref.3), custom_call_target="tpu_custom_call" | custom-call | flops 8000000000 | bytes 8000000 | tf_op jit(solution)/shard_map/project_in/pallas_call | solution.py:423
  133.7 31.6 %attention_forward.3 = (bf16[4,392,512]{2,1,0:T(8,128)(2,1)}, f32[16,8,1664]{2,1,0:T(8,128)}, bf16[16,392,1664]{2,1,0:T(8,128)(2,1)}) custom-call(bf16[4,392,1536]{2,1,0:T(8,128)(2,1)} %get-tuple-element.70.refs_0_.refs_1_.refs_2_.q_ref.k_ref.v_ref, bf16[4,392,1536]{2,1,0:T(8,128)(2,1)} %get-tuple-element.70.refs_0_.refs_1_.refs_2_.q_ref.k_ref.v_ref, ...), custom_call_target="tpu_custom_call" | custom-call | flops 31000000512 | bytes 31000000 | tf_op jit(solution)/shard_map/attention_forward/pallas_call | solution.py:177
  165.3 27.6 %feed_forward.3 = (f32[4,392,512]{2,1,0:T(8,128)}, bf16[4,392,512]{2,1,0:T(8,128)(2,1)}, bf16[4,392,2048]{2,1,0:T(8,128)(2,1)}, bf16[4,392,2048]{2,1,0:T(8,128)(2,1)}, bf16[4,392,512]{2,1,0:T(8,128)(2,1)}) custom-call(f32[4,392,512]{2,1,0:T(8,128)} %bitcast.266, bf16[4,392,512]{2,1,0:T(8,128)(2,1)} %get-tuple-element.72.o_ref, bf16[2,512,512]{2,1,0:T(8,128)(2,1)} %wp_ref.7, ...), custom_call_target="tpu_custom_call" | custom-call | flops 28000000000 | bytes 28000000 | tf_op jit(solution)/shard_map/feed_forward/pallas_call | solution.py:435
  192.9 1.6 copy.183
  195.4 28.5 %feed_backward.2 = (f32[4,392,512]{2,1,0:T(8,128)}, bf16[4,392,512]{2,1,0:T(8,128)(2,1)}, f32[8,2048]{1,0:T(8,128)}, bf16[16,1152,128]{2,1,0:T(8,128)(2,1)}) custom-call(bf16[4,392,512]{2,1,0:T(8,128)(2,1)} %bitcast.281, f32[4,392,512]{2,1,0:T(8,128)} %get-tuple-element.73.x1_ref, bf16[4,392,512]{2,1,0:T(8,128)(2,1)} %get-tuple-element.74.n_ref, ...), custom_call_target="tpu_custom_call" | custom-call | flops 28000000000 | bytes 28000000 | tf_op jit(solution)/shard_map/feed_backward/pallas_call | solution.py:453
  223.9 52.5 %attention_backward.2 = (bf16[4,392,512]{2,1,0:T(8,128)(2,1)}, bf16[4,392,512]{2,1,0:T(8,128)(2,1)}, bf16[4,392,512]{2,1,0:T(8,128)(2,1)}, f32[4,4,8,1536]{3,2,1,0:T(8,128)}) custom-call(bf16[4,392,1536]{2,1,0:T(8,128)(2,1)} %get-tuple-element.70.refs_0_.refs_1_.refs_2_.q_ref.k_ref.v_ref, ...), custom_call_target="tpu_custom_call" | custom-call | flops 51999997952 | bytes 52000000 | tf_op jit(solution)/shard_map/attention_backward/pallas_call | solution.py:199
  277.6 3.8 copy.208
  281.4 2.9 slice_bitcast_fusion.7
  287.2 12.8 %project_back.2 = (f32[4,392,512]{2,1,0:T(8,128)}, f32[8,2048]{1,0:T(8,128)}, bf16[16,384,128]{2,1,0:T(8,128)(2,1)}) custom-call(bf16[4,392,512]{2,1,0:T(8,128)(2,1)} %get-tuple-element.80.dq_ref, bf16[4,392,512]{2,1,0:T(8,128)(2,1)} %get-tuple-element.81.dk_ref, bf16[4,392,512]{2,1,0:T(8,128)(2,1)} %get-tuple-element.82.dv_ref, ...), custom_call_target="tpu_custom_call" | custom-call | flops 12999999488 | bytes 13000000 | tf_op jit(solution)/shard_map/project_back/pallas_call | solution.py:469
  301.0 3.1 maximum_bitcast_fusion
  308.0 12.6 %collective-permute-done.3 = bf16[14,14,4,512]{3,2,1,0:T(4,128)(2,1)S(1)} collective-permute-done((bf16[14,14,4,512]{3,2,1,0:T(4,128)(2,1)S(1)}, bf16[14,14,4,512]{3,2,1,0:T(4,128)(2,1)S(1)}, u32[]{:S(2)}, u32[]{:S(2)}) %collective-permute-start.3) | collective-permute-done | bytes 802848 | tf_op jit(solution)/shard_map/ppermute | solution.py:485
  322.6 2.0 copy.185
  324.6 28.3 %feed_backward.3 = (f32[4,392,512]{2,1,0:T(8,128)}, bf16[4,392,512]{2,1,0:T(8,128)(2,1)}, f32[8,2048]{1,0:T(8,128)}, bf16[16,1152,128]{2,1,0:T(8,128)(2,1)}) custom-call(f32[4,392,512]{2,1,0:T(8,128)} %bitcast.270, f32[4,392,512]{2,1,0:T(8,128)} %get-tuple-element.89.x1_ref, bf16[4,392,512]{2,1,0:T(8,128)(2,1)} %get-tuple-element.90.n_ref, ...), custom_call_target="tpu_custom_call" | custom-call | flops 28000000000 | bytes 28000000 | tf_op jit(solution)/shard_map/feed_backward/pallas_call | solution.py:453
  353.0 52.3 %attention_backward.3 = (bf16[4,392,512]{2,1,0:T(8,128)(2,1)}, bf16[4,392,512]{2,1,0:T(8,128)(2,1)}, bf16[4,392,512]{2,1,0:T(8,128)(2,1)}, f32[4,4,8,1536]{3,2,1,0:T(8,128)}) custom-call(bf16[4,392,1536]{2,1,0:T(8,128)(2,1)} %get-tuple-element.66.refs_0_.refs_1_.refs_2_.q_ref.k_ref.v_ref, ...), custom_call_target="tpu_custom_call" | custom-call | flops 51999997952 | bytes 52000000 | tf_op jit(solution)/shard_map/attention_backward/pallas_call | solution.py:199
  406.4 3.9 copy.207
  410.3 4.2 slice_bitcast_fusion.15
  414.6 1.6 collective-permute-start.4
  416.2 3.1 pad_add_fusion.1
  421.9 1.9 convert_add_fusion.2
  423.8 12.7 %project_back.3 = (bf16[4,392,512]{2,1,0:T(8,128)(2,1)}, f32[8,2048]{1,0:T(8,128)}, bf16[16,384,128]{2,1,0:T(8,128)(2,1)}) custom-call(bf16[4,392,512]{2,1,0:T(8,128)(2,1)} %get-tuple-element.98.dq_ref, bf16[4,392,512]{2,1,0:T(8,128)(2,1)} %get-tuple-element.99.dk_ref, bf16[4,392,512]{2,1,0:T(8,128)(2,1)} %get-tuple-element.100.dv_ref, ...), custom_call_target="tpu_custom_call" | custom-call | flops 12999999488 | bytes 13000000 | tf_op jit(solution)/shard_map/project_back/pallas_call | solution.py:469
  439.0 2.4 pad_maximum_fusion
  441.5 1.7 copy.215
  443.2 3.9 collective-permute-done.5
  447.1 1.7 convert_add_fusion
  450.4 44.8 %reduce-scatter.5.cloned.1.call-done = bf16[1,1152,128]{2,1,0:T(8,128)(2,1)} async-done(((bf16[16,1152,128]{2,1,0:T(8,128)(2,1)}), bf16[1,1152,128]{2,1,0:T(8,128)(2,1)}) %reduce-scatter.5.cloned.1.call-update) | async-done | bytes 294928 | tf_op jit(solution)/shard_map/reduce_scatter | solution.py:523
  496.7 6.2 %collective-permute-done.7 = bf16[1152,128]{1,0:T(8,128)(2,1)S(1)} collective-permute-done((bf16[1152,128]{1,0:T(8,128)(2,1)}, bf16[1152,128]{1,0:T(8,128)(2,1)S(1)}, u32[]{:S(2)}, u32[]{:S(2)}) %collective-permute-start.7) | collective-permute-done | bytes 294944 | tf_op jit(solution)/shard_map/ppermute | solution.py:485
  504.0 2.0 bitcast_add_fusion
  508.4 2.8 copy.186
  511.9 4.5 collective-permute-done.8
  519.9 6.6 %collective-permute-done.9 = bf16[1,814,128]{2,1,0:T(8,128)(2,1)S(1)} collective-permute-done((bf16[1,814,128]{2,1,0:T(8,128)(2,1)S(1)}, bf16[1,814,128]{2,1,0:T(8,128)(2,1)S(1)}, u32[]{:S(2)}, u32[]{:S(2)}) %collective-permute-start.9) | collective-permute-done | bytes 208416 | tf_op jit(solution)/shard_map/ppermute | solution.py:528
  528.0 4.4 collective-permute-done.10
  532.6 1.8 collective-permute-start.12
  536.5 1.9 collective-permute-start.14
  538.4 2.6 collective-permute-start.16
  541.7 2.4 collective-permute-done.14
  544.2 3.8 collective-permute-done.15
  (201 shorter events, 61.1 us)
Async XLA Ops:
  7.2 9.0 %copy-start.13 = (bf16[2,2535,16]{1,2,0:T(8,128)(2,1)S(1)}, bf16[2,2535,16]{1,2,0:T(8,128)(2,1)}, u32[]{:S(2)}) copy-start(bf16[2,2535,16]{1,2,0:T(8,128)(2,1)} %param.24) | copy-start | bytes 486724
  7.2 407.4 %reduce-scatter.3.cloned.1.call-start = ((), (), s32[]{:S(2)}) async-start(), calls=%async_computation.2 | async-start | bytes 5013504 | tf_op jit(solution)/shard_map/reduce_scatter | solution.py:523
  10.7 89.1 %collective-permute-start = (bf16[14,14,4,512]{3,2,1,0:T(4,128)(2,1)}, bf16[14,14,4,512]{3,2,1,0:T(4,128)(2,1)S(1)}, u32[]{:S(2)}, u32[]{:S(2)}) collective-permute-start(bf16[14,14,4,512]{3,2,1,0:T(4,128)(2,1)} %get-tuple-element.234), channel_id=1, source_target_pairs={{0,15},{1,0},{2,1},{3,2},{4,3},{5,4},{6,5},{7,6},{8,7},{9,8},{10,9... | collective-permute-start | bytes 2408456 | tf_op jit(solution)/shard_map/ppermute | solution.py:485
  23.2 1.7 copy-start.8
  26.2 5.7 %copy-start.14 = (s32[1,128]{1,0:T(1,128)S(1)}, s32[1,128]{1,0:T(1,128)}, u32[]{:S(2)}) copy-start(s32[1,128]{1,0:T(1,128)} %param.18) | copy-start | bytes 1540
  101.0 2.5 copy-start.4
  103.9 1.7 copy-start.1
  106.9 13.8 %collective-permute-start.1 = (bf16[14,14,4,512]{3,2,1,0:T(4,128)(2,1)}, bf16[14,14,4,512]{3,2,1,0:T(4,128)(2,1)}, u32[]{:S(2)}, u32[]{:S(2)}) collective-permute-start(bf16[14,14,4,512]{3,2,1,0:T(4,128)(2,1)} %slice.582), channel_id=1, source_target_pairs={{0,15},{1,0},{2,1},{3,2},{4,3},{5,4},{6,5},{7,6},{8,7},{9,8},{10,9... | collective-permute-start | bytes 2408456 | tf_op jit(solution)/shard_map/ppermute | solution.py:485
  114.7 5.5 copy-start.2
  195.3 105.7 %collective-permute-start.2 = (bf16[14,14,4,512]{3,2,1,0:T(4,128)(2,1)S(1)}, bf16[14,14,4,512]{3,2,1,0:T(4,128)(2,1)}, u32[]{:S(2)}, u32[]{:S(2)}) collective-permute-start(bf16[14,14,4,512]{3,2,1,0:T(4,128)(2,1)S(1)} %get-tuple-element.232), channel_id=1, source_target_pairs={{0,1},{1,2},{2,3},{3,4},{4,5},{5,6},{6,7},{7,8},{8,9},{9,10},{10,1... | collective-permute-start | bytes 2408456 | tf_op jit(solution)/shard_map/ppermute | solution.py:485
  223.9 271.4 %reduce-scatter.5.cloned.1.call-start = ((), (), s32[]{:S(2)}) async-start(), calls=%async_computation.3 | async-start | bytes 5013504 | tf_op jit(solution)/shard_map/reduce_scatter | solution.py:523
  300.0 4.1 copy-start.5
  305.4 2.6 copy-start.3
  305.8 14.7 %collective-permute-start.3 = (bf16[14,14,4,512]{3,2,1,0:T(4,128)(2,1)S(1)}, bf16[14,14,4,512]{3,2,1,0:T(4,128)(2,1)S(1)}, u32[]{:S(2)}, u32[]{:S(2)}) collective-permute-start(bf16[14,14,4,512]{3,2,1,0:T(4,128)(2,1)S(1)} %slice.581), channel_id=1, source_target_pairs={{0,1},{1,2},{2,3},{3,4},{4,5},{5,6},{6,7},{7,8},{8,9},{9,10},{10,1... | collective-permute-start | bytes 2408456 | tf_op jit(solution)/shard_map/ppermute | solution.py:485
  320.6 1.4 slice-start
  414.6 7.3 %collective-permute-start.4 = (bf16[1152,128]{1,0:T(8,128)(2,1)}, bf16[1152,128]{1,0:T(8,128)(2,1)}, u32[]{:S(2)}, u32[]{:S(2)}) collective-permute-start(bf16[1152,128]{1,0:T(8,128)(2,1)} %bitcast.298), channel_id=1, source_target_pairs={{0,16},{16,0},{1,17},{17,1},{2,18},{18,2},{3,19},{19,3},{4,20},{20... | collective-permute-start | bytes 884744 | tf_op jit(solution)/shard_map/ppermute | solution.py:485
  419.3 2.6 copy-start.12
  423.8 13.7 %copy-start.11 = (bf16[1,46704]{1,0:T(2,128)(2,1)S(1)}, bf16[1,46704]{1,0:T(2,128)(2,1)}, u32[]{:S(2)}) copy-start(bf16[1,46704]{1,0:T(2,128)(2,1)} %stack.142) | copy-start | bytes 280228
  443.2 3.9 collective-permute-start.5
  448.7 1.7 copy-start
  450.4 53.6 %collective-permute-start.6 = (bf16[4,814,128]{2,0,1:T(4,128)(2,1)S(1)}, bf16[4,814,128]{2,0,1:T(4,128)(2,1)}, u32[]{:S(2)}, u32[]{:S(2)}) collective-permute-start(bf16[4,814,128]{2,0,1:T(4,128)(2,1)S(1)} %copy.196), channel_id=1, source_target_pairs={{0,2},{1,3},{2,0},{3,1},{4,6},{5,7},{6,4},{7,5},{8,10},{9,11},{10,... | collective-permute-start | bytes 2500616 | tf_op jit(solution)/shard_map/ppermute | solution.py:528
  495.2 7.7 %collective-permute-start.7 = (bf16[1152,128]{1,0:T(8,128)(2,1)}, bf16[1152,128]{1,0:T(8,128)(2,1)S(1)}, u32[]{:S(2)}, u32[]{:S(2)}) collective-permute-start(bf16[1152,128]{1,0:T(8,128)(2,1)} %bitcast.297), channel_id=1, source_target_pairs={{0,16},{16,0},{1,17},{17,1},{2,18},{18,2},{3,19},{19,3},{4,20},{20... | collective-permute-start | bytes 884744 | tf_op jit(solution)/shard_map/ppermute | solution.py:485
  504.0 7.2 %copy-start.7 = (f32[1152,128]{1,0:T(8,128)}, f32[1152,128]{1,0:T(8,128)S(1)}, u32[]{:S(2)}) copy-start(f32[1152,128]{1,0:T(8,128)S(1)} %convert_add_fusion.1) | copy-start | bytes 1769476
  504.0 3.4 copy-start.6
  506.0 2.3 slice-start.1
  506.9 9.6 %collective-permute-start.8 = (bf16[2,814,128]{2,1,0:T(8,128)(2,1)}, bf16[2,814,128]{2,1,0:T(8,128)(2,1)}, u32[]{:S(2)}, u32[]{:S(2)}) collective-permute-start(bf16[2,814,128]{2,1,0:T(8,128)(2,1)} %fusion.10), channel_id=1, source_target_pairs={{0,4},{1,5},{2,6},{3,7},{4,0},{5,1},{6,2},{7,3},{8,12},{9,13},{10,... | collective-permute-start | bytes 1250312 | tf_op jit(solution)/shard_map/ppermute | solution.py:528
  511.2 6.7 %copy-start.10 = (f32[1,128,512]{1,2,0:T(8,128)S(1)}, f32[1,128,512]{1,2,0:T(8,128)}, u32[]{:S(2)}) copy-start(f32[1,128,512]{1,2,0:T(8,128)} %get-tuple-element.238) | copy-start | bytes 786436
  517.6 1.4 copy-start.9
  517.6 1.6 slice-start.2
  517.6 8.9 %collective-permute-start.9 = (bf16[1,814,128]{2,1,0:T(8,128)(2,1)S(1)}, bf16[1,814,128]{2,1,0:T(8,128)(2,1)S(1)}, u32[]{:S(2)}, u32[]{:S(2)}) collective-permute-start(bf16[1,814,128]{2,1,0:T(8,128)(2,1)S(1)} %dynamic-slice_convert_fusion.2), channel_id=1, source_target_pairs={{0,8},{1,9},{2,10},{3,11},{4,12},{5,13},{6,14},{7,15},{8,0},{9,1},... | collective-permute-start | bytes 625160 | tf_op jit(solution)/shard_map/ppermute | solution.py:528
  526.6 5.9 %collective-permute-start.10 = (bf16[814,128]{1,0:T(8,128)(2,1)S(1)}, bf16[814,128]{1,0:T(8,128)(2,1)S(1)}, u32[]{:S(2)}, u32[]{:S(2)}) collective-permute-start(bf16[814,128]{1,0:T(8,128)(2,1)S(1)} %fusion.12), channel_id=1, source_target_pairs={{0,16},{16,0},{1,17},{17,1},{2,18},{18,2},{3,19},{19,3},{4,20},{20... | collective-permute-start | bytes 625160 | tf_op jit(solution)/shard_map/ppermute | solution.py:485
  532.5 3.3 collective-permute-start.11
  532.6 3.9 collective-permute-start.12
  534.4 2.1 collective-permute-start.13
  536.5 7.6 %collective-permute-start.14 = (f32[4,46,128]{2,1,0:T(8,128)S(1)}, f32[4,46,128]{2,1,0:T(8,128)S(1)}, u32[]{:S(2)}, u32[]{:S(2)}) collective-permute-start(f32[4,46,128]{2,1,0:T(8,128)S(1)} %pad_maximum_fusion.20), channel_id=1, source_target_pairs={{0,12},{1,13},{2,14},{3,15},{4,8},{5,9},{6,10},{7,11},{8,4},{9,5},... | collective-permute-start | bytes 282632 | tf_op jit(solution)/shard_map/ppermute | solution.py:528
  538.4 9.6 %collective-permute-start.15 = (f32[4,46,128]{2,1,0:T(8,128)S(1)}, f32[4,46,128]{2,1,0:T(8,128)S(1)}, u32[]{:S(2)}, u32[]{:S(2)}) collective-permute-start(f32[4,46,128]{2,1,0:T(8,128)S(1)} %pad_maximum_fusion.20), channel_id=1, source_target_pairs={{0,8},{1,9},{2,10},{3,11},{4,12},{5,13},{6,14},{7,15},{8,0},{9,1},... | collective-permute-start | bytes 282632 | tf_op jit(solution)/shard_map/ppermute | solution.py:528
  538.4 9.6 %collective-permute-start.16 = (f32[4,46,128]{2,1,0:T(8,128)S(1)}, f32[4,46,128]{2,1,0:T(8,128)S(1)}, u32[]{:S(2)}, u32[]{:S(2)}) collective-permute-start(f32[4,46,128]{2,1,0:T(8,128)S(1)} %pad_maximum_fusion.20), channel_id=1, source_target_pairs={{0,4},{1,5},{2,6},{3,7},{4,0},{5,1},{6,2},{7,3},{8,12},{9,13},{10,... | collective-permute-start | bytes 282632 | tf_op jit(solution)/shard_map/ppermute | solution.py:528
Sparse Core Ops, SparseCore 0:
  224.0 76.7 reduce-scatter.2
  414.7 80.5 reduce-scatter.4

commit v5 on v4

--- a/solution.py
+++ b/solution.py
@@ -151,9 +151,13 @@
         for h in range(GROUP):
             coded = dot_nt(bias_sum[:, 384 * h : 384 * h + 512].astype(BF16), place_ref[h])
             total = jnp.zeros((8, BASE), F32)
-            for spot in range(49):
-                piece = jnp.concatenate([coded[8 * spot : 8 * spot + 8], pad], axis=1)
-                total = total + pltpu.roll(piece, code_shift(spot), axis=1)
+            for hj in range(WIN_S):
+                line = coded[8 * (WIN_S * hj + 6) : 8 * (WIN_S * hj + 6) + 8]
+                for wj in range(WIN_S - 1):
+                    spot = WIN_S * hj + wj
+                    line = line + pltpu.roll(coded[8 * spot : 8 * spot + 8], 8 * (6 - wj), axis=1)
+                line = jnp.concatenate([line, pad], axis=1)
+                total = total + (pltpu.roll(line, 104 * (6 - hj), axis=1) if hj < 6 else line)
             dtab_ref[0, h] = total
 
 def busy(microseconds):

time: 570 us -> 571 us (level)
  no operation moved by 1% of the time
where the time goes in v5:
time: 571 us; the launch traced here: 561 us
  Pallas kernels  321 us (56%)
  waiting for transfers between devices  87.7 us (15%)
  local copies, waits for them, and re-layouts  83.6 us (15%)
  other arithmetic  31.2 us (5%)
  starting transfers between devices  20.4 us (4%)
  between operations  16.5 us (3%)
    pallas_call x2, Pallas kernels, attention_backward(): pl.pallas_call(backward_kernel, grid=(GROUPS, WINDOWS), in_specs=[head_bl...  106 us
    pallas_call x2, Pallas kernels, attention_forward(): pl.pallas_call(partial(forward_kernel, masked), grid=(GROUPS, WINDOWS), i...  62.5 us
    pallas_call x2, Pallas kernels, feed_backward(): pl.pallas_call(partial(feed_backward_kernel, layer, shards), grid=(WINDOW...  57.2 us
    pallas_call x2, Pallas kernels, feed_forward(): pl.pallas_call(partial(feed_forward_kernel, layer), grid=(WINDOWS,), in_s...  55.3 us
    reduce_scatter x2, waiting for transfers between devices, scattered(): shard = lax.psum_scatter(grad, 'tm', scatter_dimension=0, tiled=True)  44.8 us
    pallas_call x2, Pallas kernels, project_back(): pl.pallas_call(partial(project_back_kernel, layer, shards), grid=(WINDOWS...  25.4 us
    ppermute x7, waiting for transfers between devices, passed_along(): return lax.ppermute(value, axis, pairs)  21.8 us
    ppermute x10, waiting for transfers between devices, swapped(): lax.ppermute(value, 'tm', [(source, source ^ reach) for source in range(c...  21.1 us
  transfers between devices with their start and end apart: 19, of which 11 were waited for; matrix products, arithmetic and copies ran while one was open for 15% of the time, Pallas kernels for 45%

profile of v5, /device:TPU:0, one launch (start us, length us, event | category | flops | bytes accessed | tf_op | source)
XLA Modules:
  0.0 560.5 jit_solution(10617448745044740601)
XLA Ops:
  7.2 3.4 fusion.60
  10.7 5.4 collective-permute-start
  16.8 3.2 copy.174
  20.0 3.1 copy.175
  26.2 2.1 fusion.refs_4_.place_ref
  32.0 7.2 %project_in.2 = (bf16[4,392,512]{2,1,0:T(8,128)(2,1)}, bf16[4,392,1536]{2,1,0:T(8,128)(2,1)}) custom-call(bf16[4,392,512]{2,1,0:T(8,128)(2,1)} %bitcast.276, bf16[2,512]{1,0:T(2,128)(2,1)} %gain_ref.15, bf16[2,512]{1,0:T(2,128)(2,1)} %shift_ref.6, bf16[2,512,1536]{2,1,0:T(8,128)(2,1)} %w_ref.7, bf16[2,512]{1,0:T(2,128)(2,1)} %qb_ref.3, bf16[2,512]{1,0:T(2,128)(2,1)} %vb_ref.3), custom_call_target="tpu_custom_call" | custom-call | flops 8000000000 | bytes 8000000 | tf_op jit(solution)/shard_map/project_in/pallas_call | solution.py:427
  39.2 30.9 %attention_forward.2 = (bf16[4,392,512]{2,1,0:T(8,128)(2,1)}, f32[16,8,1664]{2,1,0:T(8,128)}, bf16[16,392,1664]{2,1,0:T(8,128)(2,1)}) custom-call(bf16[4,392,1536]{2,1,0:T(8,128)(2,1)} %get-tuple-element.66.refs_0_.refs_1_.refs_2_.q_ref.k_ref.v_ref, bf16[4,392,1536]{2,1,0:T(8,128)(2,1)} %get-tuple-element.66.refs_0_.refs_1_.refs_2_.q_ref.k_ref.v_ref, ...), custom_call_target="tpu_custom_call" | custom-call | flops 31000000512 | bytes 31000000 | tf_op jit(solution)/shard_map/attention_forward/pallas_call | solution.py:181
  70.1 27.7 %feed_forward.2 = (f32[4,392,512]{2,1,0:T(8,128)}, bf16[4,392,512]{2,1,0:T(8,128)(2,1)}, bf16[4,392,2048]{2,1,0:T(8,128)(2,1)}, bf16[4,392,2048]{2,1,0:T(8,128)(2,1)}, f32[4,392,512]{2,1,0:T(8,128)}) custom-call(bf16[4,392,512]{2,1,0:T(8,128)(2,1)} %bitcast.277, bf16[4,392,512]{2,1,0:T(8,128)(2,1)} %get-tuple-element.67.o_ref, bf16[2,512,512]{2,1,0:T(8,128)(2,1)} %wp_ref.7, ...), custom_call_target="tpu_custom_call" | custom-call | flops 28000000000 | bytes 28000000 | tf_op jit(solution)/shard_map/feed_forward/pallas_call | solution.py:439
  103.9 1.7 copy-done.1
  107.6 5.2 copy.179
  112.8 1.8 copy.180
  123.9 2.1 copy.178
  126.0 7.7 %project_in.3 = (bf16[4,392,512]{2,1,0:T(8,128)(2,1)}, bf16[4,392,1536]{2,1,0:T(8,128)(2,1)}) custom-call(f32[4,392,512]{2,1,0:T(8,128)} %bitcast.265, bf16[2,512]{1,0:T(2,128)(2,1)} %gain_ref.15, bf16[2,512]{1,0:T(2,128)(2,1)} %shift_ref.6, bf16[2,512,1536]{2,1,0:T(8,128)(2,1)} %w_ref.7, bf16[2,512]{1,0:T(2,128)(2,1)} %qb_ref.3, bf16[2,512]{1,0:T(2,128)(2,1)} %vb_ref.3), custom_call_target="tpu_custom_call" | custom-call | flops 8000000000 | bytes 8000000 | tf_op jit(solution)/shard_map/project_in/pallas_call | solution.py:427
  133.7 31.6 %attention_forward.3 = (bf16[4,392,512]{2,1,0:T(8,128)(2,1)}, f32[16,8,1664]{2,1,0:T(8,128)}, bf16[16,392,1664]{2,1,0:T(8,128)(2,1)}) custom-call(bf16[4,392,1536]{2,1,0:T(8,128)(2,1)} %get-tuple-element.70.refs_0_.refs_1_.refs_2_.q_ref.k_ref.v_ref, bf16[4,392,1536]{2,1,0:T(8,128)(2,1)} %get-tuple-element.70.refs_0_.refs_1_.refs_2_.q_ref.k_ref.v_ref, ...), custom_call_target="tpu_custom_call" | custom-call | flops 31000000512 | bytes 31000000 | tf_op jit(solution)/shard_map/attention_forward/pallas_call | solution.py:181
  165.3 27.6 %feed_forward.3 = (f32[4,392,512]{2,1,0:T(8,128)}, bf16[4,392,512]{2,1,0:T(8,128)(2,1)}, bf16[4,392,2048]{2,1,0:T(8,128)(2,1)}, bf16[4,392,2048]{2,1,0:T(8,128)(2,1)}, bf16[4,392,512]{2,1,0:T(8,128)(2,1)}) custom-call(f32[4,392,512]{2,1,0:T(8,128)} %bitcast.266, bf16[4,392,512]{2,1,0:T(8,128)(2,1)} %get-tuple-element.72.o_ref, bf16[2,512,512]{2,1,0:T(8,128)(2,1)} %wp_ref.7, ...), custom_call_target="tpu_custom_call" | custom-call | flops 28000000000 | bytes 28000000 | tf_op jit(solution)/shard_map/feed_forward/pallas_call | solution.py:439
  192.9 1.6 copy.183
  195.4 28.5 %feed_backward.2 = (f32[4,392,512]{2,1,0:T(8,128)}, bf16[4,392,512]{2,1,0:T(8,128)(2,1)}, f32[8,2048]{1,0:T(8,128)}, bf16[16,1152,128]{2,1,0:T(8,128)(2,1)}) custom-call(bf16[4,392,512]{2,1,0:T(8,128)(2,1)} %bitcast.281, f32[4,392,512]{2,1,0:T(8,128)} %get-tuple-element.73.x1_ref, bf16[4,392,512]{2,1,0:T(8,128)(2,1)} %get-tuple-element.74.n_ref, ...), custom_call_target="tpu_custom_call" | custom-call | flops 28000000000 | bytes 28000000 | tf_op jit(solution)/shard_map/feed_backward/pallas_call | solution.py:457
  223.9 53.0 %attention_backward.2 = (bf16[4,392,512]{2,1,0:T(8,128)(2,1)}, bf16[4,392,512]{2,1,0:T(8,128)(2,1)}, bf16[4,392,512]{2,1,0:T(8,128)(2,1)}, f32[4,4,8,1536]{3,2,1,0:T(8,128)}) custom-call(bf16[4,392,1536]{2,1,0:T(8,128)(2,1)} %get-tuple-element.70.refs_0_.refs_1_.refs_2_.q_ref.k_ref.v_ref, ...), custom_call_target="tpu_custom_call" | custom-call | flops 51999997952 | bytes 52000000 | tf_op jit(solution)/shard_map/attention_backward/pallas_call | solution.py:203
  278.0 3.8 copy.208
  281.9 2.9 slice_bitcast_fusion.7
  287.6 12.8 %project_back.2 = (f32[4,392,512]{2,1,0:T(8,128)}, f32[8,2048]{1,0:T(8,128)}, bf16[16,384,128]{2,1,0:T(8,128)(2,1)}) custom-call(bf16[4,392,512]{2,1,0:T(8,128)(2,1)} %get-tuple-element.80.dq_ref, bf16[4,392,512]{2,1,0:T(8,128)(2,1)} %get-tuple-element.81.dk_ref, bf16[4,392,512]{2,1,0:T(8,128)(2,1)} %get-tuple-element.82.dv_ref, ...), custom_call_target="tpu_custom_call" | custom-call | flops 12999999488 | bytes 13000000 | tf_op jit(solution)/shard_map/project_back/pallas_call | solution.py:473
  301.4 3.1 maximum_bitcast_fusion
  308.0 12.5 %collective-permute-done.3 = bf16[14,14,4,512]{3,2,1,0:T(4,128)(2,1)S(1)} collective-permute-done((bf16[14,14,4,512]{3,2,1,0:T(4,128)(2,1)S(1)}, bf16[14,14,4,512]{3,2,1,0:T(4,128)(2,1)S(1)}, u32[]{:S(2)}, u32[]{:S(2)}) %collective-permute-start.3) | collective-permute-done | bytes 802848 | tf_op jit(solution)/shard_map/ppermute | solution.py:489
  322.6 2.0 copy.185
  324.7 28.7 %feed_backward.3 = (f32[4,392,512]{2,1,0:T(8,128)}, bf16[4,392,512]{2,1,0:T(8,128)(2,1)}, f32[8,2048]{1,0:T(8,128)}, bf16[16,1152,128]{2,1,0:T(8,128)(2,1)}) custom-call(f32[4,392,512]{2,1,0:T(8,128)} %bitcast.270, f32[4,392,512]{2,1,0:T(8,128)} %get-tuple-element.89.x1_ref, bf16[4,392,512]{2,1,0:T(8,128)(2,1)} %get-tuple-element.90.n_ref, ...), custom_call_target="tpu_custom_call" | custom-call | flops 28000000000 | bytes 28000000 | tf_op jit(solution)/shard_map/feed_backward/pallas_call | solution.py:457
  353.4 52.7 %attention_backward.3 = (bf16[4,392,512]{2,1,0:T(8,128)(2,1)}, bf16[4,392,512]{2,1,0:T(8,128)(2,1)}, bf16[4,392,512]{2,1,0:T(8,128)(2,1)}, f32[4,4,8,1536]{3,2,1,0:T(8,128)}) custom-call(bf16[4,392,1536]{2,1,0:T(8,128)(2,1)} %get-tuple-element.66.refs_0_.refs_1_.refs_2_.q_ref.k_ref.v_ref, ...), custom_call_target="tpu_custom_call" | custom-call | flops 51999997952 | bytes 52000000 | tf_op jit(solution)/shard_map/attention_backward/pallas_call | solution.py:203
  407.3 3.9 copy.207
  411.1 4.2 slice_bitcast_fusion.15
  415.4 1.6 collective-permute-start.4
  417.0 3.1 pad_add_fusion.1
  422.7 1.9 convert_add_fusion.2
  424.6 12.7 %project_back.3 = (bf16[4,392,512]{2,1,0:T(8,128)(2,1)}, f32[8,2048]{1,0:T(8,128)}, bf16[16,384,128]{2,1,0:T(8,128)(2,1)}) custom-call(bf16[4,392,512]{2,1,0:T(8,128)(2,1)} %get-tuple-element.98.dq_ref, bf16[4,392,512]{2,1,0:T(8,128)(2,1)} %get-tuple-element.99.dk_ref, bf16[4,392,512]{2,1,0:T(8,128)(2,1)} %get-tuple-element.100.dv_ref, ...), custom_call_target="tpu_custom_call" | custom-call | flops 12999999488 | bytes 13000000 | tf_op jit(solution)/shard_map/project_back/pallas_call | solution.py:473
  439.8 2.4 pad_maximum_fusion
  442.4 1.7 copy.215
  444.0 3.9 collective-permute-done.5
  447.9 1.7 convert_add_fusion
  451.3 44.8 %reduce-scatter.5.cloned.1.call-done = bf16[1,1152,128]{2,1,0:T(8,128)(2,1)} async-done(((bf16[16,1152,128]{2,1,0:T(8,128)(2,1)}), bf16[1,1152,128]{2,1,0:T(8,128)(2,1)}) %reduce-scatter.5.cloned.1.call-update) | async-done | bytes 294928 | tf_op jit(solution)/shard_map/reduce_scatter | solution.py:527
  497.5 5.8 %collective-permute-done.7 = bf16[1152,128]{1,0:T(8,128)(2,1)S(1)} collective-permute-done((bf16[1152,128]{1,0:T(8,128)(2,1)}, bf16[1152,128]{1,0:T(8,128)(2,1)S(1)}, u32[]{:S(2)}, u32[]{:S(2)}) %collective-permute-start.7) | collective-permute-done | bytes 294944 | tf_op jit(solution)/shard_map/ppermute | solution.py:489
  504.3 2.0 bitcast_add_fusion
  509.2 2.8 copy.186
  512.7 3.6 collective-permute-done.8
  520.8 5.7 %collective-permute-done.9 = bf16[1,814,128]{2,1,0:T(8,128)(2,1)S(1)} collective-permute-done((bf16[1,814,128]{2,1,0:T(8,128)(2,1)S(1)}, bf16[1,814,128]{2,1,0:T(8,128)(2,1)S(1)}, u32[]{:S(2)}, u32[]{:S(2)}) %collective-permute-start.9) | collective-permute-done | bytes 208416 | tf_op jit(solution)/shard_map/ppermute | solution.py:532
  528.9 3.5 collective-permute-done.10
  532.5 2.7 collective-permute-start.12
  537.3 1.9 collective-permute-start.14
  539.2 2.6 collective-permute-start.16
  542.5 2.4 collective-permute-done.14
  544.9 3.9 collective-permute-done.15
  (201 shorter events, 62.9 us)
Async XLA Ops:
  7.2 9.0 %copy-start.13 = (bf16[2,2535,16]{1,2,0:T(8,128)(2,1)S(1)}, bf16[2,2535,16]{1,2,0:T(8,128)(2,1)}, u32[]{:S(2)}) copy-start(bf16[2,2535,16]{1,2,0:T(8,128)(2,1)} %param.24) | copy-start | bytes 486724
  7.2 408.2 %reduce-scatter.3.cloned.1.call-start = ((), (), s32[]{:S(2)}) async-start(), calls=%async_computation.2 | async-start | bytes 5013504 | tf_op jit(solution)/shard_map/reduce_scatter | solution.py:527
  10.7 89.1 %collective-permute-start = (bf16[14,14,4,512]{3,2,1,0:T(4,128)(2,1)}, bf16[14,14,4,512]{3,2,1,0:T(4,128)(2,1)S(1)}, u32[]{:S(2)}, u32[]{:S(2)}) collective-permute-start(bf16[14,14,4,512]{3,2,1,0:T(4,128)(2,1)} %get-tuple-element.234), channel_id=1, source_target_pairs={{0,15},{1,0},{2,1},{3,2},{4,3},{5,4},{6,5},{7,6},{8,7},{9,8},{10,9... | collective-permute-start | bytes 2408456 | tf_op jit(solution)/shard_map/ppermute | solution.py:489
  23.2 1.7 copy-start.8
  26.2 5.7 %copy-start.14 = (s32[1,128]{1,0:T(1,128)S(1)}, s32[1,128]{1,0:T(1,128)}, u32[]{:S(2)}) copy-start(s32[1,128]{1,0:T(1,128)} %param.18) | copy-start | bytes 1540
  101.0 2.5 copy-start.4
  103.9 1.7 copy-start.1
  106.9 13.8 %collective-permute-start.1 = (bf16[14,14,4,512]{3,2,1,0:T(4,128)(2,1)}, bf16[14,14,4,512]{3,2,1,0:T(4,128)(2,1)}, u32[]{:S(2)}, u32[]{:S(2)}) collective-permute-start(bf16[14,14,4,512]{3,2,1,0:T(4,128)(2,1)} %slice.582), channel_id=1, source_target_pairs={{0,15},{1,0},{2,1},{3,2},{4,3},{5,4},{6,5},{7,6},{8,7},{9,8},{10,9... | collective-permute-start | bytes 2408456 | tf_op jit(solution)/shard_map/ppermute | solution.py:489
  114.7 5.5 copy-start.2
  195.3 106.1 %collective-permute-start.2 = (bf16[14,14,4,512]{3,2,1,0:T(4,128)(2,1)S(1)}, bf16[14,14,4,512]{3,2,1,0:T(4,128)(2,1)}, u32[]{:S(2)}, u32[]{:S(2)}) collective-permute-start(bf16[14,14,4,512]{3,2,1,0:T(4,128)(2,1)S(1)} %get-tuple-element.232), channel_id=1, source_target_pairs={{0,1},{1,2},{2,3},{3,4},{4,5},{5,6},{6,7},{7,8},{8,9},{9,10},{10,1... | collective-permute-start | bytes 2408456 | tf_op jit(solution)/shard_map/ppermute | solution.py:489
  223.9 272.1 %reduce-scatter.5.cloned.1.call-start = ((), (), s32[]{:S(2)}) async-start(), calls=%async_computation.3 | async-start | bytes 5013504 | tf_op jit(solution)/shard_map/reduce_scatter | solution.py:527
  300.4 4.1 copy-start.5
  305.8 2.3 copy-start.3
  306.2 14.3 %collective-permute-start.3 = (bf16[14,14,4,512]{3,2,1,0:T(4,128)(2,1)S(1)}, bf16[14,14,4,512]{3,2,1,0:T(4,128)(2,1)S(1)}, u32[]{:S(2)}, u32[]{:S(2)}) collective-permute-start(bf16[14,14,4,512]{3,2,1,0:T(4,128)(2,1)S(1)} %slice.581), channel_id=1, source_target_pairs={{0,1},{1,2},{2,3},{3,4},{4,5},{5,6},{6,7},{7,8},{8,9},{9,10},{10,1... | collective-permute-start | bytes 2408456 | tf_op jit(solution)/shard_map/ppermute | solution.py:489
  320.6 1.4 slice-start
  415.4 7.3 %collective-permute-start.4 = (bf16[1152,128]{1,0:T(8,128)(2,1)}, bf16[1152,128]{1,0:T(8,128)(2,1)}, u32[]{:S(2)}, u32[]{:S(2)}) collective-permute-start(bf16[1152,128]{1,0:T(8,128)(2,1)} %bitcast.298), channel_id=1, source_target_pairs={{0,16},{16,0},{1,17},{17,1},{2,18},{18,2},{3,19},{19,3},{4,20},{20... | collective-permute-start | bytes 884744 | tf_op jit(solution)/shard_map/ppermute | solution.py:489
  420.1 2.6 copy-start.12
  424.6 13.7 %copy-start.11 = (bf16[1,46704]{1,0:T(2,128)(2,1)S(1)}, bf16[1,46704]{1,0:T(2,128)(2,1)}, u32[]{:S(2)}) copy-start(bf16[1,46704]{1,0:T(2,128)(2,1)} %stack.142) | copy-start | bytes 280228
  444.0 3.9 collective-permute-start.5
  449.6 1.7 copy-start
  451.3 53.1 %collective-permute-start.6 = (bf16[4,814,128]{2,0,1:T(4,128)(2,1)S(1)}, bf16[4,814,128]{2,0,1:T(4,128)(2,1)}, u32[]{:S(2)}, u32[]{:S(2)}) collective-permute-start(bf16[4,814,128]{2,0,1:T(4,128)(2,1)S(1)} %copy.196), channel_id=1, source_target_pairs={{0,2},{1,3},{2,0},{3,1},{4,6},{5,7},{6,4},{7,5},{8,10},{9,11},{10,... | collective-permute-start | bytes 2500616 | tf_op jit(solution)/shard_map/ppermute | solution.py:532
  496.0 7.2 %collective-permute-start.7 = (bf16[1152,128]{1,0:T(8,128)(2,1)}, bf16[1152,128]{1,0:T(8,128)(2,1)S(1)}, u32[]{:S(2)}, u32[]{:S(2)}) collective-permute-start(bf16[1152,128]{1,0:T(8,128)(2,1)} %bitcast.297), channel_id=1, source_target_pairs={{0,16},{16,0},{1,17},{17,1},{2,18},{18,2},{3,19},{19,3},{4,20},{20... | collective-permute-start | bytes 884744 | tf_op jit(solution)/shard_map/ppermute | solution.py:489
  504.3 7.7 %copy-start.7 = (f32[1152,128]{1,0:T(8,128)}, f32[1152,128]{1,0:T(8,128)S(1)}, u32[]{:S(2)}) copy-start(f32[1152,128]{1,0:T(8,128)S(1)} %convert_add_fusion.1) | copy-start | bytes 1769476
  504.3 3.8 copy-start.6
  506.4 2.7 slice-start.1
  507.2 9.1 %collective-permute-start.8 = (bf16[2,814,128]{2,1,0:T(8,128)(2,1)}, bf16[2,814,128]{2,1,0:T(8,128)(2,1)}, u32[]{:S(2)}, u32[]{:S(2)}) collective-permute-start(bf16[2,814,128]{2,1,0:T(8,128)(2,1)} %fusion.10), channel_id=1, source_target_pairs={{0,4},{1,5},{2,6},{3,7},{4,0},{5,1},{6,2},{7,3},{8,12},{9,13},{10,... | collective-permute-start | bytes 1250312 | tf_op jit(solution)/shard_map/ppermute | solution.py:532
  512.0 6.8 %copy-start.10 = (f32[1,128,512]{1,2,0:T(8,128)S(1)}, f32[1,128,512]{1,2,0:T(8,128)}, u32[]{:S(2)}) copy-start(f32[1,128,512]{1,2,0:T(8,128)} %get-tuple-element.238) | copy-start | bytes 786436
  517.4 2.4 copy-start.9
  517.5 2.6 slice-start.2
  517.5 9.0 %collective-permute-start.9 = (bf16[1,814,128]{2,1,0:T(8,128)(2,1)S(1)}, bf16[1,814,128]{2,1,0:T(8,128)(2,1)S(1)}, u32[]{:S(2)}, u32[]{:S(2)}) collective-permute-start(bf16[1,814,128]{2,1,0:T(8,128)(2,1)S(1)} %dynamic-slice_convert_fusion.2), channel_id=1, source_target_pairs={{0,8},{1,9},{2,10},{3,11},{4,12},{5,13},{6,14},{7,15},{8,0},{9,1},... | collective-permute-start | bytes 625160 | tf_op jit(solution)/shard_map/ppermute | solution.py:532
  526.5 5.9 %collective-permute-start.10 = (bf16[814,128]{1,0:T(8,128)(2,1)S(1)}, bf16[814,128]{1,0:T(8,128)(2,1)S(1)}, u32[]{:S(2)}, u32[]{:S(2)}) collective-permute-start(bf16[814,128]{1,0:T(8,128)(2,1)S(1)} %fusion.12), channel_id=1, source_target_pairs={{0,16},{16,0},{1,17},{17,1},{2,18},{18,2},{3,19},{19,3},{4,20},{20... | collective-permute-start | bytes 625160 | tf_op jit(solution)/shard_map/ppermute | solution.py:489
  532.4 3.3 collective-permute-start.11
  532.5 4.7 collective-permute-start.12
  535.2 2.0 collective-permute-start.13
  537.3 7.6 %collective-permute-start.14 = (f32[4,46,128]{2,1,0:T(8,128)S(1)}, f32[4,46,128]{2,1,0:T(8,128)S(1)}, u32[]{:S(2)}, u32[]{:S(2)}) collective-permute-start(f32[4,46,128]{2,1,0:T(8,128)S(1)} %pad_maximum_fusion.20), channel_id=1, source_target_pairs={{0,12},{1,13},{2,14},{3,15},{4,8},{5,9},{6,10},{7,11},{8,4},{9,5},... | collective-permute-start | bytes 282632 | tf_op jit(solution)/shard_map/ppermute | solution.py:532
  539.2 9.6 %collective-permute-start.15 = (f32[4,46,128]{2,1,0:T(8,128)S(1)}, f32[4,46,128]{2,1,0:T(8,128)S(1)}, u32[]{:S(2)}, u32[]{:S(2)}) collective-permute-start(f32[4,46,128]{2,1,0:T(8,128)S(1)} %pad_maximum_fusion.20), channel_id=1, source_target_pairs={{0,8},{1,9},{2,10},{3,11},{4,12},{5,13},{6,14},{7,15},{8,0},{9,1},... | collective-permute-start | bytes 282632 | tf_op jit(solution)/shard_map/ppermute | solution.py:532
  539.2 9.6 %collective-permute-start.16 = (f32[4,46,128]{2,1,0:T(8,128)S(1)}, f32[4,46,128]{2,1,0:T(8,128)S(1)}, u32[]{:S(2)}, u32[]{:S(2)}) collective-permute-start(f32[4,46,128]{2,1,0:T(8,128)S(1)} %pad_maximum_fusion.20), channel_id=1, source_target_pairs={{0,4},{1,5},{2,6},{3,7},{4,0},{5,1},{6,2},{7,3},{8,12},{9,13},{10,... | collective-permute-start | bytes 282632 | tf_op jit(solution)/shard_map/ppermute | solution.py:532
Sparse Core Ops, SparseCore 0:
  224.0 76.7 reduce-scatter.2
  415.5 80.4 reduce-scatter.4
